TPU v7x, 32 devices: a whole 2x2x4 slice. The times are simulated.
32 devices in a mesh: dp: 2 (over x), context: 4 (over z), experts: 4 (over y, core).
Axes of the slice: x: 2, y: 2, z: 4, core: 2. Of those that a mesh axis runs over, the one named last changes fastest.
Arguments:
- layer_input: bfloat16 [2, 2048, 2048], P('dp', ('context', 'experts')), may hold values from -6 to 6
- cotangent: bfloat16 [2, 2048, 2048], P('dp', ('context', 'experts')), may hold values from -6 to 6
- routes: int32 [2, 2048, 6], P('dp', ('context', 'experts')), may hold values from 0 to 15, all different within a row; in each aligned block of 128 rows (0 to 127, 128 to 255, ..., all dimensions but the last counted through in order) at most 64 rows name the same one
- span_order: int32 [8], replicated, may hold values from 0 to 7, each once
- attn_gain: bfloat16 [2048], P('dp'), may hold values from 0.5 to 1.5
- query_proj: bfloat16 [2048, 3072], P('dp', 'experts'), may hold values from -0.125 to 0.125
- latent_proj: bfloat16 [2048, 576], P('dp'), may hold values from -0.125 to 0.125
- latent_gain: bfloat16 [512], P('dp'), may hold values from 0.5 to 1.5
- expand_proj: bfloat16 [512, 4096], P('dp', 'experts'), may hold values from -0.25 to 0.25
- output_proj: bfloat16 [2048, 2048], P('experts', 'dp'), may hold values from -0.375 to 0.375
- moe_gain: bfloat16 [2048], P('dp'), may hold values from 0.5 to 1.5
- router_proj: bfloat16 [2048, 16], P('dp'), may hold values from -0.25 to 0.25
- shared_in: bfloat16 [2048, 2, 2816], P('dp', None, 'experts'), may hold values from -0.125 to 0.125
- shared_out: bfloat16 [2816, 2048], P('experts', 'dp'), may hold values from -0.109375 to 0.109375
- expert_in: bfloat16 [16, 2048, 2, 1408], P(('context', 'experts'), None, None, 'dp'), may hold values from -0.125 to 0.125
- expert_out: bfloat16 [16, 1408, 2048], P(('context', 'experts'), 'dp'), may hold values from -0.15625 to 0.15625
Outputs:
- block_output: float32 [2, 2048, 2048], P('dp', ('context', 'experts'))
- input_grad: float32 [2, 2048, 2048], P('dp', ('context', 'experts'))
- attn_gain_grad: float32 [2048], P('dp')
- query_proj_grad: float32 [2048, 3072], P('dp', 'experts')
- latent_proj_grad: float32 [2048, 576], P('dp')
- latent_gain_grad: float32 [512], P('dp')
- expand_proj_grad: float32 [512, 4096], P('dp', 'experts')
- output_proj_grad: float32 [2048, 2048], P('experts', 'dp')
- moe_gain_grad: float32 [2048], P('dp')
- router_proj_grad: float32 [2048, 16], P('dp')
- shared_in_grad: float32 [2048, 2, 2816], P('dp', None, 'experts')
- shared_out_grad: float32 [2816, 2048], P('experts', 'dp')
- expert_in_grad: float32 [16, 2048, 2, 1408], P(('context', 'experts'), None, None, 'dp')
- expert_out_grad: float32 [16, 1408, 2048], P(('context', 'experts'), 'dp')
Inputs may be any that keep to these rules, and one draw needn't show every extreme that they name: `routes`: each token names 6 different experts; among the 128 tokens of one device no expert is named more than 64 times. `span_order`: A permutation: each position block appears once.
All inputs are finite; a program needn't handle non-finite values.
Results may differ from a plain program's by a relative error of at most 0.025.
Values may be sent and summed in bfloat16 or wider, within the bound.
A program may use at most 320 MiB of HBM per device.

v0:
```python
import math

import jax
import jax.numpy as jnp
from jax import lax
from jax.sharding import PartitionSpec as P

D = 2048
NOPE = 128
ROPE = 64
VDIM = 128
RANK = 512
TOPK = 6


eps_norm = 1e-06
route_scale = 2.446
rope_base = 50000.0
masked_value = -1e30


def rope_tables(positions, width):
    count = width // 2
    exponents = jnp.arange(count, dtype=jnp.float32) * (2.0 / width)
    freqs = jnp.power(jnp.float32(rope_base), -exponents)
    angles = positions.astype(jnp.float32)[:, None] * freqs[None, :]
    cosine = jnp.cos(angles)
    sine = jnp.sin(angles)
    return (jnp.concatenate([cosine, cosine], axis=1), jnp.concatenate([sine, sine], axis=1))


def rotate(values, cosine, sine):
    count = values.shape[-1] // 2
    turned = jnp.concatenate([-values[..., count:], values[..., :count]], axis=-1)
    return values * cosine + turned * sine


def rotate_back(grads, cosine, sine):
    count = grads.shape[-1] // 2
    scaled = grads * sine
    turned = jnp.concatenate([scaled[..., count:], -scaled[..., :count]], axis=-1)
    return grads * cosine + turned


def rms_back(grad_normed, values, scale, gain):
    gained = grad_normed * gain
    gain_grad = jnp.sum(grad_normed * values * scale, axis=0)
    value_grad = scale * gained - values * (scale * scale * scale) * jnp.mean(
        gained * values, axis=1, keepdims=True
    )
    return (value_grad, gain_grad)


def gated_act(pre, width):
    gate = pre[:, :width]
    return (gate * jax.nn.sigmoid(gate) * pre[:, width:]).astype(jnp.bfloat16)


def gated_back(act_grad, pre, width):
    gate = pre[:, :width]
    upper = pre[:, width:]
    sig = jax.nn.sigmoid(gate)
    return jnp.concatenate(
        [act_grad * upper * sig * (1.0 + gate * (1.0 - sig)), act_grad * gate * sig], axis=1
    ).astype(jnp.bfloat16)


def expert_forward(rows, gate_up, down):
    width = down.shape[0]
    pre = jnp.dot(
        rows, gate_up.reshape(gate_up.shape[0], 2 * width), preferred_element_type=jnp.float32
    )
    result = jnp.dot(gated_act(pre, width), down, preferred_element_type=jnp.float32).astype(
        jnp.bfloat16
    )
    return (result, pre)


def expert_backward(rows, pre, grad_rows, gate_up, down):
    width = down.shape[0]
    flat = gate_up.reshape(gate_up.shape[0], 2 * width)
    act_grad = jnp.dot(grad_rows, down.T, preferred_element_type=jnp.float32)
    pre_grad = gated_back(act_grad, pre, width)
    down_grad = jnp.dot(gated_act(pre, width).T, grad_rows, preferred_element_type=jnp.float32)
    in_grad = jnp.dot(rows.T, pre_grad, preferred_element_type=jnp.float32).reshape(gate_up.shape)
    back = jnp.dot(pre_grad, flat.T, preferred_element_type=jnp.float32).astype(jnp.bfloat16)
    return (back, in_grad, down_grad)


def slot_places(route_block, experts, capacity):
    flat = route_block.reshape(-1)
    hits = (flat[:, None] == jnp.arange(experts, dtype=jnp.int32)[None, :]).astype(jnp.int32)
    ranks = jnp.sum(hits * jnp.cumsum(hits, axis=0), axis=1) - 1
    return flat * capacity + ranks


def block_scores(query_block, query_pos, key_block, rope_block, key_pos, score_scale):
    scores = jnp.einsum(
        "qhd,khd->hqk",
        query_block[:, :, :NOPE],
        key_block[:, :, :NOPE],
        preferred_element_type=jnp.float32,
    )
    scores = scores + jnp.einsum(
        "qhd,kd->hqk", query_block[:, :, NOPE:], rope_block, preferred_element_type=jnp.float32
    )
    scores = scores * score_scale
    allowed = key_pos[None, :] <= query_pos[:, None]
    return jnp.where(allowed[None, :, :], scores, masked_value)


def keep_state(state):
    return state


def shards(
    layer_input,
    cotangent,
    routes,
    span_order,
    attn_gain,
    query_proj,
    latent_proj,
    latent_gain,
    expand_proj,
    output_proj,
    moe_gain,
    router_proj,
    shared_in,
    shared_out,
    expert_in,
    expert_out,
):
    (
        attn_gain,
        query_proj,
        latent_proj,
        latent_gain,
        expand_proj,
        output_proj,
        moe_gain,
        router_proj,
        shared_in,
        shared_out,
    ) = (
        lax.all_gather(attn_gain, "dp", axis=0, tiled=True),
        lax.all_gather(query_proj, "dp", axis=0, tiled=True),
        lax.all_gather(latent_proj, "dp", axis=0, tiled=True),
        lax.all_gather(latent_gain, "dp", axis=0, tiled=True),
        lax.all_gather(expand_proj, "dp", axis=0, tiled=True),
        lax.all_gather(output_proj, "dp", axis=1, tiled=True),
        lax.all_gather(moe_gain, "dp", axis=0, tiled=True),
        lax.all_gather(router_proj, "dp", axis=0, tiled=True),
        lax.all_gather(shared_in, "dp", axis=0, tiled=True),
        lax.all_gather(shared_out, "dp", axis=1, tiled=True),
    )
    whole_input, whole_cot = (
        lax.all_gather(layer_input, "experts", axis=1, tiled=True),
        lax.all_gather(cotangent, "experts", axis=1, tiled=True),
    )
    rows_dev = layer_input.shape[1]
    inputs = whole_input[0].astype(jnp.float32)
    cot_rows = whole_cot[0]
    span_rows = inputs.shape[0]
    half = span_rows // 2
    heads_here = query_proj.shape[1] // (NOPE + ROPE)
    experts = router_proj.shape[1]
    score_scale = 1.0 / math.sqrt(NOPE + ROPE)
    mine = lax.axis_index("experts") * rows_dev
    offsets = jnp.arange(half, dtype=jnp.int32)
    query_order = lax.dynamic_slice_in_dim(span_order, 2 * lax.axis_index("context"), 2, 0)
    positions = (query_order[:, None] * half + offsets[None, :]).reshape(span_rows)
    cosine, sine = rope_tables(positions, ROPE)
    scale_one = lax.rsqrt(jnp.mean(inputs * inputs, axis=1, keepdims=True) + eps_norm)
    normed = (inputs * scale_one * attn_gain.astype(jnp.float32)).astype(jnp.bfloat16)
    query_raw = jnp.dot(normed, query_proj, preferred_element_type=jnp.float32).reshape(
        span_rows, heads_here, NOPE + ROPE
    )
    queries = jnp.concatenate(
        [
            query_raw[:, :, :NOPE],
            rotate(query_raw[:, :, NOPE:], cosine[:, None, :], sine[:, None, :]),
        ],
        axis=2,
    ).astype(jnp.bfloat16)
    compressed = jnp.dot(normed, latent_proj, preferred_element_type=jnp.float32)
    latent = compressed[:, :RANK]
    scale_latent = lax.rsqrt(jnp.mean(latent * latent, axis=1, keepdims=True) + eps_norm)
    latent_normed = (latent * scale_latent * latent_gain.astype(jnp.float32)).astype(jnp.bfloat16)
    key_rope = rotate(compressed[:, RANK:], cosine, sine).astype(jnp.bfloat16)
    own_keyvals = jnp.dot(latent_normed, expand_proj, preferred_element_type=jnp.float32).astype(
        jnp.bfloat16
    )
    outgoing_keys = jnp.concatenate([own_keyvals, key_rope], axis=1)
    gathered = lax.all_gather(outgoing_keys, "context", axis=0, tiled=True)
    total_rows = gathered.shape[0]
    blocks = total_rows // half
    keyvals = gathered[:, : heads_here * (NOPE + VDIM)]
    rope_all = gathered[:, gathered.shape[1] - ROPE :]
    key_blocks = keyvals.reshape(blocks, half, heads_here, NOPE + VDIM)
    rope_blocks = rope_all.reshape(blocks, half, ROPE)
    query_blocks = queries.reshape(2, half, heads_here, NOPE + ROPE)

    def forward_update(which, key_block, rope_block, key_pos):
        query_pos = query_order[which] * half + offsets

        def update(state):
            top, total, accum = state
            scores = block_scores(
                query_blocks[which], query_pos, key_block, rope_block, key_pos, score_scale
            )
            new_top = jnp.maximum(top, jnp.max(scores, axis=2))
            factor = jnp.exp(top - new_top)
            weights = jnp.exp(scores - new_top[:, :, None])
            total = total * factor + jnp.sum(weights, axis=2)
            accum = accum * factor[:, :, None] + jnp.einsum(
                "hqk,khd->hqd",
                weights.astype(jnp.bfloat16),
                key_block[:, :, NOPE:],
                preferred_element_type=jnp.float32,
            )
            return (new_top, total, accum)

        return update

    def forward_step(carry, pieces):
        key_block, rope_block, key_place = pieces
        key_pos = key_place * half + offsets
        updated = []
        for which in range(2):
            updated.append(
                lax.cond(
                    key_place <= query_order[which],
                    forward_update(which, key_block, rope_block, key_pos),
                    keep_state,
                    carry[which],
                )
            )
        return (tuple(updated), None)

    start_state = (
        jnp.full((heads_here, half), masked_value, jnp.float32),
        jnp.zeros((heads_here, half), jnp.float32),
        jnp.zeros((heads_here, half, VDIM), jnp.float32),
    )
    final_state, unused = lax.scan(
        forward_step, (start_state, start_state), (key_blocks, rope_blocks, span_order)
    )
    lses = jnp.stack(
        [
            final_state[0][0] + jnp.log(final_state[0][1]),
            final_state[1][0] + jnp.log(final_state[1][1]),
        ]
    )
    outs = [
        (final_state[which][2] / final_state[which][1][:, :, None]).transpose(1, 0, 2)
        for which in range(2)
    ]
    attended = (
        jnp.concatenate(outs, axis=0).reshape(span_rows, heads_here * VDIM).astype(jnp.bfloat16)
    )
    partial_heads = jnp.dot(attended, output_proj, preferred_element_type=jnp.float32)
    mixed = lax.psum(partial_heads.astype(jnp.bfloat16), "experts").astype(jnp.float32)
    hidden = inputs + mixed
    scale_two = lax.rsqrt(jnp.mean(hidden * hidden, axis=1, keepdims=True) + eps_norm)
    hidden_normed = (hidden * scale_two * moe_gain.astype(jnp.float32)).astype(jnp.bfloat16)
    own_normed = lax.dynamic_slice_in_dim(hidden_normed, mine, rows_dev, 0)
    gates = jax.nn.sigmoid(jnp.dot(own_normed, router_proj, preferred_element_type=jnp.float32))
    route_rows = routes[0]
    picked = (route_rows[:, :, None] == jnp.arange(experts, dtype=jnp.int32)[None, None, :]).astype(
        jnp.float32
    )
    chosen = jnp.sum(picked * gates[:, None, :], axis=2)
    chosen_total = jnp.sum(chosen, axis=1, keepdims=True)
    route_weights = route_scale * chosen / chosen_total
    capacity = rows_dev * TOPK * 4 // (3 * experts)
    halves = lax.axis_size("dp")
    places = slot_places(route_rows, experts, capacity)
    local_experts = expert_in.shape[0]

    def spread(values):
        filled = (
            jnp.zeros((experts * capacity, D), jnp.bfloat16)
            .at[places]
            .set(values)
            .reshape(1, experts, capacity, D)
        )
        return jnp.broadcast_to(filled, (halves, experts, capacity, D)).reshape(
            halves * experts, capacity, D
        )

    def collect(arrived):
        flat = arrived.reshape(halves, experts * capacity, D)[:, places]
        return jnp.sum(flat.astype(jnp.float32), axis=0).reshape(rows_dev, TOPK, D)

    def group(values):
        count = values.shape[1]
        sources = values.shape[0] // local_experts
        return (
            values.reshape(sources, local_experts, count, values.shape[2])
            .transpose(1, 0, 2, 3)
            .reshape(local_experts, sources * count, values.shape[2])
        )

    def ungroup(values, count):
        sources = values.shape[1] // count
        return (
            values.reshape(local_experts, sources, count, values.shape[2])
            .transpose(1, 0, 2, 3)
            .reshape(sources * local_experts, count, values.shape[2])
        )

    arrived = lax.all_to_all(
        spread(jnp.repeat(own_normed, TOPK, axis=0)),
        ("dp", "context", "experts"),
        split_axis=0,
        concat_axis=0,
        tiled=True,
    )
    count = arrived.shape[1]
    results, preacts = jax.vmap(expert_forward)(group(arrived), expert_in, expert_out)
    results, preacts, arrived = (ungroup(results, count), ungroup(preacts, count), arrived)
    returned = lax.all_to_all(
        results, ("dp", "context", "experts"), split_axis=0, concat_axis=0, tiled=True
    )
    expert_rows = collect(returned)
    routed = jnp.sum(route_weights[:, :, None] * expert_rows, axis=1)
    shared_width = shared_out.shape[0]
    shared_flat = shared_in.reshape(D, 2 * shared_width)
    shared_pre = jnp.dot(hidden_normed, shared_flat, preferred_element_type=jnp.float32)
    shared_act = gated_act(shared_pre, shared_width)
    shared_sum = lax.psum_scatter(
        jnp.dot(shared_act, shared_out, preferred_element_type=jnp.float32).astype(jnp.bfloat16),
        "experts",
        scatter_dimension=0,
        tiled=True,
    ).astype(jnp.float32)
    own_hidden = lax.dynamic_slice_in_dim(hidden, mine, rows_dev, 0)
    block_output = own_hidden + routed + shared_sum
    cot_own = cotangent[0].astype(jnp.float32)
    shared_pre_grad = gated_back(
        jnp.dot(cot_rows, shared_out.T, preferred_element_type=jnp.float32),
        shared_pre,
        shared_width,
    )
    shared_out_grad = jnp.dot(shared_act.T, cot_rows, preferred_element_type=jnp.float32)
    shared_in_grad = jnp.dot(
        hidden_normed.T, shared_pre_grad, preferred_element_type=jnp.float32
    ).reshape(D, 2, shared_width)
    normed_grad = jnp.dot(shared_pre_grad, shared_flat.T, preferred_element_type=jnp.float32)
    weight_grad = jnp.sum(cot_own[:, None, :] * expert_rows, axis=2)
    sent = (
        (route_weights[:, :, None] * cot_own[:, None, :])
        .astype(jnp.bfloat16)
        .reshape(rows_dev * TOPK, D)
    )
    arrived_grad = lax.all_to_all(
        spread(sent), ("dp", "context", "experts"), split_axis=0, concat_axis=0, tiled=True
    )
    backs, expert_in_grad, expert_out_grad = jax.vmap(expert_backward)(
        group(arrived), group(preacts), group(arrived_grad), expert_in, expert_out
    )
    back_rows = lax.all_to_all(
        ungroup(backs, capacity),
        ("dp", "context", "experts"),
        split_axis=0,
        concat_axis=0,
        tiled=True,
    )
    routed_grad = jnp.sum(collect(back_rows), axis=1)
    chosen_grad = route_scale * weight_grad / chosen_total - route_scale * jnp.sum(
        weight_grad * chosen, axis=1, keepdims=True
    ) / (chosen_total * chosen_total)
    logit_grad = jnp.sum(picked * (chosen_grad * chosen * (1.0 - chosen))[:, :, None], axis=1)
    own_grad_rows = routed_grad + jnp.dot(
        logit_grad, router_proj.astype(jnp.float32).T, precision=lax.Precision.HIGHEST
    )
    router_grad = jnp.dot(
        own_normed.astype(jnp.float32).T, logit_grad, precision=lax.Precision.HIGHEST
    )
    normed_grad = lax.dynamic_update_slice_in_dim(
        normed_grad,
        lax.dynamic_slice_in_dim(normed_grad, mine, rows_dev, 0) + own_grad_rows,
        mine,
        0,
    )
    normed_grad, router_grad = (
        lax.psum(normed_grad.astype(jnp.bfloat16), "experts").astype(jnp.float32),
        lax.psum(router_grad.astype(jnp.bfloat16), "experts").astype(jnp.float32),
    )
    norm_part, moe_gain_grad = rms_back(
        normed_grad, hidden, scale_two, moe_gain.astype(jnp.float32)
    )
    hidden_grad = cot_rows.astype(jnp.float32) + norm_part
    hidden_round = hidden_grad.astype(jnp.bfloat16)
    output_proj_grad = jnp.dot(attended.T, hidden_round, preferred_element_type=jnp.float32)
    attended_grad = jnp.dot(hidden_round, output_proj.T, preferred_element_type=jnp.float32).astype(
        jnp.bfloat16
    )
    out_blocks = attended.reshape(2, half, heads_here, VDIM)
    grad_blocks = attended_grad.reshape(2, half, heads_here, VDIM)
    deltas = jnp.sum(
        out_blocks.astype(jnp.float32) * grad_blocks.astype(jnp.float32), axis=3
    ).transpose(0, 2, 1)

    def backward_update(which, key_block, rope_block, key_pos):
        query_pos = query_order[which] * half + offsets
        query_block = query_blocks[which]
        grad_block = grad_blocks[which]

        def update(state):
            query_grad, key_grad, rope_grad = state
            scores = block_scores(
                query_block, query_pos, key_block, rope_block, key_pos, score_scale
            )
            probs = jnp.exp(scores - lses[which][:, :, None])
            prob_round = probs.astype(jnp.bfloat16)
            prob_grad = jnp.einsum(
                "qhd,khd->hqk",
                grad_block,
                key_block[:, :, NOPE:],
                preferred_element_type=jnp.float32,
            )
            score_grad = (probs * (prob_grad - deltas[which][:, :, None])).astype(jnp.bfloat16)
            query_grad = query_grad + score_scale * jnp.concatenate(
                [
                    jnp.einsum(
                        "hqk,khd->qhd",
                        score_grad,
                        key_block[:, :, :NOPE],
                        preferred_element_type=jnp.float32,
                    ),
                    jnp.einsum(
                        "hqk,kd->qhd", score_grad, rope_block, preferred_element_type=jnp.float32
                    ),
                ],
                axis=2,
            )
            key_grad = key_grad + jnp.concatenate(
                [
                    score_scale
                    * jnp.einsum(
                        "hqk,qhd->khd",
                        score_grad,
                        query_block[:, :, :NOPE],
                        preferred_element_type=jnp.float32,
                    ),
                    jnp.einsum(
                        "hqk,qhd->khd", prob_round, grad_block, preferred_element_type=jnp.float32
                    ),
                ],
                axis=2,
            )
            rope_grad = rope_grad + score_scale * jnp.einsum(
                "hqk,qhd->kd",
                score_grad,
                query_block[:, :, NOPE:],
                preferred_element_type=jnp.float32,
            )
            return (query_grad, key_grad, rope_grad)

        return update

    def backward_step(carry, pieces):
        key_block, rope_block, key_place = pieces
        key_pos = key_place * half + offsets
        key_grad = jnp.zeros((half, heads_here, NOPE + VDIM), jnp.float32)
        rope_grad = jnp.zeros((half, ROPE), jnp.float32)
        updated = []
        for which in range(2):
            query_grad, key_grad, rope_grad = lax.cond(
                key_place <= query_order[which],
                backward_update(which, key_block, rope_block, key_pos),
                keep_state,
                (carry[which], key_grad, rope_grad),
            )
            updated.append(query_grad)
        return (tuple(updated), (key_grad, rope_grad))

    zero_query = jnp.zeros((half, heads_here, NOPE + ROPE), jnp.float32)
    query_grads, (key_grads, rope_grads) = lax.scan(
        backward_step, (zero_query, zero_query), (key_blocks, rope_blocks, span_order)
    )
    keyval_grad = key_grads.reshape(total_rows, heads_here * (NOPE + VDIM))
    rope_grad_all = rope_grads.reshape(total_rows, ROPE)
    expand_float = expand_proj.astype(jnp.float32)
    outgoing_grad = jnp.concatenate([keyval_grad, rope_grad_all], axis=1)
    own_grad = lax.psum_scatter(
        outgoing_grad.astype(jnp.bfloat16), "context", scatter_dimension=0, tiled=True
    ).astype(jnp.float32)
    own_keyval_grad = own_grad[:, : heads_here * (NOPE + VDIM)]
    latent_part = jnp.concatenate(
        [
            jnp.dot(own_keyval_grad, expand_float.T, precision=lax.Precision.HIGHEST),
            own_grad[:, own_grad.shape[1] - ROPE :],
        ],
        axis=1,
    )
    expand_grad = jnp.dot(
        latent_normed.astype(jnp.float32).T, own_keyval_grad, precision=lax.Precision.HIGHEST
    )
    query_grad = jnp.concatenate([query_grads[0], query_grads[1]], axis=0)
    query_raw_grad = (
        jnp.concatenate(
            [
                query_grad[:, :, :NOPE],
                rotate_back(query_grad[:, :, NOPE:], cosine[:, None, :], sine[:, None, :]),
            ],
            axis=2,
        )
        .reshape(span_rows, heads_here * (NOPE + ROPE))
        .astype(jnp.bfloat16)
    )
    query_proj_grad = jnp.dot(normed.T, query_raw_grad, preferred_element_type=jnp.float32)
    input_normed_grad = jnp.dot(query_raw_grad, query_proj.T, preferred_element_type=jnp.float32)
    input_normed_grad, latent_part = (
        lax.psum(input_normed_grad.astype(jnp.bfloat16), "experts").astype(jnp.float32),
        lax.psum(latent_part.astype(jnp.bfloat16), "experts").astype(jnp.float32),
    )
    latent_grad, latent_gain_grad = rms_back(
        latent_part[:, :RANK], latent, scale_latent, latent_gain.astype(jnp.float32)
    )
    compressed_grad = jnp.concatenate(
        [latent_grad, rotate_back(latent_part[:, RANK:], cosine, sine)], axis=1
    ).astype(jnp.bfloat16)
    latent_proj_grad = jnp.dot(normed.T, compressed_grad, preferred_element_type=jnp.float32)
    input_normed_grad = input_normed_grad + jnp.dot(
        compressed_grad, latent_proj.T, preferred_element_type=jnp.float32
    )
    first_part, attn_gain_grad = rms_back(
        input_normed_grad, inputs, scale_one, attn_gain.astype(jnp.float32)
    )
    input_grad = lax.dynamic_slice_in_dim(hidden_grad + first_part, mine, rows_dev, 0)
    (
        attn_gain_grad,
        query_proj_grad,
        latent_proj_grad,
        latent_gain_grad,
        expand_grad,
        output_proj_grad,
        moe_gain_grad,
        router_grad,
        shared_in_grad,
        shared_out_grad,
    ) = (
        lax.psum_scatter(
            attn_gain_grad.astype(jnp.bfloat16), "dp", scatter_dimension=0, tiled=True
        ).astype(jnp.float32),
        lax.psum_scatter(
            query_proj_grad.astype(jnp.bfloat16), "dp", scatter_dimension=0, tiled=True
        ).astype(jnp.float32),
        lax.psum_scatter(
            latent_proj_grad.astype(jnp.bfloat16), "dp", scatter_dimension=0, tiled=True
        ).astype(jnp.float32),
        lax.psum_scatter(
            latent_gain_grad.astype(jnp.bfloat16), "dp", scatter_dimension=0, tiled=True
        ).astype(jnp.float32),
        lax.psum_scatter(
            expand_grad.astype(jnp.bfloat16), "dp", scatter_dimension=0, tiled=True
        ).astype(jnp.float32),
        lax.psum_scatter(
            output_proj_grad.astype(jnp.bfloat16), "dp", scatter_dimension=1, tiled=True
        ).astype(jnp.float32),
        lax.psum_scatter(
            moe_gain_grad.astype(jnp.bfloat16), "dp", scatter_dimension=0, tiled=True
        ).astype(jnp.float32),
        lax.psum_scatter(
            router_grad.astype(jnp.bfloat16), "dp", scatter_dimension=0, tiled=True
        ).astype(jnp.float32),
        lax.psum_scatter(
            shared_in_grad.astype(jnp.bfloat16), "dp", scatter_dimension=0, tiled=True
        ).astype(jnp.float32),
        lax.psum_scatter(
            shared_out_grad.astype(jnp.bfloat16), "dp", scatter_dimension=1, tiled=True
        ).astype(jnp.float32),
    )
    (
        attn_gain_grad,
        query_proj_grad,
        latent_proj_grad,
        latent_gain_grad,
        expand_grad,
        output_proj_grad,
        moe_gain_grad,
        router_grad,
        shared_in_grad,
        shared_out_grad,
    ) = (
        lax.psum(attn_gain_grad.astype(jnp.bfloat16), "context").astype(jnp.float32),
        lax.psum(query_proj_grad.astype(jnp.bfloat16), "context").astype(jnp.float32),
        lax.psum(latent_proj_grad.astype(jnp.bfloat16), "context").astype(jnp.float32),
        lax.psum(latent_gain_grad.astype(jnp.bfloat16), "context").astype(jnp.float32),
        lax.psum(expand_grad.astype(jnp.bfloat16), "context").astype(jnp.float32),
        lax.psum(output_proj_grad.astype(jnp.bfloat16), "context").astype(jnp.float32),
        lax.psum(moe_gain_grad.astype(jnp.bfloat16), "context").astype(jnp.float32),
        lax.psum(router_grad.astype(jnp.bfloat16), "context").astype(jnp.float32),
        lax.psum(shared_in_grad.astype(jnp.bfloat16), "context").astype(jnp.float32),
        lax.psum(shared_out_grad.astype(jnp.bfloat16), "context").astype(jnp.float32),
    )
    return (
        block_output[None],
        input_grad[None],
        attn_gain_grad,
        query_proj_grad,
        latent_proj_grad,
        latent_gain_grad,
        expand_grad,
        output_proj_grad,
        moe_gain_grad,
        router_grad,
        shared_in_grad,
        shared_out_grad,
        expert_in_grad,
        expert_out_grad,
    )


def solution(mesh):
    return jax.shard_map(
        shards,
        mesh=mesh,
        in_specs=(
            P("dp", ("context", "experts"), None),
            P("dp", ("context", "experts"), None),
            P("dp", ("context", "experts"), None),
            P(),
            P("dp"),
            P("dp", "experts"),
            P("dp", None),
            P("dp"),
            P("dp", "experts"),
            P("experts", "dp"),
            P("dp"),
            P("dp", None),
            P("dp", None, "experts"),
            P("experts", "dp"),
            P(("context", "experts"), None, None, "dp"),
            P(("context", "experts"), "dp", None),
        ),
        out_specs=(
            P("dp", ("context", "experts"), None),
            P("dp", ("context", "experts"), None),
            P("dp"),
            P("dp", "experts"),
            P("dp", None),
            P("dp"),
            P("dp", "experts"),
            P("experts", "dp"),
            P("dp"),
            P("dp", None),
            P("dp", None, "experts"),
            P("experts", "dp"),
            P(("context", "experts"), None, None, "dp"),
            P(("context", "experts"), "dp", None),
        ),
        check_vma=False,
    )
```

profile of v0, /device:TPU:0, one launch (start us, length us, event | category | flops | bytes accessed | tf_op | source)
XLA Modules:
  0.0 2428.6 jit_solution(16837026591376769476)
XLA Ops:
  21.6 13.3 all-gather.11.cloned.1.call-done
  37.6 34.9 %all-gather.13.cloned.1.call-done = bf16[2048,576]{0,1:T(8,128)(2,1)} async-done(((bf16[1024,576]{0,1:T(8,128)(2,1)}), bf16[2048,576]{0,1:T(8,128)(2,1)}) %all-gather.13.cloned.1.call-update) | async-done | bytes 2359312 | tf_op jit(solution)/shard_map/all_gather | solution.py:148
  80.1 15.3 all-gather.15.cloned.1.call-done
  101.6 40.2 %all-gather.19.cloned.1.call-done = bf16[2048,768]{1,0:T(8,128)(2,1)} async-done(((bf16[1024,768]{1,0:T(8,128)(2,1)}), bf16[2048,768]{1,0:T(8,128)(2,1)}) %all-gather.19.cloned.1.call-update) | async-done | bytes 3145744 | tf_op jit(solution)/shard_map/all_gather | solution.py:147
  160.0 73.1 %all-gather.17.cloned.1.call-done = bf16[2048,1088]{1,0:T(8,128)(2,1)} async-done(((bf16[512,1088]{1,0:T(8,128)(2,1)}), bf16[2048,1088]{1,0:T(8,128)(2,1)}) %all-gather.17.cloned.1.call-update) | async-done | bytes 4456464 | tf_op jit(solution)/shard_map/all_gather | solution.py:195
  237.8 8.0 reshape.557
  253.4 67.9 %while.45 = (s32[]{:T(128)}, f32[4,256]{1,0:T(4,128)S(1)}, f32[4,256]{1,0:T(4,128)S(1)}, f32[4,256,128]{2,1,0:T(8,128)}, f32[4,256]{1,0:T(4,128)S(1)}, /*index=5...) while((s32[]{:T(128)}, f32[4,256]{1,0:T(4,128)S(1)}, ...), condition=%wide.region_11.12_spmd.clone.clone, body=%wide.region_2.11_spmd.clone.clone.sunk | while | flops 340398848 | bytes 26225244 | solution.py:246
  337.7 69.6 %all-reduce.12.cloned.1.call-done = bf16[512,2048]{1,0:T(8,128)(2,1)} async-done(((bf16[512,2048]{1,0:T(8,128)(2,1)}), bf16[512,2048]{1,0:T(8,128)(2,1)}) %all-reduce.12.cloned.1.call-update) | async-done | bytes 2097168 | tf_op jit(solution)/shard_map/psum | solution.py:263
  422.6 10.5 scatter_custom_fusion
  451.3 8.3 mul.639
  459.6 39.8 %all_gather.48 = bf16[2048,16]{0,1:T(8,128)(2,1)S(1)} all-gather(bf16[1024,16]{0,1:T(8,128)(2,1)S(1)} %copy-done.63), channel_id=1, replica_groups=mesh['dp'=2,'context'=4,'experts'=4] {'dp'}, dimensions={0}, use_global_device_ids=true | all-gather | bytes 98304 | tf_op jit(solution)/shard_map/all_gather | solution.py:153
  500.3 14.5 scatter_custom_fusion.1
  514.9 114.7 %all-to-all-done = bf16[32,64,2048]{2,1,0:T(8,128)(2,1)} async-done(((bf16[32,64,2048]{2,1,0:T(8,128)(2,1)}), bf16[32,64,2048]{2,1,0:T(8,128)(2,1)}, u32[]{:S(2)}, u32[]{:S(2)}) %all-to-all-start) | async-done | bytes 8388640 | tf_op jit(solution)/shard_map/all_to_all | solution.py:313
  640.3 18.8 convolution_bitcast_fusion.12
  659.2 165.9 %all-to-all-done.2 = bf16[32,64,2048]{2,1,0:T(8,128)(2,1)} async-done(((bf16[32,64,2048]{2,1,0:T(8,128)(2,1)}), bf16[32,64,2048]{2,1,0:T(8,128)(2,1)}, u32[]{:S(2)}, u32[]{:S(2)}) %all-to-all-start.2) | async-done | bytes 8388640 | tf_op jit(solution)/shard_map/all_to_all | solution.py:357
  825.0 15.1 fusion.116
  840.1 9.5 convolution_convert_fusion.2
  853.5 18.3 convolution_convert_fusion.1
  871.8 166.4 %all-to-all-done.1 = bf16[32,64,2048]{2,1,0:T(8,128)(2,1)} async-done(((bf16[32,64,2048]{2,1,0:T(8,128)(2,1)}), bf16[32,64,2048]{2,1,0:T(8,128)(2,1)}, u32[]{:S(2)}, u32[]{:S(2)}) %all-to-all-start.1) | async-done | bytes 8388640 | tf_op jit(solution)/shard_map/all_to_all | solution.py:323
  1044.1 142.8 %all-gather.23.cloned.1.call-done = bf16[2048,2,704]{0,2,1:T(8,128)(2,1)} async-done(((bf16[1024,2,704]{0,2,1:T(8,128)(2,1)}), bf16[2048,2,704]{0,2,1:T(8,128)(2,1)}) %all-gather.23.cloned.1.call-update) | async-done | bytes 5767184 | tf_op jit(solution)/shard_map/all_gather | solution.py:154
  1186.9 7.7 fusion.167
  1194.6 47.4 %all-gather.25.cloned.1.call-done = bf16[704,2048]{1,0:T(8,128)(2,1)} async-done(((bf16[704,1024]{1,0:T(8,128)(2,1)}), bf16[704,2048]{1,0:T(8,128)(2,1)}) %all-gather.25.cloned.1.call-update) | async-done | bytes 2883600 | tf_op jit(solution)/shard_map/all_gather | solution.py:155
  1242.0 23.8 all-gather.27.cloned.1.call-done
  1272.3 8.2 fusion.139
  1280.5 16.4 copy.245
  1296.9 30.3 %gather_fusion = bf16[768,2,2048]{2,1,0:T(2,128)(2,1)} fusion(bf16[2,1024,2048]{2,0,1:T(2,128)(2,1)} %copy.245, s32[1024]{0:T(1024)S(1)} %pad_clamp_fusion), kind=kCustom, calls=%fused_computation | custom fusion | bytes 12585984 | tf_op jit(solution)/shard_map/gather | solution.py:293
  1327.2 21.1 convert_reduce_fusion.1
  1348.3 7.9 reshape.567
  1363.6 16.4 copy.249
  1380.0 30.5 %gather_fusion.1 = bf16[768,2,2048]{2,1,0:T(2,128)(2,1)} fusion(bf16[2,1024,2048]{2,0,1:T(2,128)(2,1)} %copy.249, s32[1024]{0:T(1024)S(1)} %pad_clamp_fusion), kind=kCustom, calls=%fused_computation.1 | custom fusion | bytes 12585984 | tf_op jit(solution)/shard_map/gather | solution.py:293
  1410.5 21.1 convert_reduce_fusion
  1431.6 7.8 reshape.572
  1452.5 51.4 %all-reduce.14.cloned.1.call-done = bf16[512,2048]{1,0:T(8,128)(2,1)} async-done(((bf16[512,2048]{1,0:T(8,128)(2,1)}), bf16[512,2048]{1,0:T(8,128)(2,1)}) %all-reduce.14.cloned.1.call-update) | async-done | bytes 2097168 | tf_op jit(solution)/shard_map/psum | solution.py:388
  1516.6 84.5 %while.46 = (s32[]{:T(128)}, f32[256,4,192]{0,2,1:T(8,128)}, f32[256,4,192]{0,2,1:T(8,128)}, bf16[8,256,4,256]{1,3,2,0:T(8,128)(2,1)}, bf16[8,256,64]{1,2,0:T(8,...) while((s32[]{:T(128)}, f32[256,4,192]{0,2,1:T(8,128)}, ...), condition=%wide.region_37.38_spmd.clone.clone, body=%wide.region_32.37_spmd.clone.clone.sunk | while | flops 879018752 | bytes 45919280 | solution.py:481
  1616.6 115.5 %reduce-scatter.12.cloned.1.call-done = bf16[512,1088]{0,1:T(8,128)(2,1)} async-done(((bf16[2048,1088]{0,1:T(8,128)(2,1)}), bf16[512,1088]{0,1:T(8,128)(2,1)}) %reduce-scatter.12.cloned.1.call-update) | async-done | bytes 1114128 | tf_op jit(solution)/shard_map/reduce_scatter | solution.py:488
  1740.9 7.5 convolution_convert_fusion
  1761.9 35.5 %all-reduce.16.cloned.1.call-done = (bf16[512,2048]{1,0:T(8,128)(2,1)}, bf16[512,576]{0,1:T(8,128)(2,1)}) async-done(((bf16[512,2048]{1,0:T(8,128)(2,1)}, bf16[512,576]{0,1:T(8,128)(2,1)}), (bf16[512,2048]{1,0:T(8,128)(2,1)}, bf16[512,576]{0,1:T(8,128)(2,1)})) %all-reduce.16.cloned.1.call-update) | async-done | bytes 2686992 | tf_op jit(solution)/shard_map/psum | solution.py:517
  1811.7 29.1 %reduce-scatter.24.cloned.1.call-done = bf16[704,1024]{1,0:T(8,128)(2,1)} async-done(((bf16[704,2048]{1,0:T(8,128)(2,1)}), bf16[704,1024]{1,0:T(8,128)(2,1)}) %reduce-scatter.24.cloned.1.call-update) | async-done | bytes 1441808 | tf_op jit(solution)/shard_map/reduce_scatter | solution.py:573
  1840.8 74.2 %reduce-scatter.22.cloned.1.call-done = bf16[1024,2,704]{0,2,1:T(8,128)(2,1)} async-done(((bf16[2048,2,704]{0,2,1:T(8,128)(2,1)}), bf16[1024,2,704]{0,2,1:T(8,128)(2,1)}) %reduce-scatter.22.cloned.1.call-update) | async-done | bytes 2883600 | tf_op jit(solution)/shard_map/reduce_scatter | solution.py:570
  1915.0 34.6 %reduce-scatter.20.cloned.1.call-done = bf16[512,1024]{1,0:T(8,128)(2,1)} async-done(((bf16[512,2048]{1,0:T(8,128)(2,1)}), bf16[512,1024]{1,0:T(8,128)(2,1)}) %reduce-scatter.20.cloned.1.call-update) | async-done | bytes 1048592 | tf_op jit(solution)/shard_map/reduce_scatter | solution.py:561
  1949.6 46.1 %reduce-scatter.14.cloned.1.call-done = bf16[1024,768]{1,0:T(8,128)(2,1)} async-done(((bf16[2048,768]{1,0:T(8,128)(2,1)}), bf16[1024,768]{1,0:T(8,128)(2,1)}) %reduce-scatter.14.cloned.1.call-update) | async-done | bytes 1572880 | tf_op jit(solution)/shard_map/reduce_scatter | solution.py:549
  1995.7 23.1 reduce-scatter.18.cloned.1.call-done
  2018.8 37.7 %reduce-scatter.16.cloned.1.call-done = bf16[1024,576]{0,1:T(8,128)(2,1)} async-done(((bf16[2048,576]{0,1:T(8,128)(2,1)}), bf16[1024,576]{0,1:T(8,128)(2,1)}) %reduce-scatter.16.cloned.1.call-update) | async-done | bytes 1179664 | tf_op jit(solution)/shard_map/reduce_scatter | solution.py:552
  2063.5 11.0 convolution_bitcast_fusion.14
  2074.5 17.1 convolution_bitcast_fusion.13
  2091.6 12.8 psum.120
  2119.5 21.4 all-reduce.4
  2146.6 261.6 %all-reduce.18.cloned.1.call-done = (bf16[1024,768]{1,0:T(8,128)(2,1)}, bf16[1024,576]{0,1:T(8,128)(2,1)}, bf16[256,1024]{1,0:T(8,128)(2,1)}, bf16[512,1024]{1,0...) async-done(((bf16[1024,768]{1,0:T(8,128)(2,1)}, bf16[1024,576]{0,1:T(8,128)(2,1)}, bf16[256,1024]{1,0:T(8,128)(2,1)}, bf16[512,1024]{1,0:T(8,128)(2,1)}, ...) | async-done | bytes 8650768 | tf_op jit(solution)/shard_map/psum | solution.py:590
  (673 shorter events, 404.1 us)
Async XLA Ops:
  7.2 817.9 %copy-start = (bf16[1,704,2048]{2,1,0:T(8,128)(2,1)S(1)}, bf16[1,704,2048]{2,1,0:T(8,128)(2,1)}, u32[]{:S(2)}) copy-start(bf16[1,704,2048]{2,1,0:T(8,128)(2,1)} %param.43) | copy-start | bytes 8650756
  7.2 27.7 %all-gather.11.cloned.1.call-start = ((), (), s32[]{:S(2)}) async-start(), calls=%async_computation.13 | async-start | bytes 2621440 | tf_op jit(solution)/shard_map/all_gather | solution.py:158
  7.9 64.6 %all-gather.13.cloned.1.call-start = ((), (), s32[]{:S(2)}) async-start(), calls=%async_computation.14 | async-start | bytes 3538944 | tf_op jit(solution)/shard_map/all_gather | solution.py:148
  8.7 86.7 %all-gather.15.cloned.1.call-start = ((), (), s32[]{:S(2)}) async-start(), calls=%async_computation.15 | async-start | bytes 1572864 | tf_op jit(solution)/shard_map/all_gather | solution.py:150
  9.4 132.3 %all-gather.19.cloned.1.call-start = ((), (), s32[]{:S(2)}) async-start(), calls=%async_computation.17 | async-start | bytes 4718592 | tf_op jit(solution)/shard_map/all_gather | solution.py:147
  10.0 223.1 %all-gather.17.cloned.1.call-start = ((), (), s32[]{:S(2)}) async-start(), calls=%async_computation.16 | async-start | bytes 5898240 | tf_op jit(solution)/shard_map/all_gather | solution.py:195
  15.5 130.8 %copy-start.72 = (f32[2048]{0:T(1024)}, f32[2048]{0:T(1024)S(1)}, u32[]{:S(2)}) copy-start(f32[2048]{0:T(1024)S(1)} %convert_element_type.311) | copy-start | bytes 24580
  21.3 74.1 %copy-start.67 = (f32[2,1,256]{2,1,0:T(1,128)}, f32[2,1,256]{2,1,0:T(1,128)S(1)}, u32[]{:S(2)}) copy-start(f32[2,1,256]{2,1,0:T(1,128)S(1)} %convert_element_type.391) | copy-start | bytes 6148
  21.6 54.7 %copy-start.45 = (f32[512,32]{0,1:T(8,128)}, f32[512,32]{0,1:T(8,128)S(1)}, u32[]{:S(2)}) copy-start(f32[512,32]{0,1:T(8,128)S(1)} %get-tuple-element.966) | copy-start | bytes 196612
  21.6 54.7 %copy-start.47 = (f32[512,32]{0,1:T(8,128)}, f32[512,32]{0,1:T(8,128)S(1)}, u32[]{:S(2)}) copy-start(f32[512,32]{0,1:T(8,128)S(1)} %get-tuple-element.965) | copy-start | bytes 196612
  37.6 108.8 %copy-start.75 = (f32[512]{0:T(512)}, f32[512]{0:T(512)S(1)}, u32[]{:S(2)}) copy-start(f32[512]{0:T(512)S(1)} %get-tuple-element.968) | copy-start | bytes 6148
  78.0 72.9 %copy-start.32 = (f32[512,64]{0,1:T(8,128)}, f32[512,64]{0,1:T(8,128)S(1)}, u32[]{:S(2)}) copy-start(f32[512,64]{0,1:T(8,128)S(1)} %get-tuple-element.964) | copy-start | bytes 393220
  80.1 66.3 %copy-start.65 = (f32[512]{0:T(512)}, f32[512]{0:T(512)S(1)}, u32[]{:S(2)}) copy-start(f32[512]{0:T(512)S(1)} %get-tuple-element.970) | copy-start | bytes 6148
  98.9 227.0 %all-gather.21.cloned.1.call-start = ((), (), s32[]{:S(2)}) async-start(), calls=%async_computation.18 | async-start | bytes 3145728 | tf_op jit(solution)/shard_map/all_gather | solution.py:151
  99.4 307.9 %all-reduce.12.cloned.1.call-start = ((), (), s32[]{:S(2)}) async-start(), calls=%async_computation.19 | async-start | bytes 4194304 | tf_op jit(solution)/shard_map/psum | solution.py:263
  321.3 8.9 copy-start.41
  335.3 75.8 %copy-start.59 = (f32[2048]{0:T(1024)}, f32[2048]{0:T(1024)S(1)}, u32[]{:S(2)}) copy-start(f32[2048]{0:T(1024)S(1)} %convert_element_type.326) | copy-start | bytes 24580
  413.6 85.8 %copy-start.18 = (bf16[128,2048]{1,0:T(8,128)(2,1)}, bf16[128,2048]{1,0:T(8,128)(2,1)S(1)}, u32[]{:S(2)}) copy-start(bf16[128,2048]{1,0:T(8,128)(2,1)S(1)} %constant_dynamic-slice_fusion) | copy-start | bytes 1572868
  440.0 189.6 %all-to-all-start = ((bf16[32,64,2048]{2,1,0:T(8,128)(2,1)}), bf16[32,64,2048]{2,1,0:T(8,128)(2,1)}, u32[]{:S(2)}, u32[]{:S(2)}) async-start(bf16[32,64,2048]{2,1,0:T(8,128)(2,1)} %bitcast.362), calls=%async_computation | async-start | bytes 16777216 | tf_op jit(solution)/shard_map/all_to_all | solution.py:313
  636.5 188.6 %all-to-all-start.2 = ((bf16[32,64,2048]{2,1,0:T(8,128)(2,1)}), bf16[32,64,2048]{2,1,0:T(8,128)(2,1)}, u32[]{:S(2)}, u32[]{:S(2)}) async-start(bf16[32,64,2048]{2,1,0:T(8,128)(2,1)} %bitcast.363), calls=%async_computation.3 | async-start | bytes 16777216 | tf_op jit(solution)/shard_map/all_to_all | solution.py:357
  840.1 9.5 copy-start.85
  849.6 188.6 %all-to-all-start.1 = ((bf16[32,64,2048]{2,1,0:T(8,128)(2,1)}), bf16[32,64,2048]{2,1,0:T(8,128)(2,1)}, u32[]{:S(2)}, u32[]{:S(2)}) async-start(bf16[32,64,2048]{2,1,0:T(8,128)(2,1)} %bitcast.370), calls=%async_computation.1 | async-start | bytes 16777216 | tf_op jit(solution)/shard_map/all_to_all | solution.py:323
  1038.2 325.4 %all-to-all-start.3 = ((bf16[32,64,2048]{2,1,0:T(8,128)(2,1)}), bf16[32,64,2048]{2,1,0:T(8,128)(2,1)}, u32[]{:S(2)}, u32[]{:S(2)}) async-start(bf16[32,64,2048]{2,1,0:T(8,128)(2,1)} %bitcast.369), calls=%async_computation.4 | async-start | bytes 16777216 | tf_op jit(solution)/shard_map/all_to_all | solution.py:363
  1041.9 145.0 %copy-start.22 = (bf16[512,2048]{1,0:T(8,128)(2,1)S(1)}, bf16[512,2048]{1,0:T(8,128)(2,1)}, u32[]{:S(2)}) copy-start(bf16[512,2048]{1,0:T(8,128)(2,1)} %copy-done.21) | copy-start | bytes 6291460
  1041.9 145.0 %all-gather.23.cloned.1.call-start = ((), (), s32[]{:S(2)}) async-start(), calls=%async_computation.20 | async-start | bytes 8650752 | tf_op jit(solution)/shard_map/all_gather | solution.py:154
  1042.7 199.3 %all-gather.25.cloned.1.call-start = ((), (), s32[]{:S(2)}) async-start(), calls=%async_computation.21 | async-start | bytes 4325376 | tf_op jit(solution)/shard_map/all_gather | solution.py:155
  1043.4 222.4 %all-gather.27.cloned.1.call-start = ((), (), s32[]{:S(2)}) async-start(), calls=%async_computation.23 | async-start | bytes 2621440 | tf_op jit(solution)/shard_map/all_gather | solution.py:159
  1044.0 459.9 %all-reduce.14.cloned.1.call-start = ((), (), s32[]{:S(2)}) async-start(), calls=%async_computation.24 | async-start | bytes 4194304 | tf_op jit(solution)/shard_map/psum | solution.py:388
  1448.3 55.6 %copy-start.3 = (bf16[1,512,2048]{2,1,0:T(8,128)(2,1)S(1)}, bf16[1,512,2048]{2,1,0:T(8,128)(2,1)}, u32[]{:S(2)}) copy-start(bf16[1,512,2048]{2,1,0:T(8,128)(2,1)} %all-gather.11.cloned.1.call-done) | copy-start | bytes 6291460
  1448.3 55.6 %copy-start.60 = (f32[2048]{0:T(1024)S(1)}, f32[2048]{0:T(1024)}, u32[]{:S(2)}) copy-start(f32[2048]{0:T(1024)} %copy-done.59) | copy-start | bytes 24580
  1448.3 55.6 %copy-start.62 = (f32[512]{0:T(512)S(1)}, f32[512]{0:T(512)}, u32[]{:S(2)}) copy-start(f32[512]{0:T(512)} %copy-done.61) | copy-start | bytes 6148
  1452.3 56.1 %copy-start.71 = (f32[512]{0:T(512)S(1)}, f32[512]{0:T(512)}, u32[]{:S(2)}) copy-start(f32[512]{0:T(512)} %get-tuple-element.971) | copy-start | bytes 6148
  1452.3 279.8 %reduce-scatter.12.cloned.1.call-start = ((), (), s32[]{:S(2)}) async-start(), calls=%async_computation.25 | async-start | bytes 5570560 | tf_op jit(solution)/shard_map/reduce_scatter | solution.py:488
  1609.7 187.7 %all-reduce.16.cloned.1.call-start = ((), (), s32[]{:S(2)}) async-start(), calls=%async_computation.33 | async-start | bytes 5373952 | tf_op jit(solution)/shard_map/psum | solution.py:517
  1613.4 118.7 %copy-start.80 = (bf16[512,1024]{1,0:T(8,128)(2,1)S(1)}, bf16[512,1024]{1,0:T(8,128)(2,1)}, u32[]{:S(2)}) copy-start(bf16[512,1024]{1,0:T(8,128)(2,1)} %all-gather.15.cloned.1.call-done) | copy-start | bytes 3145732
  1616.6 119.2 %copy-start.82 = (bf16[512,704]{1,0:T(8,128)(2,1)S(1)}, bf16[512,704]{1,0:T(8,128)(2,1)}, u32[]{:S(2)}) copy-start(bf16[512,704]{1,0:T(8,128)(2,1)} %get-tuple-element.953) | copy-start | bytes 2162692
  1735.8 105.0 %reduce-scatter.24.cloned.1.call-start = ((), (), s32[]{:S(2)}) async-start(), calls=%async_computation.31 | async-start | bytes 4325376 | tf_op jit(solution)/shard_map/reduce_scatter | solution.py:573
  1740.9 174.1 %reduce-scatter.22.cloned.1.call-start = ((), (), s32[]{:S(2)}) async-start(), calls=%async_computation.30 | async-start | bytes 8650752 | tf_op jit(solution)/shard_map/reduce_scatter | solution.py:570
  1748.5 201.0 %reduce-scatter.20.cloned.1.call-start = ((), (), s32[]{:S(2)}) async-start(), calls=%async_computation.29 | async-start | bytes 3145728 | tf_op jit(solution)/shard_map/reduce_scatter | solution.py:561
  1754.4 241.3 %reduce-scatter.14.cloned.1.call-start = ((), (), s32[]{:S(2)}) async-start(), calls=%async_computation.26 | async-start | bytes 4718592 | tf_op jit(solution)/shard_map/reduce_scatter | solution.py:549
  1758.2 42.0 %copy-start.46 = (f32[512,32]{0,1:T(8,128)S(1)}, f32[512,32]{0,1:T(8,128)}, u32[]{:S(2)}) copy-start(f32[512,32]{0,1:T(8,128)} %copy-done.45) | copy-start | bytes 196612
  1758.3 42.1 %copy-start.48 = (f32[512,32]{0,1:T(8,128)S(1)}, f32[512,32]{0,1:T(8,128)}, u32[]{:S(2)}) copy-start(f32[512,32]{0,1:T(8,128)} %copy-done.47) | copy-start | bytes 196612
  1758.3 42.1 %copy-start.70 = (f32[512]{0:T(512)S(1)}, f32[512]{0:T(512)}, u32[]{:S(2)}) copy-start(f32[512]{0:T(512)} %get-tuple-element.969) | copy-start | bytes 6148
  1758.3 260.5 %reduce-scatter.18.cloned.1.call-start = ((), (), s32[]{:S(2)}) async-start(), calls=%async_computation.28 | async-start | bytes 1572864 | tf_op jit(solution)/shard_map/reduce_scatter | solution.py:558
  1761.6 294.8 %reduce-scatter.16.cloned.1.call-start = ((), (), s32[]{:S(2)}) async-start(), calls=%async_computation.27 | async-start | bytes 3538944 | tf_op jit(solution)/shard_map/reduce_scatter | solution.py:552
  1804.8 286.8 %reduce-scatter.26.cloned.1.call-start = ((), (), s32[]{:S(2)}) async-start(), calls=%async_computation.32 | async-start | bytes 98304 | tf_op jit(solution)/shard_map/reduce_scatter | solution.py:567
  1805.8 298.6 %reduce-scatter.10.cloned.1.call-start = ((), (), s32[]{:S(2)}) async-start(), calls=%async_computation.22 | async-start | bytes 2621440 | tf_op jit(solution)/shard_map/reduce_scatter | solution.py:332
  1811.6 596.5 %all-reduce.18.cloned.1.call-start = ((), (), s32[]{:S(2)}) async-start(), calls=%async_computation.34 | async-start | bytes 17301504 | tf_op jit(solution)/shard_map/psum | solution.py:590
  (75 other events, 284.1 us)
Sparse Core Ops, SparseCore 0:
  9.6 25.2 all-gather.10
  36.4 36.0 all-gather.12
  74.0 21.2 all-gather.14
  96.8 44.8 all-gather.18
  143.7 89.3 all-gather.16
  234.5 31.4 all-gather.20
  330.4 76.8 all-reduce.11
  1044.3 142.5 all-gather.22
  1188.5 53.4 all-gather.24
  1243.4 22.3 all-gather.26
  1452.5 51.3 all-reduce.13
  1609.8 122.2 reduce-scatter.11
  1735.9 61.5 all-reduce.15
  1800.1 40.6 reduce-scatter.23
  1843.5 71.4 reduce-scatter.21
  1917.6 31.8 reduce-scatter.19
  1952.2 43.4 reduce-scatter.13
  1998.4 20.3 reduce-scatter.17
  2021.6 34.7 reduce-scatter.15
  2059.1 10.0 reduce-scatter.25
  2072.2 31.6 reduce-scatter.9
  2107.1 300.9 all-reduce.17
where the time goes:
time: 2430 us
  waiting for transfers between devices  1620 us (67%)
  local copies, waits for them, and re-layouts  285 us (12%)
  matrix products  195 us (8%)
  other arithmetic  143 us (6%)
  blocking collectives  93.4 us (4%)
  loops' own time  54.2 us (2%)
    psum x1, waiting for transfers between devices, shards(): lax.psum(query_proj_grad.astype(jnp.bfloat16), 'context')  262 us
    all_to_all x1, waiting for transfers between devices, shards(): lax.all_to_all(results, ('dp', 'context', 'experts'), split_axis=0, conca...  166 us
    all_to_all x1, waiting for transfers between devices, shards(): lax.all_to_all(spread(sent), ('dp', 'context', 'experts'), split_axis=0,...  166 us
    all_gather x1, waiting for transfers between devices, shards(): lax.all_gather(shared_in, 'dp', axis=0, tiled=True)  143 us
    reduce_scatter x1, waiting for transfers between devices, shards(): lax.psum_scatter(outgoing_grad.astype(jnp.bfloat16), 'context', scatter_d...  115 us
    all_to_all x1, waiting for transfers between devices, shards(): lax.all_to_all(spread(jnp.repeat(own_normed, TOPK, axis=0)), ('dp', 'cont...  115 us
    reduce_scatter x1, waiting for transfers between devices, shards(): lax.psum_scatter(shared_in_grad.astype(jnp.bfloat16), 'dp', scatter_dimen...  74.2 us
    all_gather x1, waiting for transfers between devices, shards(): gathered = lax.all_gather(outgoing_keys, 'context', axis=0, tiled=True)  73.1 us
  transfers between devices with their start and end apart: 26, of which 22 were waited for; matrix products, arithmetic and copies ran while one was open for 15% of the time, Pallas kernels for 0%

commit v1 on v0

v1 whole, which is shorter than its diff:
```python
import math

import jax
import jax.numpy as jnp
from jax import lax
from jax.experimental import pallas as pl
from jax.experimental.pallas import tpu as pltpu
from jax.sharding import PartitionSpec as P


D = 2048
NOPE = 128
ROPE = 64
VDIM = 128
RANK = 512
TOPK = 6


eps_norm = 1e-06
route_scale = 2.446
rope_base = 50000.0
masked_value = -1e30


def rope_tables(positions, width):
    count = width // 2
    exponents = jnp.arange(count, dtype=jnp.float32) * (2.0 / width)
    freqs = jnp.power(jnp.float32(rope_base), -exponents)
    angles = positions.astype(jnp.float32)[:, None] * freqs[None, :]
    cosine = jnp.cos(angles)
    sine = jnp.sin(angles)
    return (jnp.concatenate([cosine, cosine], axis=1), jnp.concatenate([sine, sine], axis=1))


def rotate(values, cosine, sine):
    count = values.shape[-1] // 2
    turned = jnp.concatenate([-values[..., count:], values[..., :count]], axis=-1)
    return values * cosine + turned * sine


def rotate_back(grads, cosine, sine):
    count = grads.shape[-1] // 2
    scaled = grads * sine
    turned = jnp.concatenate([scaled[..., count:], -scaled[..., :count]], axis=-1)
    return grads * cosine + turned


def rms_back(grad_normed, values, scale, gain):
    gained = grad_normed * gain
    gain_grad = jnp.sum(grad_normed * values * scale, axis=0)
    value_grad = scale * gained - values * (scale * scale * scale) * jnp.mean(
        gained * values, axis=1, keepdims=True
    )
    return (value_grad, gain_grad)


EVERY = ("dp", "context", "experts")
NT = (((1,), (1,)), ((), ()))
TN = (((0,), (0,)), ((), ()))


def mm(left, right, dims=None):
    if dims is None:
        return jnp.dot(left, right, preferred_element_type=jnp.float32)
    return lax.dot_general(left, right, dims, preferred_element_type=jnp.float32)


def gate(*values):
    return lax.optimization_barrier(values)


def swap(values, axis, mask):
    count = lax.axis_size(axis)
    return lax.ppermute(values, axis, [(i, i ^ mask) for i in range(count)])


def masks_of(axis):
    count = lax.axis_size(axis)
    return [1 << bit for bit in range(count.bit_length() - 1)]


def cube_gather(values, axis):
    held = {0: values}
    for mask in reversed(masks_of(axis)):
        keys = sorted(held)
        rows = values.shape[0]
        got = swap(jnp.concatenate([held[key] for key in keys], axis=0), axis, mask)
        for at, key in enumerate(keys):
            held[key | mask] = got[at * rows : (at + 1) * rows]
    return jnp.concatenate([held[key] for key in sorted(held)], axis=0)


def cube_scatter(values, axis):
    count = lax.axis_size(axis)
    rows = values.shape[0] // count
    held = {key: values[key * rows : (key + 1) * rows] for key in range(count)}
    for mask in masks_of(axis):
        kept = [key for key in sorted(held) if not key & mask]
        sent = jnp.concatenate([held[key | mask] for key in kept], axis=0)
        got = swap(sent.astype(jnp.bfloat16), axis, mask).astype(jnp.float32)
        held = {
            key: held[key].astype(jnp.float32) + got[at * rows : (at + 1) * rows]
            for at, key in enumerate(kept)
        }
    return held[0]


def sum_everywhere(values):
    for axis in ("experts", "context", "dp"):
        for mask in masks_of(axis):
            values = values + swap(values, axis, mask)
    return values


def join_dp(values, other, axis):
    first = lax.axis_index("dp") == 0
    return jnp.where(
        first,
        jnp.concatenate([values, other], axis=axis),
        jnp.concatenate([other, values], axis=axis),
    )


def pick_rows(take, parts, width):
    sources, capacity, rows_dev = take.shape
    per = 4
    wide = [part.shape[1] for part in parts]

    def body(take_ref, *refs):
        out_ref = refs[-1]
        for one in range(per):
            start = 0
            for ref in refs[:-1]:
                span = min(ref.shape[1], width - start)
                out_ref[one * capacity : (one + 1) * capacity, start : start + span] = mm(
                    take_ref[one], ref[one * rows_dev : (one + 1) * rows_dev, :span]
                ).astype(jnp.bfloat16)
                start += span

    return pl.pallas_call(
        body,
        grid=(sources // per,),
        in_specs=[pl.BlockSpec((per, capacity, rows_dev), lambda s: (s, 0, 0))]
        + [pl.BlockSpec((per * rows_dev, size), lambda s: (s, 0)) for size in wide],
        out_specs=pl.BlockSpec((per * capacity, width), lambda s: (s, 0)),
        out_shape=jax.ShapeDtypeStruct((sources * capacity, width), jnp.bfloat16),
        compiler_params=pltpu.CompilerParams(vmem_limit_bytes=40 << 20),
        cost_estimate=pl.CostEstimate(
            flops=2 * sources * capacity * rows_dev * width,
            bytes_accessed=2 * sources * (rows_dev + capacity) * width,
            transcendentals=0,
        ),
        name="pick_rows",
    )(take, *parts)


def place_rows(take, values, extra, widths):
    sources, capacity, rows_dev = take.shape
    per = 4
    inputs = [values] if extra is None else [values, extra]
    shapes = list(widths)
    if extra is not None:
        shapes[-1] += extra.shape[1]

    def body(take_ref, *refs):
        ins, outs = refs[: len(inputs)], refs[len(inputs) :]
        for one in range(per):
            slots = slice(one * capacity, (one + 1) * capacity)
            rows = slice(one * rows_dev, (one + 1) * rows_dev)
            start = 0
            for ref, span in zip(outs, widths):
                ref[rows, :span] = mm(
                    take_ref[one], ins[0][slots, start : start + span], TN
                ).astype(jnp.bfloat16)
                start += span
            if extra is not None:
                outs[-1][rows, widths[-1] :] = mm(take_ref[one], ins[1][slots, :], TN).astype(
                    jnp.bfloat16
                )

    return pl.pallas_call(
        body,
        grid=(sources // per,),
        in_specs=[pl.BlockSpec((per, capacity, rows_dev), lambda s: (s, 0, 0))]
        + [pl.BlockSpec((per * capacity, one.shape[1]), lambda s: (s, 0)) for one in inputs],
        out_specs=[pl.BlockSpec((per * rows_dev, size), lambda s: (s, 0)) for size in shapes],
        out_shape=[
            jax.ShapeDtypeStruct((sources * rows_dev, size), jnp.bfloat16) for size in shapes
        ],
        compiler_params=pltpu.CompilerParams(vmem_limit_bytes=40 << 20),
        cost_estimate=pl.CostEstimate(
            flops=2 * sources * capacity * rows_dev * sum(shapes),
            bytes_accessed=2 * sources * (rows_dev + capacity) * sum(shapes),
            transcendentals=0,
        ),
        name="place_rows",
    )(take, *inputs)


def gated_parts(gate, upper, act_grad):
    sig = jax.nn.sigmoid(gate)
    act = (gate * sig * upper).astype(jnp.bfloat16)
    pre_grad = jnp.concatenate(
        [act_grad * upper * sig * (1.0 + gate * (1.0 - sig)), act_grad * gate * sig], axis=1
    ).astype(jnp.bfloat16)
    return act, pre_grad


def attend_fwd_body(scale, qn_ref, qr_ref, kv_ref, kr_ref, qp_ref, kp_ref, out_ref, lse_ref):
    scores = mm(qn_ref[...], kv_ref[:, :NOPE], NT) + mm(qr_ref[0], kr_ref[...], NT)
    scores = jnp.where(kp_ref[...] <= qp_ref[...], scores * scale, masked_value)
    top = jnp.max(scores, axis=1, keepdims=True)
    weights = jnp.exp(scores - top)
    total = jnp.sum(weights, axis=1, keepdims=True)
    out = mm(weights.astype(jnp.bfloat16), kv_ref[:, NOPE:])
    out_ref[...] = (out / total).astype(jnp.bfloat16)
    lse_ref[0] = top + jnp.log(total)


def attend_fwd(q_nope, q_rope, keyvals, rope_keys, q_pos, k_pos, scale):
    heads, rows, rope = q_rope.shape
    keys = keyvals.shape[0]
    tile = min(rows, 256)
    return pl.pallas_call(
        lambda *refs: attend_fwd_body(scale, *refs),
        grid=(heads, rows // tile),
        in_specs=[
            pl.BlockSpec((tile, NOPE), lambda h, i: (i, h)),
            pl.BlockSpec((1, tile, rope), lambda h, i: (h, i, 0)),
            pl.BlockSpec((keys, NOPE + VDIM), lambda h, i: (0, h)),
            pl.BlockSpec((keys, rope), lambda h, i: (0, 0)),
            pl.BlockSpec((tile, 1), lambda h, i: (i, 0)),
            pl.BlockSpec((1, keys), lambda h, i: (0, 0)),
        ],
        out_specs=[
            pl.BlockSpec((tile, VDIM), lambda h, i: (i, h)),
            pl.BlockSpec((1, tile, 1), lambda h, i: (h, i, 0)),
        ],
        out_shape=[
            jax.ShapeDtypeStruct((rows, heads * VDIM), jnp.bfloat16),
            jax.ShapeDtypeStruct((heads, rows, 1), jnp.float32),
        ],
        compiler_params=pltpu.CompilerParams(vmem_limit_bytes=60 << 20),
        cost_estimate=pl.CostEstimate(
            flops=2 * heads * rows * keys * (NOPE + rope + VDIM),
            bytes_accessed=4 * keys * heads * (NOPE + VDIM),
            transcendentals=heads * rows * keys,
        ),
        name="attend_fwd",
    )(q_nope, q_rope, keyvals, rope_keys, q_pos, k_pos)


def attend_bwd_body(
    scale,
    qn_ref,
    qr_ref,
    kv_ref,
    kr_ref,
    qp_ref,
    kp_ref,
    out_ref,
    grad_ref,
    lse_ref,
    dqn_ref,
    dqr_ref,
    dkv_ref,
    dkr_ref,
    dk_sum,
    dv_sum,
    dr_sum,
):
    head, tile = pl.program_id(1), pl.program_id(2)
    tiles = pl.num_programs(2)
    grad = grad_ref[...]
    q_nope, q_rope = qn_ref[...], qr_ref[0]
    keys, values = kv_ref[:, :NOPE], kv_ref[:, NOPE:]
    scores = mm(q_nope, keys, NT) + mm(q_rope, kr_ref[...], NT)
    probs = jnp.exp(scores * scale - lse_ref[0])
    probs = jnp.where(kp_ref[...] <= qp_ref[...], probs, 0.0)
    delta = jnp.sum(
        out_ref[...].astype(jnp.float32) * grad.astype(jnp.float32), axis=1, keepdims=True
    )
    score_grad = (probs * (mm(grad, values, NT) - delta)).astype(jnp.bfloat16)
    dqn_ref[0] = scale * mm(score_grad, keys)
    dqr_ref[0, 0] = scale * mm(score_grad, kr_ref[...])
    key_part = mm(score_grad, q_nope, TN)
    value_part = mm(probs.astype(jnp.bfloat16), grad, TN)
    rope_part = mm(score_grad, q_rope, TN)

    @pl.when(tile == 0)
    def _():
        dk_sum[...] = key_part
        dv_sum[...] = value_part

    @pl.when(tile > 0)
    def _():
        dk_sum[...] += key_part
        dv_sum[...] += value_part

    @pl.when((tile == 0) & (head == 0))
    def _():
        dr_sum[...] = rope_part

    @pl.when((tile > 0) | (head > 0))
    def _():
        dr_sum[...] += rope_part

    @pl.when(tile == tiles - 1)
    def _():
        dkv_ref[:, :NOPE] = (scale * dk_sum[...]).astype(jnp.bfloat16)
        dkv_ref[:, NOPE:] = dv_sum[...].astype(jnp.bfloat16)

    @pl.when((tile == tiles - 1) & (head == pl.num_programs(1) - 1))
    def _():
        dkr_ref[...] = (scale * dr_sum[...]).astype(jnp.bfloat16)


def attend_bwd(q_nope, q_rope, keyvals, rope_keys, q_pos, k_pos, attended, grad, lse, scale):
    heads, rows, rope = q_rope.shape
    keys = keyvals.shape[0]
    tile = min(rows, 256)
    chunk = min(keys, 2048)
    chunks = keys // chunk
    dqn, dqr, dkv, dkr = pl.pallas_call(
        lambda *refs: attend_bwd_body(scale, *refs),
        grid=(chunks, heads, rows // tile),
        in_specs=[
            pl.BlockSpec((tile, NOPE), lambda c, h, i: (i, h)),
            pl.BlockSpec((1, tile, rope), lambda c, h, i: (h, i, 0)),
            pl.BlockSpec((chunk, NOPE + VDIM), lambda c, h, i: (c, h)),
            pl.BlockSpec((chunk, rope), lambda c, h, i: (c, 0)),
            pl.BlockSpec((tile, 1), lambda c, h, i: (i, 0)),
            pl.BlockSpec((1, chunk), lambda c, h, i: (0, c)),
            pl.BlockSpec((tile, VDIM), lambda c, h, i: (i, h)),
            pl.BlockSpec((tile, VDIM), lambda c, h, i: (i, h)),
            pl.BlockSpec((1, tile, 1), lambda c, h, i: (h, i, 0)),
        ],
        out_specs=[
            pl.BlockSpec((1, tile, NOPE), lambda c, h, i: (c, i, h)),
            pl.BlockSpec((1, 1, tile, rope), lambda c, h, i: (c, h, i, 0)),
            pl.BlockSpec((chunk, NOPE + VDIM), lambda c, h, i: (c, h)),
            pl.BlockSpec((chunk, rope), lambda c, h, i: (c, 0)),
        ],
        out_shape=[
            jax.ShapeDtypeStruct((chunks, rows, heads * NOPE), jnp.float32),
            jax.ShapeDtypeStruct((chunks, heads, rows, rope), jnp.float32),
            jax.ShapeDtypeStruct((keys, heads * (NOPE + VDIM)), jnp.bfloat16),
            jax.ShapeDtypeStruct((keys, rope), jnp.bfloat16),
        ],
        scratch_shapes=[
            pltpu.VMEM((chunk, NOPE), jnp.float32),
            pltpu.VMEM((chunk, VDIM), jnp.float32),
            pltpu.VMEM((chunk, rope), jnp.float32),
        ],
        compiler_params=pltpu.CompilerParams(vmem_limit_bytes=60 << 20),
        cost_estimate=pl.CostEstimate(
            flops=2 * heads * rows * keys * (3 * NOPE + 3 * rope + 2 * VDIM),
            bytes_accessed=8 * keys * heads * (NOPE + VDIM),
            transcendentals=heads * rows * keys,
        ),
        name="attend_bwd",
    )(q_nope, q_rope, keyvals, rope_keys, q_pos, k_pos, attended, grad, lse)
    return jnp.sum(dqn, axis=0), jnp.sum(dqr, axis=0), dkv, dkr


def layer(
    layer_input,
    cotangent,
    routes,
    span_order,
    attn_gain,
    query_proj,
    latent_proj,
    latent_gain,
    expand_proj,
    output_proj,
    moe_gain,
    router_proj,
    shared_in,
    shared_out,
    expert_in,
    expert_out,
):
    place_dp = lax.axis_index("dp")
    place_context = lax.axis_index("context")
    place_experts = lax.axis_index("experts")
    count_dp = lax.axis_size("dp")
    count_context = lax.axis_size("context")
    count_experts = lax.axis_size("experts")
    own_in = layer_input[0]
    own_cot = cotangent[0]
    rows_dev = own_in.shape[0]
    sources = count_dp * count_context * count_experts
    heads = query_proj.shape[1] // (NOPE + ROPE)
    experts = router_proj.shape[1]
    shared_width = shared_out.shape[0]
    width = expert_out.shape[1]
    score_scale = 1.0 / math.sqrt(NOPE + ROPE)

    span_rows = count_experts * rows_dev
    total_rows = span_rows * count_context
    half = span_rows // 2
    width_dp = D // count_dp
    near = place_dp * width_dp
    far = (1 - place_dp) * width_dp

    names = jnp.arange(experts, dtype=jnp.int32)
    route_code = jnp.pad(routes[0], ((0, 0), (0, 128 - TOPK))).astype(jnp.bfloat16)
    all_routes = lax.all_gather(route_code, EVERY, axis=0, tiled=True)
    all_routes = all_routes[:, :TOPK].astype(jnp.int32)
    all_cot = lax.all_gather(own_cot, EVERY, axis=0, tiled=True)

    small = jnp.concatenate([attn_gain, latent_gain, moe_gain, router_proj.reshape(-1)])
    cuts = [attn_gain.size, latent_gain.size, moe_gain.size, router_proj.size]
    starts = [sum(cuts[:i]) for i in range(4)]
    small = join_dp(small[None], swap(small, "dp", 1)[None], 0)
    attn_gain, latent_gain, moe_gain, router_flat = (
        small[:, start : start + size].reshape(-1) for start, size in zip(starts, cuts)
    )
    router_proj = router_flat.reshape(-1, experts)
    attn_gain, latent_gain, moe_gain = (
        gain.astype(jnp.float32) for gain in (attn_gain, latent_gain, moe_gain)
    )

    inputs = own_in.astype(jnp.float32)
    scale_one = lax.rsqrt(jnp.mean(inputs * inputs, axis=1, keepdims=True) + eps_norm)
    own_normed = (inputs * scale_one * attn_gain).astype(jnp.bfloat16)
    latent_shard = latent_proj.T
    far_normed = swap(lax.dynamic_slice_in_dim(own_normed, far, width_dp, 1), "dp", 1)
    compressed = mm(
        lax.dynamic_slice_in_dim(own_normed, near, width_dp, 1), latent_shard, NT
    ) + swap(mm(far_normed, latent_shard, NT), "dp", 1)

    span_in = cube_gather(own_in, "experts")
    query_shard, far_normed = gate(query_proj, far_normed)
    query_other = swap(query_shard, "dp", 1)
    expand_shard, query_other = gate(expand_proj, query_other)
    expand_other = swap(expand_shard, "dp", 1)
    output_shard, expand_other = gate(output_proj, expand_other)
    output_other = swap(output_shard, "dp", 1)
    shared_shard, down_shard, latent_late, output_other = gate(
        shared_in.transpose(1, 2, 0).reshape(2 * shared_width, width_dp),
        shared_out,
        latent_shard,
        output_other,
    )
    shared_other = swap(shared_shard, "dp", 1)
    down_other = swap(down_shard, "dp", 1)
    latent_other = swap(latent_late, "dp", 1)
    query_proj = join_dp(query_shard, query_other, 0)
    expand_proj = join_dp(expand_shard, expand_other, 0)
    output_proj = join_dp(output_shard, output_other, 1)
    shared_in = join_dp(shared_shard, shared_other, 1)
    shared_out = join_dp(down_shard, down_other, 1)
    latent_proj = join_dp(latent_late, latent_other, 1)

    order = lax.dynamic_slice_in_dim(span_order, 2 * place_context, 2, 0)
    offsets = jnp.arange(rows_dev, dtype=jnp.int32)
    members = jnp.arange(count_experts, dtype=jnp.int32) ^ place_experts
    span_places = (members[:, None] * rows_dev + offsets[None, :]).reshape(span_rows)
    positions = (
        jnp.where(span_places < half, order[0], order[1]) * half + span_places % half
    )
    key_positions = (
        span_order[:, None] * half + jnp.arange(half, dtype=jnp.int32)[None, :]
    ).reshape(1, total_rows)
    cosine, sine = rope_tables(positions, ROPE)
    own_cosine, own_sine = cosine[:rows_dev], sine[:rows_dev]

    latent = compressed[:, :RANK]
    scale_latent = lax.rsqrt(jnp.mean(latent * latent, axis=1, keepdims=True) + eps_norm)
    latent_normed = (latent * scale_latent * latent_gain).astype(jnp.bfloat16)
    key_rope = rotate(compressed[:, RANK:], own_cosine, own_sine).astype(jnp.bfloat16)
    keys_all = lax.all_gather(
        jnp.concatenate([latent_normed, key_rope], axis=1),
        ("context", "experts"),
        axis=0,
        tiled=True,
    )
    latent_all, rope_all = keys_all[:, :RANK], keys_all[:, RANK:]

    span_float = span_in.astype(jnp.float32)
    scale_span = lax.rsqrt(jnp.mean(span_float * span_float, axis=1, keepdims=True) + eps_norm)
    normed = (span_float * scale_span * attn_gain).astype(jnp.bfloat16)
    query_raw = mm(normed, query_proj).reshape(span_rows, heads, NOPE + ROPE)
    q_nope = query_raw[:, :, :NOPE].reshape(span_rows, heads * NOPE).astype(jnp.bfloat16)
    q_rope = (
        rotate(query_raw[:, :, NOPE:], cosine[:, None, :], sine[:, None, :])
        .transpose(1, 0, 2)
        .astype(jnp.bfloat16)
    )
    keyvals = mm(latent_all, expand_proj).astype(jnp.bfloat16)
    q_pos = positions[:, None]
    attended, lse = attend_fwd(
        q_nope, q_rope, keyvals, rope_all, q_pos, key_positions, score_scale
    )
    hidden = inputs + cube_scatter(mm(attended, output_proj), "experts")
    scale_two = lax.rsqrt(jnp.mean(hidden * hidden, axis=1, keepdims=True) + eps_norm)
    hidden_normed = (hidden * scale_two * moe_gain).astype(jnp.bfloat16)

    gates = jax.nn.sigmoid(mm(hidden_normed, router_proj))
    picked = jnp.any(routes[0][:, :, None] == names[None, None, :], axis=1)
    chosen = jnp.where(picked, gates, 0.0)
    chosen_total = jnp.sum(chosen, axis=1, keepdims=True)
    route_weights = route_scale * chosen / chosen_total
    weights_high = route_weights.astype(jnp.bfloat16)
    weights_low = (route_weights - weights_high.astype(jnp.float32)).astype(jnp.bfloat16)
    code_width = -(-2 * experts // 128) * 128
    all_normed = lax.all_gather(
        jnp.concatenate(
            [
                hidden_normed,
                weights_high,
                weights_low,
                jnp.zeros((rows_dev, code_width - 2 * experts), jnp.bfloat16),
            ],
            axis=1,
        ),
        EVERY,
        axis=0,
        tiled=True,
    )

    capacity = rows_dev * TOPK * 4 // (3 * experts)
    name = place_context * count_experts + place_experts
    lower = (jnp.arange(rows_dev)[:, None] <= jnp.arange(rows_dev)[None, :]).astype(jnp.bfloat16)
    slots = jnp.arange(capacity, dtype=jnp.int32)
    hit = jnp.any(all_routes == name, axis=1).reshape(sources, rows_dev)
    ranks = mm(hit.astype(jnp.bfloat16), lower).astype(jnp.int32) - 1
    take_mask = hit[:, None, :] & (ranks[:, None, :] == slots[None, :, None])
    take = take_mask.astype(jnp.bfloat16)
    gate_up = expert_in[0].transpose(1, 2, 0).reshape(2 * width, D)
    down = expert_out[0]
    grads = pick_rows(take, [all_cot], D)
    bare_grad, all_normed = gate(mm(grads, down, NT), all_normed)

    all_codes = all_normed[:, D:].astype(jnp.float32)
    code_names = jnp.arange(code_width, dtype=jnp.int32)
    weight = jnp.sum(
        jnp.where(
            (code_names == name)[None, :] | (code_names == name + experts)[None, :], all_codes, 0.0
        ),
        axis=1,
    ).reshape(sources, rows_dev)
    slot_weight = jnp.sum(
        jnp.where(take_mask, weight[:, None, :], 0.0), axis=2
    ).reshape(sources * capacity, 1)
    rows = pick_rows(take, [all_normed], D)
    pre = mm(rows, gate_up, NT)
    act, pre_grad = gated_parts(pre[:, :width], pre[:, width:], bare_grad * slot_weight)
    weight_grad = jnp.sum(act.astype(jnp.float32) * bare_grad, axis=1, keepdims=True)
    act_weighted = (act.astype(jnp.float32) * slot_weight).astype(jnp.bfloat16)
    backs = mm(pre_grad, gate_up).astype(jnp.bfloat16)
    high = weight_grad.astype(jnp.bfloat16).astype(jnp.float32)
    back_width = -(-2 * count_dp * experts // 128) * 128
    columns = jnp.arange(back_width, dtype=jnp.int32)[None, :]
    column = place_dp * experts + name
    code = jnp.where(columns == column, high, 0.0) + jnp.where(
        columns == column + count_dp * experts, weight_grad - high, 0.0
    )
    tokens = sources * rows_dev
    piece = min(tokens, 4096)
    side = D // 2

    def scatter_every(values):
        return lax.psum_scatter(values, EVERY, scatter_dimension=0, tiled=True)

    code = code.astype(jnp.bfloat16)
    if tokens > piece:
        (back,) = place_rows(take, backs[:, :side], None, (side,))
        back, backs, code = gate(scatter_every(back), backs, code)
        (other,) = place_rows(take, backs[:, side:], code, (D - side,))
        back = jnp.concatenate([back, scatter_every(other)], axis=1)
    else:
        (back,) = place_rows(take, backs, code, (D,))
        back, all_normed, all_cot, pre_grad, rows, act_weighted, grads = gate(
            back, all_normed, all_cot, pre_grad, rows, act_weighted, grads
        )
        back = scatter_every(back)

    span_start = (place_dp * count_context + place_context) * span_rows

    def span_of(values):
        return jnp.concatenate(
            [
                lax.dynamic_slice_in_dim(
                    values, span_start + (place_experts ^ one) * rows_dev, rows_dev, 0
                )
                for one in range(count_experts)
            ],
            axis=0,
        )

    def shared_parts(normed_piece, cot_piece):
        shared_pre = mm(normed_piece, shared_in, NT)
        return gated_parts(
            shared_pre[:, :shared_width],
            shared_pre[:, shared_width:],
            mm(cot_piece, shared_out, NT),
        )

    if tokens > piece:
        all_normed, all_cot, back = gate(all_normed, all_cot, back)
        span_act, span_pre_grad = shared_parts(span_of(all_normed)[:, :D], span_of(all_cot))
        span_act, span_pre_grad, all_normed, all_cot = gate(
            span_act, span_pre_grad, all_normed, all_cot
        )
    shared_in_grad, shared_out_grad = 0.0, 0.0
    for start in range(0, tokens, piece):
        normed_piece = all_normed[start : start + piece, :D]
        cot_piece = all_cot[start : start + piece]
        shared_act, shared_pre_grad = shared_parts(normed_piece, cot_piece)
        shared_in_grad += mm(
            shared_pre_grad, lax.dynamic_slice_in_dim(normed_piece, near, width_dp, 1), TN
        )
        shared_out_grad += mm(
            shared_act, lax.dynamic_slice_in_dim(cot_piece, near, width_dp, 1), TN
        )
        if tokens > piece:
            shared_in_grad, shared_out_grad, all_normed, all_cot = gate(
                shared_in_grad, shared_out_grad, all_normed, all_cot
            )
        else:
            span_act, span_pre_grad = span_of(shared_act), span_of(shared_pre_grad)

    shared_sum = cube_scatter(
        jnp.concatenate(
            [
                mm(span_act, shared_out).astype(jnp.bfloat16),
                mm(span_pre_grad, shared_in).astype(jnp.bfloat16),
            ],
            axis=1,
        ),
        "experts",
    )
    expert_in_grad = mm(pre_grad, rows, TN)
    expert_out_grad = mm(act_weighted, grads, TN)
    back, shared_sum, shared_in_grad, shared_out_grad, expert_in_grad, expert_out_grad = gate(
        back, shared_sum, shared_in_grad, shared_out_grad, expert_in_grad, expert_out_grad
    )
    shared_in_grad = shared_in_grad.reshape(2, shared_width, width_dp).transpose(2, 0, 1)
    expert_in_grad = expert_in_grad.reshape(2, width, D).transpose(2, 0, 1)[None]
    expert_out_grad = expert_out_grad[None]
    back = back.astype(jnp.float32)

    codes = back[:, D : D + 2 * count_dp * experts].reshape(rows_dev, 2 * count_dp, experts)
    weight_grad = jnp.sum(codes, axis=1)
    chosen_grad = route_scale * weight_grad / chosen_total - route_scale * jnp.sum(
        weight_grad * chosen, axis=1, keepdims=True
    ) / (chosen_total * chosen_total)
    logit_grad = jnp.where(picked, chosen_grad * gates * (1.0 - gates), 0.0)
    normed_grad = (
        back[:, :D]
        + shared_sum[:, D:]
        + jnp.dot(
            logit_grad, router_proj.astype(jnp.float32).T, precision=lax.Precision.HIGHEST
        )
    )
    norm_part, moe_gain_grad = rms_back(normed_grad, hidden, scale_two, moe_gain)
    hidden_grad = own_cot.astype(jnp.float32) + norm_part
    outgoing, act_weighted = gate(hidden_grad.astype(jnp.bfloat16), act_weighted)
    hidden_round = cube_gather(outgoing, "experts")
    results = mm(act_weighted, down).astype(jnp.bfloat16)
    (forward_rows,) = place_rows(take, results, None, (D,))
    routed = scatter_every(forward_rows)

    def sum_heads(values):
        kept = lax.dynamic_slice_in_dim(values, near, width_dp, 0)
        sent = lax.dynamic_slice_in_dim(values, far, width_dp, 0)
        kept = (kept + swap(sent.astype(jnp.bfloat16), "dp", 1).astype(jnp.float32)).astype(
            jnp.bfloat16
        )
        return lax.psum_scatter(kept, "context", scatter_dimension=0, tiled=True)

    def full_heads(values):
        return lax.all_gather(values, "context", axis=0, tiled=True).astype(jnp.float32)

    attended_grad = mm(hidden_round, output_proj, NT).astype(jnp.bfloat16)
    output_part = sum_heads(mm(hidden_round, attended, TN))
    dq_nope, dq_rope, dkv, dkr = attend_bwd(
        q_nope,
        q_rope,
        keyvals,
        rope_all,
        q_pos,
        key_positions,
        attended,
        attended_grad,
        lse,
        score_scale,
    )
    latent_outgoing = jnp.concatenate([mm(dkv, expand_proj, NT).astype(jnp.bfloat16), dkr], axis=1)
    latent_part = lax.psum_scatter(
        latent_outgoing, ("context", "experts"), scatter_dimension=0, tiled=True
    ).astype(jnp.float32)
    dq_rope = rotate_back(dq_rope.transpose(1, 0, 2), cosine[:, None, :], sine[:, None, :])
    query_raw_grad = (
        jnp.concatenate([dq_nope.reshape(span_rows, heads, NOPE), dq_rope], axis=2)
        .reshape(span_rows, heads * (NOPE + ROPE))
        .astype(jnp.bfloat16)
    )
    head_grads = jnp.concatenate(
        [mm(normed, query_raw_grad, TN), mm(latent_all, dkv, TN).reshape(D, -1)], axis=1
    )
    head_grads = sum_heads(head_grads)
    input_part = cube_scatter(mm(query_raw_grad, query_proj, NT), "experts")

    latent_grad, latent_gain_grad = rms_back(
        latent_part[:, :RANK], latent, scale_latent, latent_gain
    )
    compressed_grad = jnp.concatenate(
        [latent_grad, rotate_back(latent_part[:, RANK:], own_cosine, own_sine)], axis=1
    ).astype(jnp.bfloat16)
    latent_proj_grad = mm(own_normed, compressed_grad, TN)
    kept = lax.dynamic_slice_in_dim(latent_proj_grad, near, width_dp, 0)
    sent = lax.dynamic_slice_in_dim(latent_proj_grad, far, width_dp, 0)
    kept = kept + swap(sent.astype(jnp.bfloat16), "dp", 1).astype(jnp.float32)
    latent_proj_grad = lax.psum_scatter(
        kept.astype(jnp.bfloat16), ("context", "experts"), scatter_dimension=0, tiled=True
    )
    latent_proj_grad = lax.all_gather(
        latent_proj_grad, ("context", "experts"), axis=0, tiled=True
    ).astype(jnp.float32)
    head_grads, output_proj_grad = full_heads(head_grads), full_heads(output_part).T
    query_wide = heads * (NOPE + ROPE)
    query_proj_grad = head_grads[:, :query_wide]
    expand_grad = head_grads[:, query_wide:].reshape(RANK // count_dp, -1)

    input_normed_grad = input_part + mm(compressed_grad, latent_proj)
    first_part, attn_gain_grad = rms_back(input_normed_grad, inputs, scale_one, attn_gain)
    input_grad = hidden_grad + first_part
    router_grad = jnp.dot(
        hidden_normed.astype(jnp.float32).T, logit_grad, precision=lax.Precision.HIGHEST
    )
    early = sum_everywhere(jnp.concatenate([moe_gain_grad, router_grad.reshape(-1)]))
    late = sum_everywhere(jnp.concatenate([attn_gain_grad, latent_gain_grad]))

    def part_dp(values, start, size):
        return lax.dynamic_slice_in_dim(values, start + place_dp * size, size, 0)

    block_output = hidden + routed.astype(jnp.float32) + shared_sum[:, :D]
    return (
        block_output[None],
        input_grad[None],
        part_dp(late, 0, cuts[0]),
        query_proj_grad,
        latent_proj_grad,
        part_dp(late, D, cuts[1]),
        expand_grad,
        output_proj_grad,
        part_dp(early, 0, cuts[2]),
        part_dp(early, D, cuts[3]).reshape(-1, experts),
        shared_in_grad,
        shared_out_grad,
        expert_in_grad,
        expert_out_grad,
    )


def solution(mesh):
    return jax.shard_map(
        layer,
        mesh=mesh,
        in_specs=(
            P("dp", ("context", "experts"), None),
            P("dp", ("context", "experts"), None),
            P("dp", ("context", "experts"), None),
            P(),
            P("dp"),
            P("dp", "experts"),
            P("dp", None),
            P("dp"),
            P("dp", "experts"),
            P("experts", "dp"),
            P("dp"),
            P("dp", None),
            P("dp", None, "experts"),
            P("experts", "dp"),
            P(("context", "experts"), None, None, "dp"),
            P(("context", "experts"), "dp", None),
        ),
        out_specs=(
            P("dp", ("context", "experts"), None),
            P("dp", ("context", "experts"), None),
            P("dp"),
            P("dp", "experts"),
            P("dp", None),
            P("dp"),
            P("dp", "experts"),
            P("experts", "dp"),
            P("dp"),
            P("dp", None),
            P("dp", None, "experts"),
            P("experts", "dp"),
            P(("context", "experts"), None, None, "dp"),
            P(("context", "experts"), "dp", None),
        ),
        check_vma=False,
    )
```

time: 2430 us -> 1360 us (0.56)
  waiting for transfers between devices: 1620 us -> 714 us
  local copies, waits for them, and re-layouts: 285 us -> 104 us
  blocking collectives: 93.4 us -> 0 us
  starting transfers between devices: 17.7 us -> 99.1 us
  Pallas kernels: 0 us -> 79.6 us
  loops' own time: 54.2 us -> 0 us
  matrix products: 195 us -> 241 us
  other arithmetic: 143 us -> 101 us
    all_to_all x4 -> x0, waiting for transfers between devices: 447 us -> none  [the longest x1 166 us: shards(): lax.all_to_all(results, ('dp', 'context', 'experts'), split_axis=0, conca...]
    psum x4 -> x0, waiting for transfers between devices: 418 us -> none  [the longest x1 262 us: shards(): lax.psum(query_proj_grad.astype(jnp.bfloat16), 'context')]
    ppermute x0 -> x32, waiting for transfers between devices: none -> 255 us  [swap(): return lax.ppermute(values, axis, [(i, i ^ mask) for i in range(count)])]
    all_gather x9 -> x7, waiting for transfers between devices: 391 us -> 200 us  [the longest x1 100 us: layer(): lax.all_gather(jnp.concatenate([hidden_normed, weights_high, weights_low,...]
    reduce_scatter x9 -> x6, waiting for transfers between devices: 360 us -> 258 us  [the longest x2 170 us: scatter_every(): return lax.psum_scatter(values, EVERY, scatter_dimension=0, tiled=True)]
    ppermute x0 -> x32, starting transfers between devices: none -> 97.5 us  [swap(): return lax.ppermute(values, axis, [(i, i ^ mask) for i in range(count)])]
    pallas_call x0 -> x6, Pallas kernels: none -> 79.6 us  [the longest x1 27.8 us: attend_bwd(): pl.pallas_call(lambda *refs: attend_bwd_body(scale, *refs), grid=(chunks,...]
    gather x2 -> x0, local copies, waits for them, and re-layouts: 60.8 us -> none  [collect(): flat = arrived.reshape(halves, experts * capacity, D)[:, places]]
  transfers between devices with their start and end apart: 26 -> 45, of which waited for: 22 -> 27; matrix products, arithmetic and copies ran while one was open for 15% -> 25% of each run, Pallas kernels for 0% -> 2%
where the time goes in v1:
time: 1360 us; the launch traced here: 1350 us
  waiting for transfers between devices  714 us (52%)
  matrix products  241 us (18%)
  local copies, waits for them, and re-layouts  104 us (8%)
  other arithmetic  101 us (7%)
  starting transfers between devices  99.1 us (7%)
  Pallas kernels  79.6 us (6%)
  between operations  15.5 us (1%)
    ppermute x32, waiting for transfers between devices, swap(): return lax.ppermute(values, axis, [(i, i ^ mask) for i in range(count)])  255 us
    dot_general x17, matrix products, mm(): lax.dot_general(left, right, dims, preferred_element_type=jnp.float32)  178 us
    reduce_scatter x2, waiting for transfers between devices, scatter_every(): return lax.psum_scatter(values, EVERY, scatter_dimension=0, tiled=True)  170 us
    all_gather x1, waiting for transfers between devices, layer(): lax.all_gather(jnp.concatenate([hidden_normed, weights_high, weights_low,...  100 us
    ppermute x32, starting transfers between devices, swap(): return lax.ppermute(values, axis, [(i, i ^ mask) for i in range(count)])  97.5 us
    all_gather x1, waiting for transfers between devices, layer(): all_cot = lax.all_gather(own_cot, EVERY, axis=0, tiled=True)  84.6 us
    dot_general x10, matrix products, mm(): return jnp.dot(left, right, preferred_element_type=jnp.float32)  57.3 us
    reduce_scatter x2, waiting for transfers between devices, sum_heads(): return lax.psum_scatter(kept, 'context', scatter_dimension=0, tiled=True)  45.5 us
  transfers between devices with their start and end apart: 45, of which 27 were waited for; matrix products, arithmetic and copies ran while one was open for 25% of the time, Pallas kernels for 2%

profile of v1, /device:TPU:0, one launch (start us, length us, event | category | flops | bytes accessed | tf_op | source)
XLA Modules:
  0.0 1354.3 jit_solution(10253890729950602857)
XLA Ops:
  23.2 7.0 collective-permute-done.3
  34.5 6.1 collective-permute-done.5
  46.4 11.4 collective-permute-done
  66.7 13.7 %collective-permute-done.4 = bf16[1024,768]{1,0:T(8,128)(2,1)} collective-permute-done((bf16[1024,768]{1,0:T(8,128)(2,1)}, bf16[1024,768]{1,0:T(8,128)(2,1)}, u32[]{:S(2)}, u32[]{:S(2)}) %collective-permute-start.4) | collective-permute-done | bytes 1572896 | tf_op jit(solution)/shard_map/ppermute | solution.py:74
  84.2 7.5 collective-permute-done.6
  117.4 6.5 convolution_convert_fusion.2.refs_2_
  123.9 14.6 %attend_fwd.1 = (bf16[512,512]{1,0:T(8,128)(2,1)}, f32[4,512,1]{2,1,0:T(8,128)}) custom-call(bf16[512,512]{1,0:T(8,128)(2,1)} %copy.139.refs_0_, bf16[4,512,64]{2,1,0:T(8,128)(2,1)} %fusion.77.refs_1_, bf16[2048,1024]{1,0:T(8,128)(2,1)} %convolution_convert_fusion.2.refs_2_, bf16[2048,64]{1,0:T(8,128)(2,1)} %slice.262.refs_3_, s32[512,1]{1,0:T(8,128)} %fusion.86.refs_4_, ...), custom_call_target="tpu_custom_call" | custom-call | flops 2684354560 | bytes 8388608 | tf_op jit(solution)/shard_map/attend_fwd/pallas_call | solution.py:224
  150.9 14.6 %collective-permute-done.9 = bf16[128,2048]{1,0:T(8,128)(2,1)} collective-permute-done((bf16[128,2048]{1,0:T(8,128)(2,1)}, bf16[128,2048]{1,0:T(8,128)(2,1)}, u32[]{:S(2)}, u32[]{:S(2)}) %collective-permute-start.9) | collective-permute-done | bytes 524320 | tf_op jit(solution)/shard_map/ppermute | solution.py:74
  172.5 84.6 %all-gather.21.cloned.1.call-done = bf16[1,4096,2048]{2,1,0:T(8,128)(2,1)} async-done(((bf16[1,128,2048]{2,1,0:T(8,128)(2,1)}), bf16[1,4096,2048]{2,1,0:T(8,128)(2,1)}) %all-gather.21.cloned.1.call-update) | async-done | bytes 16777232 | tf_op jit(solution)/shard_map/all_gather | solution.py:411
  257.1 9.2 pick_rows.2
  269.7 7.9 fusion.15
  277.6 100.1 %all-gather.13.cloned.1.call-done.refs_0_ = bf16[4096,2176]{1,0:T(8,128)(2,1)} async-done(((bf16[128,2176]{1,0:T(8,128)(2,1)}), bf16[4096,2176]{1,0:T(8,128)(2,1)}) %all-gather.13.cloned.1.call-update) | async-done | bytes 17825808 | tf_op jit(solution)/shard_map/all_gather | solution.py:509
  377.7 9.4 pick_rows.3
  392.6 16.6 %fusion.142 = f32[2048,1408]{0,1:T(8,128)S(1)} fusion(bf16[2048,2048]{1,0:T(8,128)(2,1)} %copy-done.2, bf16[1408,2048]{1,0:T(8,128)(2,1)} %bitcast.158), kind=kOutput, calls=%fused_computation.305 | convolution fusion | flops 11811160064 | bytes 25690112 | tf_op jit(solution)/shard_map/dot_general | solution.py:65
  409.3 8.4 fusion.5
  417.7 6.3 pad_maximum_fusion.2
  424.0 17.2 %convolution_convert_fusion.1.refs_0_ = bf16[2048,2048]{1,0:T(8,128)(2,1)S(1)} fusion(bf16[1408,2048]{1,0:T(8,128)(2,1)} %bitcast.159, bf16[2048,704]{0,1:T(8,128)(2,1)} %get-tuple-element.165, bf16[2048,704]{0,1:T(8,128)(2,1)} %get-tuple-element.166), kind=kOutput, calls=%fused_computation.22 | convolution fusion | flops 11826888704 | bytes 19922944 | tf_op jit(solution)/shard_map/dot_general | solution.py:64
  443.0 9.4 place_rows.2
  454.6 63.6 %collective-permute-done.10 = bf16[1408,1024]{1,0:T(8,128)(2,1)} collective-permute-done((bf16[1408,1024]{1,0:T(8,128)(2,1)}, bf16[1408,1024]{1,0:T(8,128)(2,1)}, u32[]{:S(2)}, u32[]{:S(2)}) %collective-permute-start.10) | collective-permute-done | bytes 2883616 | tf_op jit(solution)/shard_map/ppermute | solution.py:74
  518.2 34.5 %fusion.64 = f32[4096,1408]{0,1:T(8,128)} fusion(bf16[1408,1024]{1,0:T(8,128)(2,1)} %collective-permute-done.10, bf16[1408,1024]{1,0:T(8,128)(2,1)} %bitcast.161, pred[]{:T(512)S(6)} %eq.85, bf16[4096,2176]{1,0:T(8,128)(2,1)} %all-gather.13.cloned.1.call-done.refs_0_), kind=kOutput, calls=%fused_computation.155 | convolution fusion | flops 23648272384 | bytes 45613056 | tf_op jit(solution)/shard_map/dot_general | solution.py:65
  552.7 14.3 %slice.216 = bf16[4096,2048]{1,0:T(8,128)(2,1)} slice(bf16[4096,2176]{1,0:T(8,128)(2,1)} %all-gather.13.cloned.1.call-done.refs_0_), slice={[0:4096], [0:2048]} | slice | bytes 33554432 | tf_op jit(solution)/shard_map/slice | solution.py:610
  567.0 29.6 %multiply_convert_fusion = (bf16[4096,704]{0,1:T(8,128)(2,1)}, bf16[4096,704]{0,1:T(8,128)(2,1)}, bf16[4096,704]{0,1:T(8,128)(2,1)}) fusion(f32[4096,1408]{0,1:T(8,128)} %fusion.64, bf16[4096,2048]{1,0:T(8,128)(2,1)} %bitcast.129, bf16[704,1024]{1,0:T(8,128)(2,1)} %collective-permute-done.11, bf16[704,1024]{1,0:T(8,128)(2,1)} %param.29, pred[]{:T(512)S(6)} %eq.85), kind=kOutput, calls=%fused_computation.10 | convolution fusion | flops 11870273536 | bytes 60030976 | tf_op jit(solution)/shard_map/dot_general | solution.py:65
  603.8 7.3 convolution_convert_fusion.5
  613.1 19.2 %fusion = f32[1408,1024]{1,0:T(8,128)} fusion(bf16[4096,704]{0,1:T(8,128)(2,1)} %get-tuple-element.160, bf16[4096,704]{0,1:T(8,128)(2,1)} %get-tuple-element.161, bf16[4096,2048]{1,0:T(8,128)(2,1)} %slice.216, s32[]{:T(128)S(6)} %select_n.166), kind=kOutput, calls=%fused_computation.9 | convolution fusion | flops 11834228736 | bytes 25690116 | tf_op jit(solution)/shard_map/dot_general | solution.py:65
  632.3 19.2 %fusion.143 = f32[1408,2048]{1,0:T(8,128)} fusion(bf16[2048,1408]{0,1:T(8,128)(2,1)} %pad_maximum_fusion.2, bf16[2048,2048]{1,0:T(8,128)(2,1)} %copy-done.2), kind=kOutput, calls=%fused_computation.306 | convolution fusion | flops 11811160064 | bytes 25690112 | tf_op jit(solution)/shard_map/dot_general | solution.py:65
  651.5 10.3 fusion.144
  664.8 72.1 %collective-permute-start.13 = (bf16[128,4096]{1,0:T(8,128)(2,1)S(1)}, bf16[128,4096]{1,0:T(8,128)(2,1)S(1)}, u32[]{:S(2)}, u32[]{:S(2)}) collective-permute-start(bf16[128,4096]{1,0:T(8,128)(2,1)S(1)} %fusion.24), channel_id=1, source_target_pairs={{0,2},{1,3},{2,0},{3,1},{4,6},{5,7},{6,4},{7,5},{8,10},{9,11},{10,... | collective-permute-start | bytes 3145736 | tf_op jit(solution)/shard_map/ppermute | solution.py:74
  736.9 9.8 fusion.1
  746.7 14.0 %collective-permute-done.13 = bf16[128,4096]{1,0:T(8,128)(2,1)S(1)} collective-permute-done((bf16[128,4096]{1,0:T(8,128)(2,1)S(1)}, bf16[128,4096]{1,0:T(8,128)(2,1)S(1)}, u32[]{:S(2)}, u32[]{:S(2)}) %collective-permute-start.13) | collective-permute-done | bytes 1048608 | tf_op jit(solution)/shard_map/ppermute | solution.py:74
  777.9 12.0 collective-permute-done.14
  797.5 27.8 %attend_bwd.1 = (f32[1,512,512]{2,1,0:T(8,128)}, f32[1,4,512,64]{3,2,1,0:T(8,128)}, bf16[2048,1024]{1,0:T(8,128)(2,1)}, bf16[2048,64]{1,0:T(8,128)(2,1)}) custom-call(bf16[512,512]{1,0:T(8,128)(2,1)} %copy.139.refs_0_, bf16[4,512,64]{2,1,0:T(8,128)(2,1)} %fusion.77.refs_1_, bf16[2048,1024]{1,0:T(8,128)(2,1)} %convolution_convert_fusion.2.refs_2_, ...), custom_call_target="tpu_custom_call" | custom-call | flops 6979321856 | bytes 16777216 | tf_op jit(solution)/shard_map/attend_bwd/pallas_call | solution.py:324
  825.3 4.9 convolution_convert_fusion.3
  858.4 5.6 collective-permute-done.26
  867.3 27.8 %reduce-scatter.13.cloned.1.call-done = bf16[128,576]{1,0:T(8,128)(2,1)} async-done(((bf16[2048,576]{1,0:T(8,128)(2,1)}), bf16[128,576]{1,0:T(8,128)(2,1)}) %reduce-scatter.13.cloned.1.call-update) | async-done | bytes 147472 | tf_op jit(solution)/shard_map/reduce_scatter | solution.py:693
  912.1 20.6 %collective-permute-done.25 = bf16[1024,576]{0,1:T(8,128)(2,1)S(1)} collective-permute-done((bf16[1024,576]{0,1:T(8,128)(2,1)S(1)}, bf16[1024,576]{0,1:T(8,128)(2,1)S(1)}, u32[]{:S(2)}, u32[]{:S(2)}) %collective-permute-start.25) | collective-permute-done | bytes 1179680 | tf_op jit(solution)/shard_map/ppermute | solution.py:74
  936.7 38.1 %collective-permute-done.24 = bf16[1024,1024]{0,1:T(8,128)(2,1)} collective-permute-done((bf16[1024,1024]{0,1:T(8,128)(2,1)}, bf16[1024,1024]{0,1:T(8,128)(2,1)}, u32[]{:S(2)}, u32[]{:S(2)}) %collective-permute-start.24) | collective-permute-done | bytes 2097184 | tf_op jit(solution)/shard_map/ppermute | solution.py:74
  974.9 5.0 fusion.13
  980.5 13.9 %reduce-scatter.19.cloned.1.call-done = bf16[64,576]{1,0:T(8,128)(2,1)} async-done(((bf16[1024,576]{1,0:T(8,128)(2,1)}), bf16[64,576]{1,0:T(8,128)(2,1)}) %reduce-scatter.19.cloned.1.call-update) | async-done | bytes 73744 | tf_op jit(solution)/shard_map/reduce_scatter | solution.py:718
  994.5 45.5 %reduce-scatter.15.cloned.1.call-done = bf16[256,1024]{0,1:T(8,128)(2,1)} async-done(((bf16[1024,1024]{0,1:T(8,128)(2,1)}), bf16[256,1024]{0,1:T(8,128)(2,1)}) %reduce-scatter.15.cloned.1.call-update) | async-done | bytes 524304 | tf_op jit(solution)/shard_map/reduce_scatter | solution.py:673
  1040.2 8.8 convolution_convert_fusion.refs_0_
  1049.0 9.1 place_rows.3
  1058.2 7.3 fusion.140
  1078.1 15.2 %collective-permute-done.28 = f32[34816]{0:T(1024)S(1)} collective-permute-done((f32[34816]{0:T(1024)S(1)}, f32[34816]{0:T(1024)S(1)}, u32[]{:S(2)}, u32[]{:S(2)}) %collective-permute-start.28) | collective-permute-done | bytes 139296 | tf_op jit(solution)/shard_map/ppermute | solution.py:74
  1094.0 6.2 collective-permute-done.29
  1101.1 5.4 fusion.49
  1123.1 7.4 collective-permute-done.22
  1144.7 15.3 %all-gather.15.cloned.1.call-done = bf16[1024,1024]{0,1:T(8,128)(2,1)} async-done(((bf16[256,1024]{0,1:T(8,128)(2,1)}), bf16[1024,1024]{0,1:T(8,128)(2,1)}) %all-gather.15.cloned.1.call-update) | async-done | bytes 2097168 | tf_op jit(solution)/shard_map/all_gather | solution.py:676
  1174.2 170.5 %reduce-scatter.11.cloned.1.call-done = bf16[128,2048]{1,0:T(8,128)(2,1)} async-done(((bf16[4096,2048]{1,0:T(8,128)(2,1)}), bf16[128,2048]{1,0:T(8,128)(2,1)}) %reduce-scatter.11.cloned.1.call-update) | async-done | bytes 524304 | tf_op jit(solution)/shard_map/reduce_scatter | solution.py:566
  (417 shorter events, 248.0 us)
Async XLA Ops:
  7.2 262.5 %copy-start = (bf16[1,704,2048]{2,1,0:T(8,128)(2,1)S(1)}, bf16[1,704,2048]{2,1,0:T(8,128)(2,1)}, u32[]{:S(2)}) copy-start(bf16[1,704,2048]{2,1,0:T(8,128)(2,1)} %param.31) | copy-start | bytes 8650756
  7.2 108.3 %all-gather.9.cloned.1.call-start = ((), (), s32[]{:S(2)}) async-start(), calls=%async_computation.6 | async-start | bytes 2785280 | tf_op jit(solution)/shard_map/all_gather | solution.py:474
  11.3 7.6 collective-permute-start.2
  22.2 8.1 collective-permute-start.3
  32.2 8.4 collective-permute-start.5
  42.3 129.0 %all-gather.11.cloned.1.call-start = ((), (), s32[]{:S(2)}) async-start(), calls=%async_computation.7 | async-start | bytes 1081344 | tf_op jit(solution)/shard_map/all_gather | solution.py:409
  43.0 214.1 %all-gather.21.cloned.1.call-start = ((), (), s32[]{:S(2)}) async-start(), calls=%async_computation.17 | async-start | bytes 17301504 | tf_op jit(solution)/shard_map/all_gather | solution.py:411
  43.8 334.0 %all-gather.13.cloned.1.call-start = ((), (), s32[]{:S(2)}) async-start(), calls=%async_computation.8 | async-start | bytes 18382848 | tf_op jit(solution)/shard_map/all_gather | solution.py:509
  44.3 13.5 collective-permute-start
  45.9 34.6 %collective-permute-start.4 = (bf16[1024,768]{1,0:T(8,128)(2,1)}, bf16[1024,768]{1,0:T(8,128)(2,1)}, u32[]{:S(2)}, u32[]{:S(2)}) collective-permute-start(bf16[1024,768]{1,0:T(8,128)(2,1)} %param.21), channel_id=1, source_target_pairs={{0,16},{16,0},{1,17},{17,1},{2,18},{18,2},{3,19},{19,3},{4,20},{20... | collective-permute-start | bytes 4718600 | tf_op jit(solution)/shard_map/ppermute | solution.py:74
  59.7 21.3 %collective-permute-start.1 = (bf16[256,2048]{1,0:T(8,128)(2,1)}, bf16[256,2048]{1,0:T(8,128)(2,1)}, u32[]{:S(2)}, u32[]{:S(2)}) collective-permute-start(bf16[256,2048]{1,0:T(8,128)(2,1)} %pad_maximum_fusion.8), channel_id=1, source_target_pairs={{0,1},{1,0},{2,3},{3,2},{4,5},{5,4},{6,7},{7,6},{8,9},{9,8},{10,11... | collective-permute-start | bytes 3145736 | tf_op jit(solution)/shard_map/ppermute | solution.py:74
  80.4 11.3 collective-permute-start.6
  92.5 23.0 %collective-permute-start.7 = (bf16[512,1024]{1,0:T(8,128)(2,1)}, bf16[512,1024]{1,0:T(8,128)(2,1)}, u32[]{:S(2)}, u32[]{:S(2)}) collective-permute-start(bf16[512,1024]{1,0:T(8,128)(2,1)} %param.25), channel_id=1, source_target_pairs={{0,16},{16,0},{1,17},{17,1},{2,18},{18,2},{3,19},{19,3},{4,20},{20... | collective-permute-start | bytes 3145736 | tf_op jit(solution)/shard_map/ppermute | solution.py:74
  142.3 2.7 collective-permute-start.8
  147.6 18.0 %collective-permute-start.9 = (bf16[128,2048]{1,0:T(8,128)(2,1)}, bf16[128,2048]{1,0:T(8,128)(2,1)}, u32[]{:S(2)}, u32[]{:S(2)}) collective-permute-start(bf16[128,2048]{1,0:T(8,128)(2,1)} %fusion.56), channel_id=1, source_target_pairs={{0,2},{1,3},{2,0},{3,1},{4,6},{5,7},{6,4},{7,5},{8,10},{9,11},{10,... | collective-permute-start | bytes 1572872 | tf_op jit(solution)/shard_map/ppermute | solution.py:74
  170.9 591.4 %reduce-scatter.9.cloned.1.call-start = ((), (), s32[]{:S(2)}) async-start(), calls=%async_computation.9 | async-start | bytes 18382848 | tf_op jit(solution)/shard_map/reduce_scatter | solution.py:566
  452.4 442.7 %reduce-scatter.13.cloned.1.call-start = ((), (), s32[]{:S(2)}) async-start(), calls=%async_computation.11 | async-start | bytes 2785280 | tf_op jit(solution)/shard_map/reduce_scatter | solution.py:693
  452.5 65.7 %collective-permute-start.10 = (bf16[1408,1024]{1,0:T(8,128)(2,1)}, bf16[1408,1024]{1,0:T(8,128)(2,1)}, u32[]{:S(2)}, u32[]{:S(2)}) collective-permute-start(bf16[1408,1024]{1,0:T(8,128)(2,1)} %bitcast.160), channel_id=1, source_target_pairs={{0,16},{16,0},{1,17},{17,1},{2,18},{18,2},{3,19},{19,3},{4,20},{20... | collective-permute-start | bytes 8650760 | tf_op jit(solution)/shard_map/ppermute | solution.py:74
  454.0 113.0 %collective-permute-start.11 = (bf16[704,1024]{1,0:T(8,128)(2,1)}, bf16[704,1024]{1,0:T(8,128)(2,1)}, u32[]{:S(2)}, u32[]{:S(2)}) collective-permute-start(bf16[704,1024]{1,0:T(8,128)(2,1)} %param.29), channel_id=1, source_target_pairs={{0,16},{16,0},{1,17},{17,1},{2,18},{18,2},{3,19},{19,3},{4,20},{20... | collective-permute-start | bytes 4325384 | tf_op jit(solution)/shard_map/ppermute | solution.py:74
  613.1 48.6 %collective-permute-start.12 = (bf16[256,4096]{1,0:T(8,128)(2,1)}, bf16[256,4096]{1,0:T(8,128)(2,1)}, u32[]{:S(2)}, u32[]{:S(2)}) collective-permute-start(bf16[256,4096]{1,0:T(8,128)(2,1)} %pad_maximum_fusion.5), channel_id=1, source_target_pairs={{0,1},{1,0},{2,3},{3,2},{4,5},{5,4},{6,7},{7,6},{8,9},{9,8},{10,11... | collective-permute-start | bytes 6291464 | tf_op jit(solution)/shard_map/ppermute | solution.py:74
  632.3 104.6 %slice-start.2 = ((s8[16777216]{0:T(1024)(128)(4,1)}), s8[4194304]{0:T(1024)(128)(4,1)S(1)}, s32[]{:S(2)}) async-start(s8[16777216]{0:T(1024)(128)(4,1)} %bitcast.130), calls=%async_computation.21 | async-start | bytes 8388608
  632.3 104.6 %slice-start.3 = ((s8[16777216]{0:T(1024)(128)(4,1)}), s8[4194304]{0:T(1024)(128)(4,1)S(1)}, s32[]{:S(2)}) async-start(s8[16777216]{0:T(1024)(128)(4,1)} %bitcast.130), calls=%async_computation.22 | async-start | bytes 8388608
  664.8 95.9 %collective-permute-start.13 = (bf16[128,4096]{1,0:T(8,128)(2,1)S(1)}, bf16[128,4096]{1,0:T(8,128)(2,1)S(1)}, u32[]{:S(2)}, u32[]{:S(2)}) collective-permute-start(bf16[128,4096]{1,0:T(8,128)(2,1)S(1)} %fusion.24), channel_id=1, source_target_pairs={{0,2},{1,3},{2,0},{3,1},{4,6},{5,7},{6,4},{7,5},{8,10},{9,11},{10,... | collective-permute-start | bytes 3145736 | tf_op jit(solution)/shard_map/ppermute | solution.py:74
  776.1 13.7 %collective-permute-start.14 = (bf16[128,2048]{1,0:T(8,128)(2,1)S(1)}, bf16[128,2048]{1,0:T(8,128)(2,1)S(1)}, u32[]{:S(2)}, u32[]{:S(2)}) collective-permute-start(bf16[128,2048]{1,0:T(8,128)(2,1)S(1)} %get-tuple-element.67), channel_id=1, source_target_pairs={{0,2},{1,3},{2,0},{3,1},{4,6},{5,7},{6,4},{7,5},{8,10},{9,11},{10,... | collective-permute-start | bytes 1572872 | tf_op jit(solution)/shard_map/ppermute | solution.py:74
  790.0 2.7 collective-permute-start.15
  832.0 147.9 %reduce-scatter.17.cloned.1.call-start = ((), (), s32[]{:S(2)}) async-start(), calls=%async_computation.15 | async-start | bytes 1310720 | tf_op jit(solution)/shard_map/reduce_scatter | solution.py:673
  838.5 25.5 %collective-permute-start.26 = (bf16[1024,512]{1,0:T(8,128)(2,1)}, bf16[1024,512]{1,0:T(8,128)(2,1)}, u32[]{:S(2)}, u32[]{:S(2)}) collective-permute-start(bf16[1024,512]{1,0:T(8,128)(2,1)} %dynamic-slice_convert_fusion.1), channel_id=1, source_target_pairs={{0,16},{16,0},{1,17},{17,1},{2,18},{18,2},{3,19},{19,3},{4,20},{20... | collective-permute-start | bytes 3145736 | tf_op jit(solution)/shard_map/ppermute | solution.py:74
  867.3 127.1 %reduce-scatter.19.cloned.1.call-start = ((), (), s32[]{:S(2)}) async-start(), calls=%async_computation.18 | async-start | bytes 1392640 | tf_op jit(solution)/shard_map/reduce_scatter | solution.py:718
  903.9 28.9 %collective-permute-start.25 = (bf16[1024,576]{0,1:T(8,128)(2,1)S(1)}, bf16[1024,576]{0,1:T(8,128)(2,1)S(1)}, u32[]{:S(2)}, u32[]{:S(2)}) collective-permute-start(bf16[1024,576]{0,1:T(8,128)(2,1)S(1)} %dynamic-slice_convert_fusion), channel_id=1, source_target_pairs={{0,16},{16,0},{1,17},{17,1},{2,18},{18,2},{3,19},{19,3},{4,20},{20... | collective-permute-start | bytes 3538952 | tf_op jit(solution)/shard_map/ppermute | solution.py:74
  911.5 63.3 %collective-permute-start.24 = (bf16[1024,1024]{0,1:T(8,128)(2,1)}, bf16[1024,1024]{0,1:T(8,128)(2,1)}, u32[]{:S(2)}, u32[]{:S(2)}) collective-permute-start(bf16[1024,1024]{0,1:T(8,128)(2,1)} %fusion.10), channel_id=1, source_target_pairs={{0,16},{16,0},{1,17},{17,1},{2,18},{18,2},{3,19},{19,3},{4,20},{20... | collective-permute-start | bytes 6291464 | tf_op jit(solution)/shard_map/ppermute | solution.py:74
  936.7 103.2 %reduce-scatter.15.cloned.1.call-start = ((), (), s32[]{:S(2)}) async-start(), calls=%async_computation.12 | async-start | bytes 2621440 | tf_op jit(solution)/shard_map/reduce_scatter | solution.py:673
  979.9 156.4 %all-gather.19.cloned.1.call-start = ((), (), s32[]{:S(2)}) async-start(), calls=%async_computation.16 | async-start | bytes 1310720 | tf_op jit(solution)/shard_map/all_gather | solution.py:676
  980.5 161.5 %all-gather.17.cloned.1.call-start = ((), (), s32[]{:S(2)}) async-start(), calls=%async_computation.14 | async-start | bytes 1392640 | tf_op jit(solution)/shard_map/all_gather | solution.py:721
  994.4 165.6 %all-gather.15.cloned.1.call-start = ((), (), s32[]{:S(2)}) async-start(), calls=%async_computation.13 | async-start | bytes 2621440 | tf_op jit(solution)/shard_map/all_gather | solution.py:676
  1040.0 304.7 %reduce-scatter.11.cloned.1.call-start = ((), (), s32[]{:S(2)}) async-start(), calls=%async_computation.10 | async-start | bytes 17301504 | tf_op jit(solution)/shard_map/reduce_scatter | solution.py:566
  1066.6 5.8 collective-permute-start.16
  1066.6 34.5 %collective-permute-start.18 = (bf16[576,1024]{1,0:T(8,128)(2,1)}, bf16[576,1024]{1,0:T(8,128)(2,1)}, u32[]{:S(2)}, u32[]{:S(2)}) collective-permute-start(bf16[576,1024]{1,0:T(8,128)(2,1)} %bitcast.10), channel_id=1, source_target_pairs={{0,16},{16,0},{1,17},{17,1},{2,18},{18,2},{3,19},{19,3},{4,20},{20... | collective-permute-start | bytes 3538952 | tf_op jit(solution)/shard_map/ppermute | solution.py:74
  1072.1 4.7 collective-permute-start.27
  1075.2 25.9 %collective-permute-start.17 = (bf16[128,2048]{1,0:T(8,128)(2,1)S(1)}, bf16[128,2048]{1,0:T(8,128)(2,1)S(1)}, u32[]{:S(2)}, u32[]{:S(2)}) collective-permute-start(bf16[128,2048]{1,0:T(8,128)(2,1)S(1)} %fusion.53), channel_id=1, source_target_pairs={{0,2},{1,3},{2,0},{3,1},{4,6},{5,7},{6,4},{7,5},{8,10},{9,11},{10,... | collective-permute-start | bytes 1572872 | tf_op jit(solution)/shard_map/ppermute | solution.py:74
  1077.5 15.8 %collective-permute-start.28 = (f32[34816]{0:T(1024)S(1)}, f32[34816]{0:T(1024)S(1)}, u32[]{:S(2)}, u32[]{:S(2)}) collective-permute-start(f32[34816]{0:T(1024)S(1)} %fusion.128), channel_id=1, source_target_pairs={{0,2},{1,3},{2,0},{3,1},{4,6},{5,7},{6,4},{7,5},{8,10},{9,11},{10,... | collective-permute-start | bytes 417800 | tf_op jit(solution)/shard_map/ppermute | solution.py:74
  1093.3 6.9 collective-permute-start.29
  1100.2 10.1 collective-permute-start.30
  1106.5 4.6 collective-permute-start.19
  1110.4 5.2 collective-permute-start.31
  1111.1 3.8 collective-permute-start.20
  1115.5 4.5 collective-permute-start.21
  1120.7 9.8 collective-permute-start.22
  1130.6 4.4 collective-permute-start.23
  (80 other events, 1021.2 us)
Sparse Core Ops, SparseCore 0:
  42.4 43.9 all-gather.8
  89.8 47.4 all-gather.10
  140.2 116.8 all-gather.20
  260.4 117.2 all-gather.12
  452.5 192.6 reduce-scatter.8
  832.1 62.9 reduce-scatter.12
  898.0 26.2 reduce-scatter.16
  936.8 57.5 reduce-scatter.18
  997.3 42.6 reduce-scatter.14
  1041.3 27.1 all-gather.18
  1070.8 40.8 all-gather.16
  1113.2 46.8 all-gather.14
  1162.3 182.3 reduce-scatter.10

commit v2 on v1

--- a/solution.py
+++ b/solution.py
@@ -103,6 +103,49 @@
             for at, key in enumerate(kept)
         }
     return held[0]
+
+
+def bits_of(axes):
+    return [(axis, mask) for axis in axes for mask in reversed(masks_of(axis))]
+
+
+def bit_here(axis, mask):
+    return (lax.axis_index(axis) // mask) % 2
+
+
+def ordered_gather(values, axes):
+    bits = bits_of(axes)
+    shape = values.shape
+    for at, (axis, mask) in enumerate(bits):
+        got = swap(values, axis, mask)
+        values = jnp.where(
+            bit_here(axis, mask) == 0,
+            jnp.stack([values, got], axis=at),
+            jnp.stack([got, values], axis=at),
+        )
+    return values.reshape(-1, *shape[1:])
+
+
+def scatter_stage(values, bits, stage, dtype):
+    at = bits.index(stage)
+    mine = bit_here(*stage)
+    kept = lax.dynamic_index_in_dim(values, mine, at, keepdims=False)
+    sent = lax.dynamic_index_in_dim(values, 1 - mine, at, keepdims=False)
+    got = swap(sent.astype(jnp.bfloat16), *stage)
+    total = kept.astype(jnp.float32) + got.astype(jnp.float32)
+    return total.astype(dtype), bits[:at] + bits[at + 1 :]
+
+
+def split_bits(values, bits):
+    return values.reshape([2] * len(bits) + [-1, values.shape[-1]])
+
+
+def ordered_scatter(values, axes, stages, dtype=jnp.float32):
+    bits = bits_of(axes)
+    values = split_bits(values, bits)
+    for stage in stages:
+        values, bits = scatter_stage(values, bits, stage, dtype)
+    return values
 
 
 def sum_everywhere(values):
@@ -406,9 +449,14 @@
 
     names = jnp.arange(experts, dtype=jnp.int32)
     route_code = jnp.pad(routes[0], ((0, 0), (0, 128 - TOPK))).astype(jnp.bfloat16)
-    all_routes = lax.all_gather(route_code, EVERY, axis=0, tiled=True)
+    all_routes = ordered_gather(route_code, EVERY)
     all_routes = all_routes[:, :TOPK].astype(jnp.int32)
-    all_cot = lax.all_gather(own_cot, EVERY, axis=0, tiled=True)
+    tokens = sources * rows_dev
+    piece = min(tokens, 4096)
+    if tokens > piece:
+        all_cot = lax.all_gather(own_cot, EVERY, axis=0, tiled=True)
+    else:
+        all_cot = ordered_gather(own_cot, EVERY)
 
     small = jnp.concatenate([attn_gain, latent_gain, moe_gain, router_proj.reshape(-1)])
     cuts = [attn_gain.size, latent_gain.size, moe_gain.size, router_proj.size]
@@ -427,9 +475,10 @@
     own_normed = (inputs * scale_one * attn_gain).astype(jnp.bfloat16)
     latent_shard = latent_proj.T
     far_normed = swap(lax.dynamic_slice_in_dim(own_normed, far, width_dp, 1), "dp", 1)
+    far_part = mm(far_normed, latent_shard, NT)
     compressed = mm(
         lax.dynamic_slice_in_dim(own_normed, near, width_dp, 1), latent_shard, NT
-    ) + swap(mm(far_normed, latent_shard, NT), "dp", 1)
+    ) + swap(far_part, "dp", 1)
 
     span_in = cube_gather(own_in, "experts")
     query_shard, far_normed = gate(query_proj, far_normed)
@@ -482,7 +531,8 @@
     span_float = span_in.astype(jnp.float32)
     scale_span = lax.rsqrt(jnp.mean(span_float * span_float, axis=1, keepdims=True) + eps_norm)
     normed = (span_float * scale_span * attn_gain).astype(jnp.bfloat16)
-    query_raw = mm(normed, query_proj).reshape(span_rows, heads, NOPE + ROPE)
+    query_raw = mm(normed, query_proj)
+    query_raw = query_raw.reshape(span_rows, heads, NOPE + ROPE)
     q_nope = query_raw[:, :, :NOPE].reshape(span_rows, heads * NOPE).astype(jnp.bfloat16)
     q_rope = (
         rotate(query_raw[:, :, NOPE:], cosine[:, None, :], sine[:, None, :])
@@ -494,11 +544,13 @@
     attended, lse = attend_fwd(
         q_nope, q_rope, keyvals, rope_all, q_pos, key_positions, score_scale
     )
-    hidden = inputs + cube_scatter(mm(attended, output_proj), "experts")
+    mixed = mm(attended, output_proj)
+    hidden = inputs + cube_scatter(mixed, "experts")
     scale_two = lax.rsqrt(jnp.mean(hidden * hidden, axis=1, keepdims=True) + eps_norm)
     hidden_normed = (hidden * scale_two * moe_gain).astype(jnp.bfloat16)
 
-    gates = jax.nn.sigmoid(mm(hidden_normed, router_proj))
+    gates = mm(hidden_normed, router_proj)
+    gates = jax.nn.sigmoid(gates)
     picked = jnp.any(routes[0][:, :, None] == names[None, None, :], axis=1)
     chosen = jnp.where(picked, gates, 0.0)
     chosen_total = jnp.sum(chosen, axis=1, keepdims=True)
@@ -558,8 +610,6 @@
     code = jnp.where(columns == column, high, 0.0) + jnp.where(
         columns == column + count_dp * experts, weight_grad - high, 0.0
     )
-    tokens = sources * rows_dev
-    piece = min(tokens, 4096)
     side = D // 2
 
     def scatter_every(values):
@@ -661,8 +711,33 @@
     outgoing, act_weighted = gate(hidden_grad.astype(jnp.bfloat16), act_weighted)
     hidden_round = cube_gather(outgoing, "experts")
     results = mm(act_weighted, down).astype(jnp.bfloat16)
-    (forward_rows,) = place_rows(take, results, None, (D,))
-    routed = scatter_every(forward_rows)
+    every_bits = bits_of(EVERY)
+    inner = [bit for bit in every_bits if bit[0] == "experts"][::-1]
+    along = [bit for bit in every_bits if bit[0] == "context"][::-1]
+    across = [bit for bit in every_bits if bit[0] == "dp"]
+    orders = (
+        inner[:1] + inner[1:] + across + along,
+        inner[:1] + along + across + inner[1:],
+    )
+    if tokens > piece:
+        (forward_rows,) = place_rows(take, results, None, (D,))
+        routed = scatter_every(forward_rows)
+    else:
+        halves = []
+        for part, values in enumerate(place_rows(take, results, None, (side, D - side))):
+            halves.append(
+                scatter_stage(
+                    split_bits(values, every_bits), every_bits, orders[part][0], jnp.bfloat16
+                )
+            )
+        hidden_round, first_half, second_half = gate(hidden_round, halves[0][0], halves[1][0])
+        routed = []
+        for part, values in enumerate((first_half, second_half)):
+            bits = halves[part][1]
+            for stage in orders[part][1:]:
+                values, bits = scatter_stage(values, bits, stage, jnp.bfloat16)
+            routed.append(values)
+        routed = jnp.concatenate(routed, axis=1)
 
     def sum_heads(values):
         kept = lax.dynamic_slice_in_dim(values, near, width_dp, 0)
@@ -690,17 +765,16 @@
         score_scale,
     )
     latent_outgoing = jnp.concatenate([mm(dkv, expand_proj, NT).astype(jnp.bfloat16), dkr], axis=1)
-    latent_part = lax.psum_scatter(
-        latent_outgoing, ("context", "experts"), scatter_dimension=0, tiled=True
-    ).astype(jnp.float32)
+    latent_part = ordered_scatter(latent_outgoing, ("context", "experts"), inner + along)
     dq_rope = rotate_back(dq_rope.transpose(1, 0, 2), cosine[:, None, :], sine[:, None, :])
     query_raw_grad = (
         jnp.concatenate([dq_nope.reshape(span_rows, heads, NOPE), dq_rope], axis=2)
         .reshape(span_rows, heads * (NOPE + ROPE))
         .astype(jnp.bfloat16)
     )
+    query_wide_grad = mm(normed, query_raw_grad, TN)
     head_grads = jnp.concatenate(
-        [mm(normed, query_raw_grad, TN), mm(latent_all, dkv, TN).reshape(D, -1)], axis=1
+        [query_wide_grad, mm(latent_all, dkv, TN).reshape(D, -1)], axis=1
     )
     head_grads = sum_heads(head_grads)
     input_part = cube_scatter(mm(query_raw_grad, query_proj, NT), "experts")
@@ -712,14 +786,9 @@
         [latent_grad, rotate_back(latent_part[:, RANK:], own_cosine, own_sine)], axis=1
     ).astype(jnp.bfloat16)
     latent_proj_grad = mm(own_normed, compressed_grad, TN)
-    kept = lax.dynamic_slice_in_dim(latent_proj_grad, near, width_dp, 0)
-    sent = lax.dynamic_slice_in_dim(latent_proj_grad, far, width_dp, 0)
-    kept = kept + swap(sent.astype(jnp.bfloat16), "dp", 1).astype(jnp.float32)
-    latent_proj_grad = lax.psum_scatter(
-        kept.astype(jnp.bfloat16), ("context", "experts"), scatter_dimension=0, tiled=True
-    )
-    latent_proj_grad = lax.all_gather(
-        latent_proj_grad, ("context", "experts"), axis=0, tiled=True
+    latent_proj_grad = ordered_scatter(latent_proj_grad, EVERY, inner + along + across)
+    latent_proj_grad = ordered_gather(
+        latent_proj_grad.astype(jnp.bfloat16), ("context", "experts")
     ).astype(jnp.float32)
     head_grads, output_proj_grad = full_heads(head_grads), full_heads(output_part).T
     query_wide = heads * (NOPE + ROPE)

time: 1360 us -> 1440 us (1.059)
  waiting for transfers between devices: 714 us -> 608 us
  other arithmetic: 101 us -> 188 us
  local copies, waits for them, and re-layouts: 104 us -> 170 us
  starting transfers between devices: 99.1 us -> 132 us
    ppermute x32 -> x64, waiting for transfers between devices: 255 us -> 608 us  [swap(): return lax.ppermute(values, axis, [(i, i ^ mask) for i in range(count)])]
    reduce_scatter x2 -> x1, waiting for transfers between devices: 170 us -> 0.01 us  [scatter_every(): return lax.psum_scatter(values, EVERY, scatter_dimension=0, tiled=True)]
    all_gather x1, waiting for transfers between devices: 100 us -> 0.01 us  [layer(): lax.all_gather(jnp.concatenate([hidden_normed, weights_high, weights_low,...]
    all_gather x3 -> x0, waiting for transfers between devices: 84.6 us -> none  [the longest x1 84.6 us: layer(): all_cot = lax.all_gather(own_cot, EVERY, axis=0, tiled=True)]
    reduce_scatter x2, waiting for transfers between devices: 45.5 us -> 0.01 us  [sum_heads(): return lax.psum_scatter(kept, 'context', scatter_dimension=0, tiled=True)]
    select_n x0 -> x24, other arithmetic: none -> 44.4 us  [ordered_gather(): jnp.where(bit_here(axis, mask) == 0, jnp.stack([values, got], axis=at), j...]
    reduce_scatter x2 -> x0, waiting for transfers between devices: 41.7 us -> none  [the longest x1 27.8 us: layer(): lax.psum_scatter(latent_outgoing, ('context', 'experts'), scatter_dimensi...]
    ppermute x32 -> x64, starting transfers between devices: 97.5 us -> 130 us  [swap(): return lax.ppermute(values, axis, [(i, i ^ mask) for i in range(count)])]
  transfers between devices with their start and end apart: 45 -> 71, of which waited for: 27 -> 36; matrix products, arithmetic and copies ran while one was open for 25% -> 31% of each run, Pallas kernels for 2% -> 3%
where the time goes in v2:
time: 1440 us; the launch traced here: 1430 us
  waiting for transfers between devices  608 us (42%)
  matrix products  238 us (17%)
  other arithmetic  188 us (13%)
  local copies, waits for them, and re-layouts  170 us (12%)
  starting transfers between devices  132 us (9%)
  Pallas kernels  81.7 us (6%)
  between operations  16.5 us (1%)
    ppermute x64, waiting for transfers between devices, swap(): return lax.ppermute(values, axis, [(i, i ^ mask) for i in range(count)])  608 us
    dot_general x17, matrix products, mm(): lax.dot_general(left, right, dims, preferred_element_type=jnp.float32)  177 us
    ppermute x64, starting transfers between devices, swap(): return lax.ppermute(values, axis, [(i, i ^ mask) for i in range(count)])  130 us
    dot_general x10, matrix products, mm(): return jnp.dot(left, right, preferred_element_type=jnp.float32)  55.8 us
    select_n x24, other arithmetic, ordered_gather(): jnp.where(bit_here(axis, mask) == 0, jnp.stack([values, got], axis=at), j...  44.4 us
    unnamed x242, local copies, waits for them, and re-layouts  42.7 us
  transfers between devices with their start and end apart: 71, of which 36 were waited for; matrix products, arithmetic and copies ran while one was open for 31% of the time, Pallas kernels for 3%

profile of v2, /device:TPU:0, one launch (start us, length us, event | category | flops | bytes accessed | tf_op | source)
XLA Modules:
  0.0 1434.4 jit_solution(14117875619348642476)
XLA Ops:
  23.2 7.0 collective-permute-done.3
  44.8 11.4 collective-permute-done
  65.1 13.7 collective-permute-done.4
  82.6 7.5 collective-permute-done.6
  122.1 14.6 %attend_fwd.1 = (bf16[512,512]{1,0:T(8,128)(2,1)}, f32[4,512,1]{2,1,0:T(8,128)}) custom-call(bf16[512,512]{1,0:T(8,128)(2,1)} %copy.249.refs_0_, bf16[4,512,64]{2,1,0:T(8,128)(2,1)} %fusion.89.refs_1_, bf16[2048,1024]{1,0:T(8,128)(2,1)} %convolution_convert_fusion.2.refs_2_, bf16[2048,64]{1,0:T(8,128)(2,1)} %slice.262.refs_3_, s32[512,1]{1,0:T(8,128)} %fusion.101.refs_4_, ...), custom_call_target="tpu_custom_call" | custom-call | flops 2684354560 | bytes 8388608 | tf_op jit(solution)/shard_map/attend_fwd/pallas_call | solution.py:267
  149.3 10.8 collective-permute-done.9
  169.3 15.2 %collective-permute-done.15 = bf16[128,2048]{1,0:T(8,128)(2,1)} collective-permute-done((bf16[128,2048]{1,0:T(8,128)(2,1)S(1)}, bf16[128,2048]{1,0:T(8,128)(2,1)}, u32[]{:S(2)}, u32[]{:S(2)}) %collective-permute-start.15) | collective-permute-done | bytes 524320 | tf_op jit(solution)/shard_map/ppermute | solution.py:74
  191.4 70.8 %collective-permute-done.16 = bf16[2,128,2048]{2,1,0:T(8,128)(2,1)} collective-permute-done((bf16[2,128,2048]{2,1,0:T(8,128)(2,1)}, bf16[2,128,2048]{2,1,0:T(8,128)(2,1)}, u32[]{:S(2)}, u32[]{:S(2)}) %collective-permute-start.16) | collective-permute-done | bytes 1048608 | tf_op jit(solution)/shard_map/ppermute | solution.py:74
  269.8 90.6 %collective-permute-done.17 = bf16[2,2,128,2048]{3,2,0,1:T(8,128)(2,1)} collective-permute-done((bf16[2,2,128,2048]{3,2,0,1:T(8,128)(2,1)}, bf16[2,2,128,2048]{3,2,0,1:T(8,128)(2,1)}, u32[]{:S(2)}, u32[]{:S(2)}) %collective-permute-start.17) | collective-permute-done | bytes 2097184 | tf_op jit(solution)/shard_map/ppermute | solution.py:74
  371.4 85.5 %collective-permute-done.18 = bf16[2,2,2,128,2048]{4,3,0,1,2:T(8,128)(2,1)} collective-permute-done((bf16[2,2,2,128,2048]{4,3,0,1,2:T(8,128)(2,1)}, bf16[2,2,2,128,2048]{4,3,0,1,2:T(8,128)(2,1)}, u32[]{:S(2)}, u32[]{:S(2)}) %collective-permute-start.18) | collective-permute-done | bytes 4194336 | tf_op jit(solution)/shard_map/ppermute | solution.py:74
  456.9 7.8 maximum_select_fusion.2
  499.2 10.0 maximum_select_fusion
  509.2 6.7 copy.257
  515.9 9.2 pick_rows.2
  528.4 7.9 fusion.19
  536.4 9.4 pick_rows.3
  551.3 16.8 %fusion.159 = f32[2048,1408]{0,1:T(8,128)S(1)} fusion(bf16[2048,2048]{1,0:T(8,128)(2,1)} %copy-done.2, bf16[1408,2048]{1,0:T(8,128)(2,1)} %bitcast.349), kind=kOutput, calls=%fused_computation.402 | convolution fusion | flops 11811160064 | bytes 25690112 | tf_op jit(solution)/shard_map/dot_general | solution.py:65
  568.0 8.2 fusion.7
  582.5 17.4 %convolution_convert_fusion.1.refs_0_ = bf16[2048,2048]{1,0:T(8,128)(2,1)S(1)} fusion(bf16[1408,2048]{1,0:T(8,128)(2,1)} %bitcast.350, bf16[2048,704]{0,1:T(8,128)(2,1)} %get-tuple-element.189, bf16[2048,704]{0,1:T(8,128)(2,1)} %get-tuple-element.190), kind=kOutput, calls=%fused_computation.29 | convolution fusion | flops 11826888704 | bytes 19922944 | tf_op jit(solution)/shard_map/dot_general | solution.py:64
  601.6 9.3 place_rows.2
  613.1 63.6 %collective-permute-done.20 = bf16[1408,1024]{1,0:T(8,128)(2,1)} collective-permute-done((bf16[1408,1024]{1,0:T(8,128)(2,1)}, bf16[1408,1024]{1,0:T(8,128)(2,1)}, u32[]{:S(2)}, u32[]{:S(2)}) %collective-permute-start.20) | collective-permute-done | bytes 2883616 | tf_op jit(solution)/shard_map/ppermute | solution.py:74
  676.8 34.5 %fusion.75 = f32[4096,1408]{0,1:T(8,128)} fusion(bf16[1408,1024]{1,0:T(8,128)(2,1)} %collective-permute-done.20, bf16[1408,1024]{1,0:T(8,128)(2,1)} %bitcast.352, pred[]{:T(512)S(6)} %eq.143, bf16[4096,2176]{1,0:T(8,128)(2,1)} %all-gather.7.cloned.1.call-done.refs_0_), kind=kOutput, calls=%fused_computation.201 | convolution fusion | flops 23648272384 | bytes 45613056 | tf_op jit(solution)/shard_map/dot_general | solution.py:65
  711.3 14.2 slice.216
  725.5 29.6 %multiply_convert_fusion = (bf16[4096,704]{0,1:T(8,128)(2,1)}, bf16[4096,704]{0,1:T(8,128)(2,1)}, bf16[4096,704]{0,1:T(8,128)(2,1)}) fusion(f32[4096,1408]{0,1:T(8,128)} %fusion.75, bf16[4096,2048]{1,0:T(8,128)(2,1)} %bitcast.279, bf16[704,1024]{1,0:T(8,128)(2,1)} %collective-permute-done.21, bf16[704,1024]{1,0:T(8,128)(2,1)} %param.29, pred[]{:T(512)S(6)} %eq.143), kind=kOutput, calls=%fused_computation.11 | convolution fusion | flops 11870273536 | bytes 60030976 | tf_op jit(solution)/shard_map/dot_general | solution.py:65
  762.4 7.3 convolution_convert_fusion.5
  771.7 19.2 %fusion = f32[1408,1024]{1,0:T(8,128)} fusion(bf16[4096,704]{0,1:T(8,128)(2,1)} %get-tuple-element.184, bf16[4096,704]{0,1:T(8,128)(2,1)} %get-tuple-element.185, bf16[4096,2048]{1,0:T(8,128)(2,1)} %slice.216, s32[]{:T(128)S(6)} %select_n.670), kind=kOutput, calls=%fused_computation.10 | convolution fusion | flops 11834228736 | bytes 25690116 | tf_op jit(solution)/shard_map/dot_general | solution.py:65
  790.9 19.5 %fusion.160 = f32[1408,2048]{1,0:T(8,128)} fusion(bf16[2048,1408]{0,1:T(8,128)(2,1)} %pad_maximum_fusion.2, bf16[2048,2048]{1,0:T(8,128)(2,1)} %copy-done.2), kind=kOutput, calls=%fused_computation.403 | convolution fusion | flops 11811160064 | bytes 25690112 | tf_op jit(solution)/shard_map/dot_general | solution.py:65
  810.3 10.3 fusion.161
  823.7 69.3 %collective-permute-start.23 = (bf16[128,4096]{1,0:T(8,128)(2,1)S(1)}, bf16[128,4096]{1,0:T(8,128)(2,1)S(1)}, u32[]{:S(2)}, u32[]{:S(2)}) collective-permute-start(bf16[128,4096]{1,0:T(8,128)(2,1)S(1)} %fusion.28), channel_id=1, source_target_pairs={{0,2},{1,3},{2,0},{3,1},{4,6},{5,7},{6,4},{7,5},{8,10},{9,11},{10,... | collective-permute-start | bytes 3145736 | tf_op jit(solution)/shard_map/ppermute | solution.py:74
  893.0 9.4 fusion.3
  902.3 14.4 %collective-permute-done.23 = bf16[128,4096]{1,0:T(8,128)(2,1)S(1)} collective-permute-done((bf16[128,4096]{1,0:T(8,128)(2,1)S(1)}, bf16[128,4096]{1,0:T(8,128)(2,1)S(1)}, u32[]{:S(2)}, u32[]{:S(2)}) %collective-permute-start.23) | collective-permute-done | bytes 1048608 | tf_op jit(solution)/shard_map/ppermute | solution.py:74
  932.4 9.0 convolution_convert_fusion.refs_0_
  941.4 11.1 place_rows.3
  952.5 8.4 constant_dynamic-slice_fusion.3
  981.7 11.3 collective-permute-done.24
  1042.5 28.0 %attend_bwd.1 = (f32[1,512,512]{2,1,0:T(8,128)}, f32[1,4,512,64]{3,2,1,0:T(8,128)}, bf16[2048,1024]{1,0:T(8,128)(2,1)}, bf16[2048,64]{1,0:T(8,128)(2,1)}) custom-call(bf16[512,512]{1,0:T(8,128)(2,1)} %copy.249.refs_0_, bf16[4,512,64]{2,1,0:T(8,128)(2,1)} %fusion.89.refs_1_, bf16[2048,1024]{1,0:T(8,128)(2,1)} %convolution_convert_fusion.2.refs_2_, ...), custom_call_target="tpu_custom_call" | custom-call | flops 6979321856 | bytes 16777216 | tf_op jit(solution)/shard_map/attend_bwd/pallas_call | solution.py:367
  1099.7 7.0 reshape.1494
  1132.7 11.4 collective-permute-done.58
  1204.2 9.8 collective-permute-done.42
  1213.9 11.0 collective-permute-done.37
  1237.5 21.6 %collective-permute-done.45 = f32[2560]{0:T(1024)S(1)} collective-permute-done((f32[2560]{0:T(1024)S(1)}, f32[2560]{0:T(1024)S(1)}, u32[]{:S(2)}, u32[]{:S(2)}) %collective-permute-start.45) | collective-permute-done | bytes 10272 | tf_op jit(solution)/shard_map/ppermute | solution.py:74
  1263.2 21.2 %collective-permute-done.46 = f32[2560]{0:T(1024)S(1)} collective-permute-done((f32[2560]{0:T(1024)S(1)}, f32[2560]{0:T(1024)S(1)}, u32[]{:S(2)}, u32[]{:S(2)}) %collective-permute-start.46) | collective-permute-done | bytes 10272 | tf_op jit(solution)/shard_map/ppermute | solution.py:74
  1293.9 10.2 collective-permute-done.50
  1311.3 14.8 %collective-permute-done.51 = bf16[2,2,64,576]{3,2,1,0:T(8,128)(2,1)S(1)} collective-permute-done((bf16[2,2,64,576]{3,2,1,0:T(8,128)(2,1)S(1)}, bf16[2,2,64,576]{3,2,1,0:T(8,128)(2,1)S(1)}, u32[]{:S(2)}, u32[]{:S(2)}) %collective-permute-start.51) | collective-permute-done | bytes 294944 | tf_op jit(solution)/shard_map/ppermute | solution.py:74
  1330.2 8.3 collective-permute-done.52
  1349.4 16.0 %collective-permute-done.54 = bf16[64,576]{1,0:T(8,128)(2,1)S(1)} collective-permute-done((bf16[64,576]{1,0:T(8,128)(2,1)S(1)}, bf16[64,576]{1,0:T(8,128)(2,1)S(1)}, u32[]{:S(2)}, u32[]{:S(2)}) %collective-permute-start.54) | collective-permute-done | bytes 73760 | tf_op jit(solution)/shard_map/ppermute | solution.py:74
  1367.0 21.5 %collective-permute-done.55 = bf16[2,64,576]{2,1,0:T(8,128)(2,1)S(1)} collective-permute-done((bf16[2,64,576]{2,1,0:T(8,128)(2,1)S(1)}, bf16[2,64,576]{2,1,0:T(8,128)(2,1)S(1)}, u32[]{:S(2)}, u32[]{:S(2)}) %collective-permute-start.55) | collective-permute-done | bytes 147488 | tf_op jit(solution)/shard_map/ppermute | solution.py:74
  1390.3 8.1 collective-permute-done.56
  (607 shorter events, 468.4 us)
Async XLA Ops:
  7.2 106.5 %all-gather.5.cloned.1.call-start = ((), (), s32[]{:S(2)}) async-start(), calls=%async_computation.3 | async-start | bytes 2785280 | tf_op jit(solution)/shard_map/all_gather | solution.py:523
  42.3 494.1 %all-gather.7.cloned.1.call-start = ((), (), s32[]{:S(2)}) async-start(), calls=%async_computation.4 | async-start | bytes 18382848 | tf_op jit(solution)/shard_map/all_gather | solution.py:561
  42.6 13.5 collective-permute-start
  44.2 34.6 %collective-permute-start.4 = (bf16[1024,768]{1,0:T(8,128)(2,1)}, bf16[1024,768]{1,0:T(8,128)(2,1)}, u32[]{:S(2)}, u32[]{:S(2)}) collective-permute-start(bf16[1024,768]{1,0:T(8,128)(2,1)} %param.21), channel_id=1, source_target_pairs={{0,16},{16,0},{1,17},{17,1},{2,18},{18,2},{3,19},{19,3},{4,20},{20... | collective-permute-start | bytes 4718600 | tf_op jit(solution)/shard_map/ppermute | solution.py:74
  58.0 21.3 %collective-permute-start.1 = (bf16[256,2048]{1,0:T(8,128)(2,1)}, bf16[256,2048]{1,0:T(8,128)(2,1)}, u32[]{:S(2)}, u32[]{:S(2)}) collective-permute-start(bf16[256,2048]{1,0:T(8,128)(2,1)} %pad_maximum_fusion.8), channel_id=1, source_target_pairs={{0,1},{1,0},{2,3},{3,2},{4,5},{5,4},{6,7},{7,6},{8,9},{9,8},{10,11... | collective-permute-start | bytes 3145736 | tf_op jit(solution)/shard_map/ppermute | solution.py:74
  90.9 22.8 %collective-permute-start.7 = (bf16[512,1024]{1,0:T(8,128)(2,1)}, bf16[512,1024]{1,0:T(8,128)(2,1)}, u32[]{:S(2)}, u32[]{:S(2)}) collective-permute-start(bf16[512,1024]{1,0:T(8,128)(2,1)} %param.25), channel_id=1, source_target_pairs={{0,16},{16,0},{1,17},{17,1},{2,18},{18,2},{3,19},{19,3},{4,20},{20... | collective-permute-start | bytes 3145736 | tf_op jit(solution)/shard_map/ppermute | solution.py:74
  145.8 14.3 collective-permute-start.9
  167.1 751.3 %reduce-scatter.4.cloned.1.call-start = ((), (), s32[]{:S(2)}) async-start(), calls=%async_computation.5 | async-start | bytes 18382848 | tf_op jit(solution)/shard_map/reduce_scatter | solution.py:616
  167.7 16.8 %collective-permute-start.15 = (bf16[128,2048]{1,0:T(8,128)(2,1)S(1)}, bf16[128,2048]{1,0:T(8,128)(2,1)}, u32[]{:S(2)}, u32[]{:S(2)}) collective-permute-start(bf16[128,2048]{1,0:T(8,128)(2,1)S(1)} %bitcast.292), channel_id=1, source_target_pairs={{0,16},{16,0},{1,17},{17,1},{2,18},{18,2},{3,19},{19,3},{4,20},{20... | collective-permute-start | bytes 1572872 | tf_op jit(solution)/shard_map/ppermute | solution.py:74
  186.9 75.2 %collective-permute-start.16 = (bf16[2,128,2048]{2,1,0:T(8,128)(2,1)}, bf16[2,128,2048]{2,1,0:T(8,128)(2,1)}, u32[]{:S(2)}, u32[]{:S(2)}) collective-permute-start(bf16[2,128,2048]{2,1,0:T(8,128)(2,1)} %maximum_select_fusion.17), channel_id=1, source_target_pairs={{0,8},{4,12},{8,0},{12,4},{1,9},{5,13},{9,1},{13,5},{2,10},{6,14},... | collective-permute-start | bytes 3145736 | tf_op jit(solution)/shard_map/ppermute | solution.py:74
  265.4 95.0 %collective-permute-start.17 = (bf16[2,2,128,2048]{3,2,0,1:T(8,128)(2,1)}, bf16[2,2,128,2048]{3,2,0,1:T(8,128)(2,1)}, u32[]{:S(2)}, u32[]{:S(2)}) collective-permute-start(bf16[2,2,128,2048]{3,2,0,1:T(8,128)(2,1)} %maximum_select_fusion.12), channel_id=1, source_target_pairs={{0,4},{4,0},{8,12},{12,8},{1,5},{5,1},{9,13},{13,9},{2,6},{6,2},{1... | collective-permute-start | bytes 6291464 | tf_op jit(solution)/shard_map/ppermute | solution.py:74
  364.9 92.0 %collective-permute-start.18 = (bf16[2,2,2,128,2048]{4,3,0,1,2:T(8,128)(2,1)}, bf16[2,2,2,128,2048]{4,3,0,1,2:T(8,128)(2,1)}, u32[]{:S(2)}, u32[]{:S(2)}) collective-permute-start(bf16[2,2,2,128,2048]{4,3,0,1,2:T(8,128)(2,1)} %maximum_select_fusion.5), channel_id=1, source_target_pairs={{0,2},{1,3},{2,0},{3,1},{4,6},{5,7},{6,4},{7,5},{8,10},{9,11},{10,... | collective-permute-start | bytes 12582920 | tf_op jit(solution)/shard_map/ppermute | solution.py:74
  464.7 34.5 %collective-permute-start.19 = (bf16[2,2,2,2,128,2048]{5,4,0,1,2,3:T(8,128)(2,1)}, bf16[2,2,2,2,128,2048]{5,4,0,1,2,3:T(8,128)(2,1)}, u32[]{:S(2)}, u32[]{:S(2)}) collective-permute-start(bf16[2,2,2,2,128,2048]{5,4,0,1,2,3:T(8,128)(2,1)} %maximum_select_fusion.2), channel_id=1, source_target_pairs={{0,1},{1,0},{2,3},{3,2},{4,5},{5,4},{6,7},{7,6},{8,9},{9,8},{10,11... | collective-permute-start | bytes 25165832 | tf_op jit(solution)/shard_map/ppermute | solution.py:74
  611.0 682.5 %reduce-scatter.8.cloned.1.call-start = ((), (), s32[]{:S(2)}) async-start(), calls=%async_computation.8 | async-start | bytes 1310720 | tf_op jit(solution)/shard_map/reduce_scatter | solution.py:748
  611.1 65.7 %collective-permute-start.20 = (bf16[1408,1024]{1,0:T(8,128)(2,1)}, bf16[1408,1024]{1,0:T(8,128)(2,1)}, u32[]{:S(2)}, u32[]{:S(2)}) collective-permute-start(bf16[1408,1024]{1,0:T(8,128)(2,1)} %bitcast.351), channel_id=1, source_target_pairs={{0,16},{16,0},{1,17},{17,1},{2,18},{18,2},{3,19},{19,3},{4,20},{20... | collective-permute-start | bytes 8650760 | tf_op jit(solution)/shard_map/ppermute | solution.py:74
  612.9 112.6 %collective-permute-start.21 = (bf16[704,1024]{1,0:T(8,128)(2,1)}, bf16[704,1024]{1,0:T(8,128)(2,1)}, u32[]{:S(2)}, u32[]{:S(2)}) collective-permute-start(bf16[704,1024]{1,0:T(8,128)(2,1)} %param.29), channel_id=1, source_target_pairs={{0,16},{16,0},{1,17},{17,1},{2,18},{18,2},{3,19},{19,3},{4,20},{20... | collective-permute-start | bytes 4325384 | tf_op jit(solution)/shard_map/ppermute | solution.py:74
  771.7 48.9 %collective-permute-start.22 = (bf16[256,4096]{1,0:T(8,128)(2,1)}, bf16[256,4096]{1,0:T(8,128)(2,1)}, u32[]{:S(2)}, u32[]{:S(2)}) collective-permute-start(bf16[256,4096]{1,0:T(8,128)(2,1)} %pad_maximum_fusion.5), channel_id=1, source_target_pairs={{0,1},{1,0},{2,3},{3,2},{4,5},{5,4},{6,7},{7,6},{8,9},{9,8},{10,11... | collective-permute-start | bytes 6291464 | tf_op jit(solution)/shard_map/ppermute | solution.py:74
  823.7 93.1 %collective-permute-start.23 = (bf16[128,4096]{1,0:T(8,128)(2,1)S(1)}, bf16[128,4096]{1,0:T(8,128)(2,1)S(1)}, u32[]{:S(2)}, u32[]{:S(2)}) collective-permute-start(bf16[128,4096]{1,0:T(8,128)(2,1)S(1)} %fusion.28), channel_id=1, source_target_pairs={{0,2},{1,3},{2,0},{3,1},{4,6},{5,7},{6,4},{7,5},{8,10},{9,11},{10,... | collective-permute-start | bytes 3145736 | tf_op jit(solution)/shard_map/ppermute | solution.py:74
  965.6 56.4 %collective-permute-start.27 = (bf16[2,2,2,2,128,1024]{5,4,3,0,1,2:T(8,128)(2,1)}, bf16[2,2,2,2,128,1024]{5,4,3,0,1,2:T(8,128)(2,1)}, u32[]{:S(2)}, u32[]{:S(2)}) collective-permute-start(bf16[2,2,2,2,128,1024]{5,4,3,0,1,2:T(8,128)(2,1)} %bitcast.270), channel_id=1, source_target_pairs={{0,1},{1,0},{2,3},{3,2},{4,5},{5,4},{6,7},{7,6},{8,9},{9,8},{10,11... | collective-permute-start | bytes 12582920 | tf_op jit(solution)/shard_map/ppermute | solution.py:74
  975.4 53.0 %collective-permute-start.26 = (bf16[2,2,2,2,128,1024]{5,4,1,2,0,3:T(8,128)(2,1)}, bf16[2,2,2,2,128,1024]{5,4,1,2,0,3:T(8,128)(2,1)}, u32[]{:S(2)}, u32[]{:S(2)}) collective-permute-start(bf16[2,2,2,2,128,1024]{5,4,1,2,0,3:T(8,128)(2,1)} %bitcast.271), channel_id=1, source_target_pairs={{0,1},{1,0},{2,3},{3,2},{4,5},{5,4},{6,7},{7,6},{8,9},{9,8},{10,11... | collective-permute-start | bytes 12582920 | tf_op jit(solution)/shard_map/ppermute | solution.py:74
  979.1 13.9 collective-permute-start.24
  994.9 24.6 %collective-permute-start.25 = (bf16[256,2048]{1,0:T(8,128)(2,1)}, bf16[256,2048]{1,0:T(8,128)(2,1)}, u32[]{:S(2)}, u32[]{:S(2)}) collective-permute-start(bf16[256,2048]{1,0:T(8,128)(2,1)} %pad_maximum_fusion.10), channel_id=1, source_target_pairs={{0,1},{1,0},{2,3},{3,2},{4,5},{5,4},{6,7},{7,6},{8,9},{9,8},{10,11... | collective-permute-start | bytes 3145736 | tf_op jit(solution)/shard_map/ppermute | solution.py:74
  1017.8 138.2 %collective-permute-start.63 = (f32[34816]{0:T(1024)S(1)}, f32[34816]{0:T(1024)}, u32[]{:S(2)}, u32[]{:S(2)}) collective-permute-start(f32[34816]{0:T(1024)S(1)} %add.638), channel_id=1, source_target_pairs={{0,16},{16,0},{1,17},{17,1},{2,18},{18,2},{3,19},{19,3},{4,20},{20... | collective-permute-start | bytes 417800 | tf_op jit(solution)/shard_map/ppermute | solution.py:74
  1110.0 88.0 %collective-permute-start.32 = (bf16[2,2,2,128,1024]{4,3,2,0,1:T(8,128)(2,1)}, bf16[2,2,2,128,1024]{4,3,2,0,1:T(8,128)(2,1)}, u32[]{:S(2)}, u32[]{:S(2)}) collective-permute-start(bf16[2,2,2,128,1024]{4,3,2,0,1:T(8,128)(2,1)} %dynamic-slice_bitcast_fusion), channel_id=1, source_target_pairs={{0,4},{4,0},{8,12},{12,8},{1,5},{5,1},{9,13},{13,9},{2,6},{6,2},{1... | collective-permute-start | bytes 6291464 | tf_op jit(solution)/shard_map/ppermute | solution.py:74
  1117.8 27.8 %collective-permute-start.38 = (bf16[2,2,2,128,576]{3,4,2,1,0:T(8,128)(2,1)}, bf16[2,2,2,128,576]{3,4,2,1,0:T(8,128)(2,1)}, u32[]{:S(2)}, u32[]{:S(2)}) collective-permute-start(bf16[2,2,2,128,576]{3,4,2,1,0:T(8,128)(2,1)} %bitcast.272), channel_id=1, source_target_pairs={{0,1},{1,0},{2,3},{3,2},{4,5},{5,4},{6,7},{7,6},{8,9},{9,8},{10,11... | collective-permute-start | bytes 3538952 | tf_op jit(solution)/shard_map/ppermute | solution.py:74
  1118.0 26.1 %collective-permute-start.58 = (bf16[1024,512]{1,0:T(8,128)(2,1)S(1)}, bf16[1024,512]{1,0:T(8,128)(2,1)S(1)}, u32[]{:S(2)}, u32[]{:S(2)}) collective-permute-start(bf16[1024,512]{1,0:T(8,128)(2,1)S(1)} %dynamic-slice_convert_fusion.2), channel_id=1, source_target_pairs={{0,16},{16,0},{1,17},{17,1},{2,18},{18,2},{3,19},{19,3},{4,20},{20... | collective-permute-start | bytes 3145736 | tf_op jit(solution)/shard_map/ppermute | solution.py:74
  1129.9 59.6 %collective-permute-start.48 = (bf16[1024,1024]{0,1:T(8,128)(2,1)}, bf16[1024,1024]{0,1:T(8,128)(2,1)}, u32[]{:S(2)}, u32[]{:S(2)}) collective-permute-start(bf16[1024,1024]{0,1:T(8,128)(2,1)} %fusion.12), channel_id=1, source_target_pairs={{0,16},{16,0},{1,17},{17,1},{2,18},{18,2},{3,19},{19,3},{4,20},{20... | collective-permute-start | bytes 6291464 | tf_op jit(solution)/shard_map/ppermute | solution.py:74
  1144.1 19.9 %collective-permute-start.36 = (bf16[256,2048]{1,0:T(8,128)(2,1)}, bf16[256,2048]{1,0:T(8,128)(2,1)}, u32[]{:S(2)}, u32[]{:S(2)}) collective-permute-start(bf16[256,2048]{1,0:T(8,128)(2,1)} %pad_maximum_fusion.11), channel_id=1, source_target_pairs={{0,1},{1,0},{2,3},{3,2},{4,5},{5,4},{6,7},{7,6},{8,9},{9,8},{10,11... | collective-permute-start | bytes 3145736 | tf_op jit(solution)/shard_map/ppermute | solution.py:74
  1145.4 193.8 %reduce-scatter.6.cloned.1.call-start = ((), (), s32[]{:S(2)}) async-start(), calls=%async_computation.6 | async-start | bytes 2621440 | tf_op jit(solution)/shard_map/reduce_scatter | solution.py:748
  1152.7 21.6 %collective-permute-start.39 = (bf16[2,2,128,576]{2,3,1,0:T(8,128)(2,1)}, bf16[2,2,128,576]{2,3,1,0:T(8,128)(2,1)}, u32[]{:S(2)}, u32[]{:S(2)}) collective-permute-start(bf16[2,2,128,576]{2,3,1,0:T(8,128)(2,1)} %bitcast.273), channel_id=1, source_target_pairs={{0,2},{1,3},{2,0},{3,1},{4,6},{5,7},{6,4},{7,5},{8,10},{9,11},{10,... | collective-permute-start | bytes 1769480 | tf_op jit(solution)/shard_map/ppermute | solution.py:74
  1156.0 57.9 %collective-permute-start.42 = (bf16[576,1024]{1,0:T(8,128)(2,1)}, bf16[576,1024]{1,0:T(8,128)(2,1)}, u32[]{:S(2)}, u32[]{:S(2)}) collective-permute-start(bf16[576,1024]{1,0:T(8,128)(2,1)} %bitcast.296), channel_id=1, source_target_pairs={{0,16},{16,0},{1,17},{17,1},{2,18},{18,2},{3,19},{19,3},{4,20},{20... | collective-permute-start | bytes 3538952 | tf_op jit(solution)/shard_map/ppermute | solution.py:74
  1164.0 68.4 %collective-permute-start.28 = (bf16[2,2,2,128,1024]{4,3,1,2,0:T(8,128)(2,1)}, bf16[2,2,2,128,1024]{4,3,1,2,0:T(8,128)(2,1)}, u32[]{:S(2)}, u32[]{:S(2)}) collective-permute-start(bf16[2,2,2,128,1024]{4,3,1,2,0:T(8,128)(2,1)} %dynamic-slice_bitcast_fusion.1), channel_id=1, source_target_pairs={{0,2},{1,3},{2,0},{3,1},{4,6},{5,7},{6,4},{7,5},{8,10},{9,11},{10,... | collective-permute-start | bytes 6291464 | tf_op jit(solution)/shard_map/ppermute | solution.py:74
  1187.6 37.3 %collective-permute-start.37 = (bf16[128,2048]{1,0:T(8,128)(2,1)}, bf16[128,2048]{1,0:T(8,128)(2,1)}, u32[]{:S(2)}, u32[]{:S(2)}) collective-permute-start(bf16[128,2048]{1,0:T(8,128)(2,1)} %fusion.62), channel_id=1, source_target_pairs={{0,2},{1,3},{2,0},{3,1},{4,6},{5,7},{6,4},{7,5},{8,10},{9,11},{10,... | collective-permute-start | bytes 1572872 | tf_op jit(solution)/shard_map/ppermute | solution.py:74
  1197.7 202.9 %all-gather.11.cloned.1.call-start = ((), (), s32[]{:S(2)}) async-start(), calls=%async_computation.9 | async-start | bytes 1310720 | tf_op jit(solution)/shard_map/all_gather | solution.py:751
  1204.1 81.8 %collective-permute-start.49 = (bf16[2,2,2,2,64,576]{5,4,3,2,1,0:T(8,128)(2,1)S(1)}, bf16[2,2,2,2,64,576]{5,4,3,2,1,0:T(8,128)(2,1)S(1)}, u32[]{:S(2)}, u32[]{:S(2)}) collective-permute-start(bf16[2,2,2,2,64,576]{5,4,3,2,1,0:T(8,128)(2,1)S(1)} %fusion.43), channel_id=1, source_target_pairs={{0,1},{1,0},{2,3},{3,2},{4,5},{5,4},{6,7},{7,6},{8,9},{9,8},{10,11... | collective-permute-start | bytes 3538952 | tf_op jit(solution)/shard_map/ppermute | solution.py:74
  1228.5 63.0 %collective-permute-start.33 = (bf16[2,2,128,1024]{3,2,1,0:T(8,128)(2,1)S(1)}, bf16[2,2,128,1024]{3,2,1,0:T(8,128)(2,1)S(1)}, u32[]{:S(2)}, u32[]{:S(2)}) collective-permute-start(bf16[2,2,128,1024]{3,2,1,0:T(8,128)(2,1)S(1)} %dynamic-slice_bitcast_fusion.2), channel_id=1, source_target_pairs={{0,8},{4,12},{8,0},{12,4},{1,9},{5,13},{9,1},{13,5},{2,10},{6,14},... | collective-permute-start | bytes 3145736 | tf_op jit(solution)/shard_map/ppermute | solution.py:74
  1235.8 23.3 %collective-permute-start.45 = (f32[2560]{0:T(1024)S(1)}, f32[2560]{0:T(1024)S(1)}, u32[]{:S(2)}, u32[]{:S(2)}) collective-permute-start(f32[2560]{0:T(1024)S(1)} %add.621), channel_id=1, source_target_pairs={{0,4},{4,0},{8,12},{12,8},{1,5},{5,1},{9,13},{13,9},{2,6},{6,2},{1... | collective-permute-start | bytes 30728 | tf_op jit(solution)/shard_map/ppermute | solution.py:74
  1236.8 69.0 %collective-permute-start.29 = (bf16[2,2,128,1024]{3,2,0,1:T(8,128)(2,1)}, bf16[2,2,128,1024]{3,2,0,1:T(8,128)(2,1)}, u32[]{:S(2)}, u32[]{:S(2)}) collective-permute-start(bf16[2,2,128,1024]{3,2,0,1:T(8,128)(2,1)} %dynamic-slice_bitcast_fusion.3), channel_id=1, source_target_pairs={{0,16},{16,0},{1,17},{17,1},{2,18},{18,2},{3,19},{19,3},{4,20},{20... | collective-permute-start | bytes 3145736 | tf_op jit(solution)/shard_map/ppermute | solution.py:74
  1259.1 25.3 %collective-permute-start.46 = (f32[2560]{0:T(1024)S(1)}, f32[2560]{0:T(1024)S(1)}, u32[]{:S(2)}, u32[]{:S(2)}) collective-permute-start(f32[2560]{0:T(1024)S(1)} %add.622), channel_id=1, source_target_pairs={{0,8},{4,12},{8,0},{12,4},{1,9},{5,13},{9,1},{13,5},{2,10},{6,14},... | collective-permute-start | bytes 30728 | tf_op jit(solution)/shard_map/ppermute | solution.py:74
  1287.2 16.8 %collective-permute-start.50 = (bf16[2,2,2,64,576]{4,3,2,1,0:T(8,128)(2,1)}, bf16[2,2,2,64,576]{4,3,2,1,0:T(8,128)(2,1)}, u32[]{:S(2)}, u32[]{:S(2)}) collective-permute-start(bf16[2,2,2,64,576]{4,3,2,1,0:T(8,128)(2,1)} %fusion.83), channel_id=1, source_target_pairs={{0,2},{1,3},{2,0},{3,1},{4,6},{5,7},{6,4},{7,5},{8,10},{9,11},{10,... | collective-permute-start | bytes 1769480 | tf_op jit(solution)/shard_map/ppermute | solution.py:74
  1292.9 33.8 %collective-permute-start.34 = (bf16[2,128,1024]{2,1,0:T(8,128)(2,1)S(1)}, bf16[2,128,1024]{2,1,0:T(8,128)(2,1)}, u32[]{:S(2)}, u32[]{:S(2)}) collective-permute-start(bf16[2,128,1024]{2,1,0:T(8,128)(2,1)S(1)} %dynamic-slice_bitcast_fusion.4), channel_id=1, source_target_pairs={{0,16},{16,0},{1,17},{17,1},{2,18},{18,2},{3,19},{19,3},{4,20},{20... | collective-permute-start | bytes 1572872 | tf_op jit(solution)/shard_map/ppermute | solution.py:74
  1293.6 119.5 %all-gather.9.cloned.1.call-start = ((), (), s32[]{:S(2)}) async-start(), calls=%async_computation.7 | async-start | bytes 2621440 | tf_op jit(solution)/shard_map/all_gather | solution.py:751
  1305.7 20.3 %collective-permute-start.51 = (bf16[2,2,64,576]{3,2,1,0:T(8,128)(2,1)S(1)}, bf16[2,2,64,576]{3,2,1,0:T(8,128)(2,1)S(1)}, u32[]{:S(2)}, u32[]{:S(2)}) collective-permute-start(bf16[2,2,64,576]{3,2,1,0:T(8,128)(2,1)S(1)} %fusion.99), channel_id=1, source_target_pairs={{0,4},{4,0},{8,12},{12,8},{1,5},{5,1},{9,13},{13,9},{2,6},{6,2},{1... | collective-permute-start | bytes 884744 | tf_op jit(solution)/shard_map/ppermute | solution.py:74
  1309.4 32.7 %collective-permute-start.30 = (bf16[2,128,1024]{2,1,0:T(8,128)(2,1)}, bf16[2,128,1024]{2,1,0:T(8,128)(2,1)}, u32[]{:S(2)}, u32[]{:S(2)}) collective-permute-start(bf16[2,128,1024]{2,1,0:T(8,128)(2,1)} %dynamic-slice_bitcast_fusion.5), channel_id=1, source_target_pairs={{0,4},{4,0},{8,12},{12,8},{1,5},{5,1},{9,13},{13,9},{2,6},{6,2},{1... | collective-permute-start | bytes 1572872 | tf_op jit(solution)/shard_map/ppermute | solution.py:74
  1328.7 37.3 %collective-permute-start.35 = (bf16[128,1024]{1,0:T(8,128)(2,1)}, bf16[128,1024]{1,0:T(8,128)(2,1)}, u32[]{:S(2)}, u32[]{:S(2)}) collective-permute-start(bf16[128,1024]{1,0:T(8,128)(2,1)} %dynamic-slice_bitcast_fusion.6), channel_id=1, source_target_pairs={{0,2},{1,3},{2,0},{3,1},{4,6},{5,7},{6,4},{7,5},{8,10},{9,11},{10,... | collective-permute-start | bytes 786440 | tf_op jit(solution)/shard_map/ppermute | solution.py:74
  1345.8 19.5 %collective-permute-start.54 = (bf16[64,576]{1,0:T(8,128)(2,1)S(1)}, bf16[64,576]{1,0:T(8,128)(2,1)S(1)}, u32[]{:S(2)}, u32[]{:S(2)}) collective-permute-start(bf16[64,576]{1,0:T(8,128)(2,1)S(1)} %fusion.106), channel_id=1, source_target_pairs={{0,8},{4,12},{8,0},{12,4},{1,9},{5,13},{9,1},{13,5},{2,10},{6,14},... | collective-permute-start | bytes 221192 | tf_op jit(solution)/shard_map/ppermute | solution.py:74
  1349.3 40.8 %collective-permute-start.31 = (bf16[128,1024]{1,0:T(8,128)(2,1)S(1)}, bf16[128,1024]{1,0:T(8,128)(2,1)S(1)}, u32[]{:S(2)}, u32[]{:S(2)}) collective-permute-start(bf16[128,1024]{1,0:T(8,128)(2,1)S(1)} %dynamic-slice_bitcast_fusion.7), channel_id=1, source_target_pairs={{0,8},{4,12},{8,0},{12,4},{1,9},{5,13},{9,1},{13,5},{2,10},{6,14},... | collective-permute-start | bytes 786440 | tf_op jit(solution)/shard_map/ppermute | solution.py:74
  1365.4 23.1 %collective-permute-start.55 = (bf16[2,64,576]{2,1,0:T(8,128)(2,1)S(1)}, bf16[2,64,576]{2,1,0:T(8,128)(2,1)S(1)}, u32[]{:S(2)}, u32[]{:S(2)}) collective-permute-start(bf16[2,64,576]{2,1,0:T(8,128)(2,1)S(1)} %maximum_select_fusion.35), channel_id=1, source_target_pairs={{0,4},{4,0},{8,12},{12,8},{1,5},{5,1},{9,13},{13,9},{2,6},{6,2},{1... | collective-permute-start | bytes 442376 | tf_op jit(solution)/shard_map/ppermute | solution.py:74
  (136 other events, 2418.8 us)
Sparse Core Ops, SparseCore 0:
  42.4 43.9 all-gather.4
  167.2 191.0 all-gather.6
  611.1 193.1 reduce-scatter.3
  1145.5 30.6 reduce-scatter.7
  1197.8 47.4 reduce-scatter.5
  1293.7 34.0 all-gather.10
  1339.4 62.7 all-gather.8

commit v3 on v2

--- a/solution.py
+++ b/solution.py
@@ -55,6 +55,7 @@
 
 
 EVERY = ("dp", "context", "experts")
+INNER = EVERY[1:]
 NT = (((1,), (1,)), ((), ()))
 TN = (((0,), (0,)), ((), ()))
 
@@ -193,7 +194,7 @@
             bytes_accessed=2 * sources * (rows_dev + capacity) * width,
             transcendentals=0,
         ),
-        name="pick_rows",
+        name="pick",
     )(take, *parts)
 
 
@@ -236,7 +237,7 @@
             bytes_accessed=2 * sources * (rows_dev + capacity) * sum(shapes),
             transcendentals=0,
         ),
-        name="place_rows",
+        name="place",
     )(take, *inputs)
 
 
@@ -289,7 +290,7 @@
             bytes_accessed=4 * keys * heads * (NOPE + VDIM),
             transcendentals=heads * rows * keys,
         ),
-        name="attend_fwd",
+        name="af",
     )(q_nope, q_rope, keyvals, rope_keys, q_pos, k_pos)
 
 
@@ -401,7 +402,7 @@
             bytes_accessed=8 * keys * heads * (NOPE + VDIM),
             transcendentals=heads * rows * keys,
         ),
-        name="attend_bwd",
+        name="ab",
     )(q_nope, q_rope, keyvals, rope_keys, q_pos, k_pos, attended, grad, lse)
     return jnp.sum(dqn, axis=0), jnp.sum(dqr, axis=0), dkv, dkr
 
@@ -453,10 +454,7 @@
     all_routes = all_routes[:, :TOPK].astype(jnp.int32)
     tokens = sources * rows_dev
     piece = min(tokens, 4096)
-    if tokens > piece:
-        all_cot = lax.all_gather(own_cot, EVERY, axis=0, tiled=True)
-    else:
-        all_cot = ordered_gather(own_cot, EVERY)
+    all_cot = lax.all_gather(own_cot, EVERY, axis=0, tiled=True)
 
     small = jnp.concatenate([attn_gain, latent_gain, moe_gain, router_proj.reshape(-1)])
     cuts = [attn_gain.size, latent_gain.size, moe_gain.size, router_proj.size]
@@ -520,12 +518,7 @@
     scale_latent = lax.rsqrt(jnp.mean(latent * latent, axis=1, keepdims=True) + eps_norm)
     latent_normed = (latent * scale_latent * latent_gain).astype(jnp.bfloat16)
     key_rope = rotate(compressed[:, RANK:], own_cosine, own_sine).astype(jnp.bfloat16)
-    keys_all = lax.all_gather(
-        jnp.concatenate([latent_normed, key_rope], axis=1),
-        ("context", "experts"),
-        axis=0,
-        tiled=True,
-    )
+    keys_all = ordered_gather(jnp.concatenate([latent_normed, key_rope], axis=1), INNER)
     latent_all, rope_all = keys_all[:, :RANK], keys_all[:, RANK:]
 
     span_float = span_in.astype(jnp.float32)
@@ -549,8 +542,7 @@
     scale_two = lax.rsqrt(jnp.mean(hidden * hidden, axis=1, keepdims=True) + eps_norm)
     hidden_normed = (hidden * scale_two * moe_gain).astype(jnp.bfloat16)
 
-    gates = mm(hidden_normed, router_proj)
-    gates = jax.nn.sigmoid(gates)
+    gates = jax.nn.sigmoid(mm(hidden_normed, router_proj))
     picked = jnp.any(routes[0][:, :, None] == names[None, None, :], axis=1)
     chosen = jnp.where(picked, gates, 0.0)
     chosen_total = jnp.sum(chosen, axis=1, keepdims=True)
@@ -742,9 +734,8 @@
     def sum_heads(values):
         kept = lax.dynamic_slice_in_dim(values, near, width_dp, 0)
         sent = lax.dynamic_slice_in_dim(values, far, width_dp, 0)
-        kept = (kept + swap(sent.astype(jnp.bfloat16), "dp", 1).astype(jnp.float32)).astype(
-            jnp.bfloat16
-        )
+        got = swap(sent.astype(jnp.bfloat16), "dp", 1)
+        kept = (kept + got.astype(jnp.float32)).astype(jnp.bfloat16)
         return lax.psum_scatter(kept, "context", scatter_dimension=0, tiled=True)
 
     def full_heads(values):
@@ -764,19 +755,20 @@
         lse,
         score_scale,
     )
-    latent_outgoing = jnp.concatenate([mm(dkv, expand_proj, NT).astype(jnp.bfloat16), dkr], axis=1)
-    latent_part = ordered_scatter(latent_outgoing, ("context", "experts"), inner + along)
     dq_rope = rotate_back(dq_rope.transpose(1, 0, 2), cosine[:, None, :], sine[:, None, :])
     query_raw_grad = (
         jnp.concatenate([dq_nope.reshape(span_rows, heads, NOPE), dq_rope], axis=2)
         .reshape(span_rows, heads * (NOPE + ROPE))
         .astype(jnp.bfloat16)
     )
-    query_wide_grad = mm(normed, query_raw_grad, TN)
     head_grads = jnp.concatenate(
-        [query_wide_grad, mm(latent_all, dkv, TN).reshape(D, -1)], axis=1
-    )
+        [mm(normed, query_raw_grad, TN), mm(latent_all, dkv, TN).reshape(D, -1)], axis=1
+    )
+    head_grads, dkv, query_raw_grad = gate(head_grads, dkv, query_raw_grad)
     head_grads = sum_heads(head_grads)
+    latent_outgoing = mm(dkv, expand_proj, NT).astype(jnp.bfloat16)
+    latent_outgoing = jnp.concatenate([latent_outgoing, dkr], axis=1)
+    latent_part = ordered_scatter(latent_outgoing, INNER, inner + along)
     input_part = cube_scatter(mm(query_raw_grad, query_proj, NT), "experts")
 
     latent_grad, latent_gain_grad = rms_back(
@@ -785,10 +777,9 @@
     compressed_grad = jnp.concatenate(
         [latent_grad, rotate_back(latent_part[:, RANK:], own_cosine, own_sine)], axis=1
     ).astype(jnp.bfloat16)
-    latent_proj_grad = mm(own_normed, compressed_grad, TN)
-    latent_proj_grad = ordered_scatter(latent_proj_grad, EVERY, inner + along + across)
-    latent_proj_grad = ordered_gather(
-        latent_proj_grad.astype(jnp.bfloat16), ("context", "experts")
+    latent_proj_grad = mm(own_normed, compressed_grad, TN).astype(jnp.bfloat16)
+    latent_proj_grad = lax.all_gather(
+        scatter_every(latent_proj_grad), INNER, axis=0, tiled=True
     ).astype(jnp.float32)
     head_grads, output_proj_grad = full_heads(head_grads), full_heads(output_part).T
     query_wide = heads * (NOPE + ROPE)

time: 1440 us -> 1390 us (0.965)
  waiting for transfers between devices: 608 us -> 567 us
  other arithmetic: 188 us -> 149 us
    ppermute x64 -> x54, waiting for transfers between devices: 608 us -> 435 us  [swap(): return lax.ppermute(values, axis, [(i, i ^ mask) for i in range(count)])]
    all_gather x1, waiting for transfers between devices: 0.01 us -> 67.5 us  [layer(): lax.all_gather(jnp.concatenate([hidden_normed, weights_high, weights_low,...]
    all_gather x2, waiting for transfers between devices: 0.01 us -> 43.9 us  [full_heads(): lax.all_gather(values, 'context', axis=0, tiled=True).astype(jnp.float32)]
    select_n x24 -> x16, other arithmetic: 44.4 us -> 11.9 us  [ordered_gather(): jnp.where(bit_here(axis, mask) == 0, jnp.stack([values, got], axis=at), j...]
    all_gather x1 -> x2, waiting for transfers between devices: 0.01 us -> 19.6 us  [the longest x1 19.6 us: layer(): lax.all_gather(scatter_every(latent_proj_grad), INNER, axis=0, tiled=True)]
    unnamed x242 -> x230, local copies, waits for them, and re-layouts: 42.7 us -> 48.5 us
    ppermute x64 -> x54, starting transfers between devices: 130 us -> 128 us  [swap(): return lax.ppermute(values, axis, [(i, i ^ mask) for i in range(count)])]
  transfers between devices with their start and end apart: 71 -> 63, of which waited for: 36 -> 34; matrix products, arithmetic and copies ran while one was open for 31% -> 27% of each run, Pallas kernels for 3% -> 3%
where the time goes in v3:
time: 1390 us; the launch traced here: 1380 us
  waiting for transfers between devices  567 us (41%)
  matrix products  247 us (18%)
  local copies, waits for them, and re-layouts  175 us (13%)
  other arithmetic  149 us (11%)
  starting transfers between devices  129 us (9%)
  Pallas kernels  94.5 us (7%)
  between operations  16.1 us (1%)
    ppermute x54, waiting for transfers between devices, swap(): return lax.ppermute(values, axis, [(i, i ^ mask) for i in range(count)])  435 us
    dot_general x17, matrix products, mm(): lax.dot_general(left, right, dims, preferred_element_type=jnp.float32)  185 us
    ppermute x54, starting transfers between devices, swap(): return lax.ppermute(values, axis, [(i, i ^ mask) for i in range(count)])  128 us
    all_gather x1, waiting for transfers between devices, layer(): lax.all_gather(jnp.concatenate([hidden_normed, weights_high, weights_low,...  67.5 us
    dot_general x10, matrix products, mm(): return jnp.dot(left, right, preferred_element_type=jnp.float32)  56.3 us
    unnamed x230, local copies, waits for them, and re-layouts  48.5 us
    all_gather x2, waiting for transfers between devices, full_heads(): lax.all_gather(values, 'context', axis=0, tiled=True).astype(jnp.float32)  43.9 us
    pallas_call x1, Pallas kernels, attend_bwd(): pl.pallas_call(lambda *refs: attend_bwd_body(scale, *refs), grid=(chunks,...  28.1 us
  transfers between devices with their start and end apart: 63, of which 34 were waited for; matrix products, arithmetic and copies ran while one was open for 27% of the time, Pallas kernels for 3%

profile of v3, /device:TPU:0, one launch (start us, length us, event | category | flops | bytes accessed | tf_op | source)
XLA Modules:
  0.0 1377.5 jit_solution(12154606624120229865)
XLA Ops:
  49.4 12.5 collective-permute-done.5
  66.6 11.9 collective-permute-done.6
  97.2 21.9 %collective-permute-done.8 = bf16[2,2,128,576]{2,3,0,1:T(8,128)(2,1)S(1)} collective-permute-done((bf16[2,2,128,576]{2,3,0,1:T(8,128)(2,1)S(1)}, bf16[2,2,128,576]{2,3,0,1:T(8,128)(2,1)S(1)}, u32[]{:S(2)}, u32[]{:S(2)}) %collective-permute-start.8) | collective-permute-done | bytes 589856 | tf_op jit(solution)/shard_map/ppermute | solution.py:75
  121.5 28.6 %collective-permute-done.4 = bf16[1024,768]{1,0:T(8,128)(2,1)S(1)} collective-permute-done((bf16[1024,768]{1,0:T(8,128)(2,1)}, bf16[1024,768]{1,0:T(8,128)(2,1)S(1)}, u32[]{:S(2)}, u32[]{:S(2)}) %collective-permute-start.4) | collective-permute-done | bytes 1572896 | tf_op jit(solution)/shard_map/ppermute | solution.py:75
  186.2 6.5 convolution_convert_fusion.2.refs_2_
  192.8 27.4 %af.1 = (bf16[512,512]{1,0:T(8,128)(2,1)}, f32[4,512,1]{2,1,0:T(8,128)}) custom-call(bf16[512,512]{1,0:T(8,128)(2,1)} %copy.194.refs_0_, bf16[4,512,64]{2,1,0:T(8,128)(2,1)} %fusion.82.refs_1_, bf16[2048,1024]{1,0:T(8,128)(2,1)} %convolution_convert_fusion.2.refs_2_, bf16[2048,64]{1,0:T(8,128)(2,1)} %slice.262.refs_3_, s32[512,1]{1,0:T(8,128)} %fusion.93.refs_4_, ...), custom_call_target="tpu_custom_call" | custom-call | flops 2684354560 | bytes 8388608 | tf_op jit(solution)/shard_map/af/pallas_call | solution.py:268
  230.6 12.9 collective-permute-done.13
  261.5 10.3 collective-permute-done.16
  282.5 9.2 pick.2
  295.1 7.9 fusion.14
  303.0 67.5 %all-gather.7.cloned.1.call-done.refs_0_ = bf16[4096,2176]{1,0:T(8,128)(2,1)} async-done(((bf16[128,2176]{1,0:T(8,128)(2,1)}), bf16[4096,2176]{1,0:T(8,128)(2,1)}) %all-gather.7.cloned.1.call-update) | async-done | bytes 17825808 | tf_op jit(solution)/shard_map/all_gather | solution.py:553
  370.5 9.4 pick.3
  385.4 16.6 %fusion.148 = f32[2048,1408]{0,1:T(8,128)S(1)} fusion(bf16[2048,2048]{1,0:T(8,128)(2,1)} %copy-done.2, bf16[1408,2048]{1,0:T(8,128)(2,1)} %bitcast.300), kind=kOutput, calls=%fused_computation.371 | convolution fusion | flops 11811160064 | bytes 25690112 | tf_op jit(solution)/shard_map/dot_general | solution.py:66
  402.0 8.6 fusion.7
  416.9 17.2 %convolution_convert_fusion.1.refs_0_ = bf16[2048,2048]{1,0:T(8,128)(2,1)S(1)} fusion(bf16[1408,2048]{1,0:T(8,128)(2,1)} %bitcast.301, bf16[2048,704]{0,1:T(8,128)(2,1)} %get-tuple-element.181, bf16[2048,704]{0,1:T(8,128)(2,1)} %get-tuple-element.182), kind=kOutput, calls=%fused_computation.23 | convolution fusion | flops 11826888704 | bytes 19922944 | tf_op jit(solution)/shard_map/dot_general | solution.py:65
  435.8 9.4 place.2
  447.4 63.6 %collective-permute-done.19 = bf16[1408,1024]{1,0:T(8,128)(2,1)} collective-permute-done((bf16[1408,1024]{1,0:T(8,128)(2,1)}, bf16[1408,1024]{1,0:T(8,128)(2,1)}, u32[]{:S(2)}, u32[]{:S(2)}) %collective-permute-start.19) | collective-permute-done | bytes 2883616 | tf_op jit(solution)/shard_map/ppermute | solution.py:75
  511.1 34.3 %fusion.68 = f32[4096,1408]{0,1:T(8,128)} fusion(bf16[1408,1024]{1,0:T(8,128)(2,1)} %collective-permute-done.19, bf16[1408,1024]{1,0:T(8,128)(2,1)} %bitcast.303, pred[]{:T(512)S(6)} %eq.128, bf16[4096,2176]{1,0:T(8,128)(2,1)} %all-gather.7.cloned.1.call-done.refs_0_), kind=kOutput, calls=%fused_computation.183 | convolution fusion | flops 23648272384 | bytes 45613056 | tf_op jit(solution)/shard_map/dot_general | solution.py:66
  545.4 14.2 %slice.216 = bf16[4096,2048]{1,0:T(8,128)(2,1)} slice(bf16[4096,2176]{1,0:T(8,128)(2,1)} %all-gather.7.cloned.1.call-done.refs_0_), slice={[0:4096], [0:2048]} | slice | bytes 33554432 | tf_op jit(solution)/shard_map/slice | solution.py:652
  559.6 29.7 %multiply_convert_fusion = (bf16[4096,704]{0,1:T(8,128)(2,1)}, bf16[4096,704]{0,1:T(8,128)(2,1)}, bf16[4096,704]{0,1:T(8,128)(2,1)}) fusion(f32[4096,1408]{0,1:T(8,128)} %fusion.68, bf16[4096,2048]{1,0:T(8,128)(2,1)} %bitcast.246, bf16[704,1024]{1,0:T(8,128)(2,1)} %collective-permute-done.20, bf16[704,1024]{1,0:T(8,128)(2,1)} %param.29, pred[]{:T(512)S(6)} %eq.128), kind=kOutput, calls=%fused_computation.10 | convolution fusion | flops 11870273536 | bytes 60030976 | tf_op jit(solution)/shard_map/dot_general | solution.py:66
  596.5 7.2 convolution_convert_fusion.6
  606.6 19.1 %fusion = f32[1408,1024]{1,0:T(8,128)} fusion(bf16[4096,704]{0,1:T(8,128)(2,1)} %get-tuple-element.176, bf16[4096,704]{0,1:T(8,128)(2,1)} %get-tuple-element.177, bf16[4096,2048]{1,0:T(8,128)(2,1)} %slice.216, s32[]{:T(128)S(6)} %select_n.522), kind=kOutput, calls=%fused_computation.9 | convolution fusion | flops 11834228736 | bytes 25690116 | tf_op jit(solution)/shard_map/dot_general | solution.py:66
  625.8 19.5 %fusion.149 = f32[1408,2048]{1,0:T(8,128)} fusion(bf16[2048,1408]{0,1:T(8,128)(2,1)} %pad_maximum_fusion.3, bf16[2048,2048]{1,0:T(8,128)(2,1)} %copy-done.2), kind=kOutput, calls=%fused_computation.372 | convolution fusion | flops 11811160064 | bytes 25690112 | tf_op jit(solution)/shard_map/dot_general | solution.py:66
  645.3 10.3 fusion.150
  658.6 73.0 %collective-permute-start.22 = (bf16[128,4096]{1,0:T(8,128)(2,1)S(1)}, bf16[128,4096]{1,0:T(8,128)(2,1)S(1)}, u32[]{:S(2)}, u32[]{:S(2)}) collective-permute-start(bf16[128,4096]{1,0:T(8,128)(2,1)S(1)} %fusion.23), channel_id=1, source_target_pairs={{0,2},{1,3},{2,0},{3,1},{4,6},{5,7},{6,4},{7,5},{8,10},{9,11},{10,... | collective-permute-start | bytes 3145736 | tf_op jit(solution)/shard_map/ppermute | solution.py:75
  731.6 9.4 fusion.3
  741.0 14.4 %collective-permute-done.22 = bf16[128,4096]{1,0:T(8,128)(2,1)S(1)} collective-permute-done((bf16[128,4096]{1,0:T(8,128)(2,1)S(1)}, bf16[128,4096]{1,0:T(8,128)(2,1)S(1)}, u32[]{:S(2)}, u32[]{:S(2)}) %collective-permute-start.22) | collective-permute-done | bytes 1048608 | tf_op jit(solution)/shard_map/ppermute | solution.py:75
  771.5 9.2 convolution_convert_fusion.refs_0_
  780.7 10.9 place.3
  791.7 8.4 constant_dynamic-slice_fusion.3
  816.4 12.1 collective-permute-done.23
  831.8 7.1 fusion.1
  846.9 28.1 %ab.1 = (f32[1,512,512]{2,1,0:T(8,128)}, f32[1,4,512,64]{3,2,1,0:T(8,128)}, bf16[2048,1024]{1,0:T(8,128)(2,1)}, bf16[2048,64]{1,0:T(8,128)(2,1)}) custom-call(bf16[512,512]{1,0:T(8,128)(2,1)} %copy.194.refs_0_, bf16[4,512,64]{2,1,0:T(8,128)(2,1)} %fusion.82.refs_1_, bf16[2048,1024]{1,0:T(8,128)(2,1)} %convolution_convert_fusion.2.refs_2_, ...), custom_call_target="tpu_custom_call" | custom-call | flops 6979321856 | bytes 16777216 | tf_op jit(solution)/shard_map/ab/pallas_call | solution.py:368
  905.7 7.3 pad_maximum_fusion.2
  919.9 6.8 reshape.1073
  926.6 8.6 constant_dynamic-slice_fusion.1
  950.3 13.9 %collective-permute-done.38 = bf16[2,2,128,576]{2,3,0,1:T(8,128)(2,1)} collective-permute-done((bf16[2,2,128,576]{2,3,0,1:T(8,128)(2,1)}, bf16[2,2,128,576]{2,3,0,1:T(8,128)(2,1)}, u32[]{:S(2)}, u32[]{:S(2)}) %collective-permute-start.38) | collective-permute-done | bytes 589856 | tf_op jit(solution)/shard_map/ppermute | solution.py:75
  979.5 18.2 %collective-permute-done.40 = bf16[128,576]{0,1:T(8,128)(2,1)} collective-permute-done((bf16[128,576]{0,1:T(8,128)(2,1)}, bf16[128,576]{0,1:T(8,128)(2,1)}, u32[]{:S(2)}, u32[]{:S(2)}) %collective-permute-start.40) | collective-permute-done | bytes 147488 | tf_op jit(solution)/shard_map/ppermute | solution.py:75
  1010.2 45.5 %collective-permute-done.47 = bf16[1024,1024]{0,1:T(8,128)(2,1)S(1)} collective-permute-done((bf16[1024,1024]{0,1:T(8,128)(2,1)S(1)}, bf16[1024,1024]{0,1:T(8,128)(2,1)S(1)}, u32[]{:S(2)}, u32[]{:S(2)}) %collective-permute-start.47) | collective-permute-done | bytes 2097184 | tf_op jit(solution)/shard_map/ppermute | solution.py:75
  1087.1 51.0 %collective-permute-done.50 = f32[34816]{0:T(1024)S(1)} collective-permute-done((f32[34816]{0:T(1024)S(1)}, f32[34816]{0:T(1024)S(1)}, u32[]{:S(2)}, u32[]{:S(2)}) %collective-permute-start.50) | collective-permute-done | bytes 139296 | tf_op jit(solution)/shard_map/ppermute | solution.py:75
  1181.1 10.8 collective-permute-done.53
  1196.2 9.9 collective-permute-done.44
  1208.9 26.5 %collective-permute-done.32 = bf16[2,2,128,1024]{3,2,1,0:T(8,128)(2,1)} collective-permute-done((bf16[2,2,128,1024]{3,2,1,0:T(8,128)(2,1)}, bf16[2,2,128,1024]{3,2,1,0:T(8,128)(2,1)}, u32[]{:S(2)}, u32[]{:S(2)}) %collective-permute-start.32) | collective-permute-done | bytes 1048608 | tf_op jit(solution)/shard_map/ppermute | solution.py:75
  1243.7 9.6 collective-permute-done.33
  1256.0 11.7 collective-permute-done.29
  1271.7 11.4 collective-permute-done.30
  1290.1 19.6 %all-gather.11.cloned.1.call-done = bf16[1024,576]{1,0:T(8,128)(2,1)} async-done(((bf16[64,576]{1,0:T(8,128)(2,1)}), bf16[1024,576]{1,0:T(8,128)(2,1)}) %all-gather.11.cloned.1.call-update) | async-done | bytes 1179664 | tf_op jit(solution)/shard_map/all_gather | solution.py:781
  1312.4 43.9 %all-gather.9.cloned.1.call-done = bf16[1024,1024]{0,1:T(8,128)(2,1)} async-done(((bf16[256,1024]{0,1:T(8,128)(2,1)}), bf16[1024,1024]{0,1:T(8,128)(2,1)}) %all-gather.9.cloned.1.call-update) | async-done | bytes 2097168 | tf_op jit(solution)/shard_map/all_gather | solution.py:742
  (556 shorter events, 418.2 us)
Async XLA Ops:
  7.2 275.3 %all-gather.15.cloned.1.call-start = ((), (), s32[]{:S(2)}) async-start(), calls=%async_computation.12 | async-start | bytes 17301504 | tf_op jit(solution)/shard_map/all_gather | solution.py:457
  7.9 362.6 %all-gather.7.cloned.1.call-start = ((), (), s32[]{:S(2)}) async-start(), calls=%async_computation.4 | async-start | bytes 18382848 | tf_op jit(solution)/shard_map/all_gather | solution.py:553
  16.5 15.9 %collective-permute-start.2 = (bf16[18688]{0:T(1024)(128)(2,1)}, bf16[18688]{0:T(1024)(128)(2,1)}, u32[]{:S(2)}, u32[]{:S(2)}) collective-permute-start(bf16[18688]{0:T(1024)(128)(2,1)} %dynamic-update-slice.3), channel_id=1, source_target_pairs={{0,16},{16,0},{1,17},{17,1},{2,18},{18,2},{3,19},{19,3},{4,20},{20... | collective-permute-start | bytes 112136 | tf_op jit(solution)/shard_map/ppermute | solution.py:75
  19.5 27.7 %collective-permute-start = (bf16[128,2048]{1,0:T(8,128)(2,1)}, bf16[128,2048]{1,0:T(8,128)(2,1)}, u32[]{:S(2)}, u32[]{:S(2)}) collective-permute-start(bf16[128,2048]{1,0:T(8,128)(2,1)} %bitcast.240), channel_id=1, source_target_pairs={{0,2},{1,3},{2,0},{3,1},{4,6},{5,7},{6,4},{7,5},{8,10},{9,11},{10,... | collective-permute-start | bytes 1572872 | tf_op jit(solution)/shard_map/ppermute | solution.py:75
  46.7 15.2 %collective-permute-start.5 = (f32[128,576]{0,1:T(8,128)S(1)}, f32[128,576]{0,1:T(8,128)S(1)}, u32[]{:S(2)}, u32[]{:S(2)}) collective-permute-start(f32[128,576]{0,1:T(8,128)S(1)} %fusion.147), channel_id=1, source_target_pairs={{0,16},{16,0},{1,17},{17,1},{2,18},{18,2},{3,19},{19,3},{4,20},{20... | collective-permute-start | bytes 884744 | tf_op jit(solution)/shard_map/ppermute | solution.py:75
  49.4 44.6 %collective-permute-start.1 = (bf16[256,2048]{1,0:T(8,128)(2,1)}, bf16[256,2048]{1,0:T(8,128)(2,1)}, u32[]{:S(2)}, u32[]{:S(2)}) collective-permute-start(bf16[256,2048]{1,0:T(8,128)(2,1)} %pad_maximum_fusion.9), channel_id=1, source_target_pairs={{0,1},{1,0},{2,3},{3,2},{4,5},{5,4},{6,7},{7,6},{8,9},{9,8},{10,11... | collective-permute-start | bytes 3145736 | tf_op jit(solution)/shard_map/ppermute | solution.py:75
  63.3 15.2 %collective-permute-start.6 = (bf16[128,576]{0,1:T(8,128)(2,1)S(1)}, bf16[128,576]{0,1:T(8,128)(2,1)S(1)}, u32[]{:S(2)}, u32[]{:S(2)}) collective-permute-start(bf16[128,576]{0,1:T(8,128)(2,1)S(1)} %get-tuple-element.219), channel_id=1, source_target_pairs={{0,8},{4,12},{8,0},{12,4},{1,9},{5,13},{9,1},{13,5},{2,10},{6,14},... | collective-permute-start | bytes 442376 | tf_op jit(solution)/shard_map/ppermute | solution.py:75
  87.5 62.5 %collective-permute-start.4 = (bf16[1024,768]{1,0:T(8,128)(2,1)}, bf16[1024,768]{1,0:T(8,128)(2,1)S(1)}, u32[]{:S(2)}, u32[]{:S(2)}) collective-permute-start(bf16[1024,768]{1,0:T(8,128)(2,1)} %param.21), channel_id=1, source_target_pairs={{0,16},{16,0},{1,17},{17,1},{2,18},{18,2},{3,19},{19,3},{4,20},{20... | collective-permute-start | bytes 4718600 | tf_op jit(solution)/shard_map/ppermute | solution.py:75
  91.5 27.5 %collective-permute-start.8 = (bf16[2,2,128,576]{2,3,0,1:T(8,128)(2,1)S(1)}, bf16[2,2,128,576]{2,3,0,1:T(8,128)(2,1)S(1)}, u32[]{:S(2)}, u32[]{:S(2)}) collective-permute-start(bf16[2,2,128,576]{2,3,0,1:T(8,128)(2,1)S(1)} %maximum_select_fusion.14), channel_id=1, source_target_pairs={{0,2},{1,3},{2,0},{3,1},{4,6},{5,7},{6,4},{7,5},{8,10},{9,11},{10,... | collective-permute-start | bytes 1769480 | tf_op jit(solution)/shard_map/ppermute | solution.py:75
  120.3 55.4 %collective-permute-start.9 = (bf16[2,2,2,128,576]{3,4,0,1,2:T(8,128)(2,1)}, bf16[2,2,2,128,576]{3,4,0,1,2:T(8,128)(2,1)}, u32[]{:S(2)}, u32[]{:S(2)}) collective-permute-start(bf16[2,2,2,128,576]{3,4,0,1,2:T(8,128)(2,1)} %maximum_select_fusion.8), channel_id=1, source_target_pairs={{0,1},{1,0},{2,3},{3,2},{4,5},{5,4},{6,7},{7,6},{8,9},{9,8},{10,11... | collective-permute-start | bytes 3538952 | tf_op jit(solution)/shard_map/ppermute | solution.py:75
  150.1 17.8 %collective-permute-start.10 = (bf16[256,1024]{1,0:T(8,128)(2,1)}, bf16[256,1024]{1,0:T(8,128)(2,1)}, u32[]{:S(2)}, u32[]{:S(2)}) collective-permute-start(bf16[256,1024]{1,0:T(8,128)(2,1)} %param.24), channel_id=1, source_target_pairs={{0,16},{16,0},{1,17},{17,1},{2,18},{18,2},{3,19},{19,3},{4,20},{20... | collective-permute-start | bytes 1572872 | tf_op jit(solution)/shard_map/ppermute | solution.py:75
  167.9 52.2 %collective-permute-start.11 = (bf16[512,1024]{1,0:T(8,128)(2,1)}, bf16[512,1024]{1,0:T(8,128)(2,1)}, u32[]{:S(2)}, u32[]{:S(2)}) collective-permute-start(bf16[512,1024]{1,0:T(8,128)(2,1)} %param.25), channel_id=1, source_target_pairs={{0,16},{16,0},{1,17},{17,1},{2,18},{18,2},{3,19},{19,3},{4,20},{20... | collective-permute-start | bytes 3145736 | tf_op jit(solution)/shard_map/ppermute | solution.py:75
  229.2 14.3 %collective-permute-start.13 = (bf16[128,2048]{1,0:T(8,128)(2,1)}, bf16[128,2048]{1,0:T(8,128)(2,1)}, u32[]{:S(2)}, u32[]{:S(2)}) collective-permute-start(bf16[128,2048]{1,0:T(8,128)(2,1)} %fusion.58), channel_id=1, source_target_pairs={{0,2},{1,3},{2,0},{3,1},{4,6},{5,7},{6,4},{7,5},{8,10},{9,11},{10,... | collective-permute-start | bytes 1572872 | tf_op jit(solution)/shard_map/ppermute | solution.py:75
  248.9 508.2 %reduce-scatter.5.cloned.1.call-start = ((), (), s32[]{:S(2)}) async-start(), calls=%async_computation.5 | async-start | bytes 18382848 | tf_op jit(solution)/shard_map/reduce_scatter | solution.py:608
  445.3 639.1 %reduce-scatter.11.cloned.1.call-start = ((), (), s32[]{:S(2)}) async-start(), calls=%async_computation.10 | async-start | bytes 1310720 | tf_op jit(solution)/shard_map/reduce_scatter | solution.py:739
  445.3 65.7 %collective-permute-start.19 = (bf16[1408,1024]{1,0:T(8,128)(2,1)}, bf16[1408,1024]{1,0:T(8,128)(2,1)}, u32[]{:S(2)}, u32[]{:S(2)}) collective-permute-start(bf16[1408,1024]{1,0:T(8,128)(2,1)} %bitcast.302), channel_id=1, source_target_pairs={{0,16},{16,0},{1,17},{17,1},{2,18},{18,2},{3,19},{19,3},{4,20},{20... | collective-permute-start | bytes 8650760 | tf_op jit(solution)/shard_map/ppermute | solution.py:75
  446.8 112.8 %collective-permute-start.20 = (bf16[704,1024]{1,0:T(8,128)(2,1)}, bf16[704,1024]{1,0:T(8,128)(2,1)}, u32[]{:S(2)}, u32[]{:S(2)}) collective-permute-start(bf16[704,1024]{1,0:T(8,128)(2,1)} %param.29), channel_id=1, source_target_pairs={{0,16},{16,0},{1,17},{17,1},{2,18},{18,2},{3,19},{19,3},{4,20},{20... | collective-permute-start | bytes 4325384 | tf_op jit(solution)/shard_map/ppermute | solution.py:75
  606.6 48.9 %collective-permute-start.21 = (bf16[256,4096]{1,0:T(8,128)(2,1)}, bf16[256,4096]{1,0:T(8,128)(2,1)}, u32[]{:S(2)}, u32[]{:S(2)}) collective-permute-start(bf16[256,4096]{1,0:T(8,128)(2,1)} %pad_maximum_fusion.6), channel_id=1, source_target_pairs={{0,1},{1,0},{2,3},{3,2},{4,5},{5,4},{6,7},{7,6},{8,9},{9,8},{10,11... | collective-permute-start | bytes 6291464 | tf_op jit(solution)/shard_map/ppermute | solution.py:75
  658.6 96.8 %collective-permute-start.22 = (bf16[128,4096]{1,0:T(8,128)(2,1)S(1)}, bf16[128,4096]{1,0:T(8,128)(2,1)S(1)}, u32[]{:S(2)}, u32[]{:S(2)}) collective-permute-start(bf16[128,4096]{1,0:T(8,128)(2,1)S(1)} %fusion.23), channel_id=1, source_target_pairs={{0,2},{1,3},{2,0},{3,1},{4,6},{5,7},{6,4},{7,5},{8,10},{9,11},{10,... | collective-permute-start | bytes 3145736 | tf_op jit(solution)/shard_map/ppermute | solution.py:75
  804.8 26.9 %collective-permute-start.26 = (bf16[2,2,2,2,128,1024]{5,4,3,0,1,2:T(8,128)(2,1)}, bf16[2,2,2,2,128,1024]{5,4,3,0,1,2:T(8,128)(2,1)}, u32[]{:S(2)}, u32[]{:S(2)}) collective-permute-start(bf16[2,2,2,2,128,1024]{5,4,3,0,1,2:T(8,128)(2,1)} %bitcast.231), channel_id=1, source_target_pairs={{0,1},{1,0},{2,3},{3,2},{4,5},{5,4},{6,7},{7,6},{8,9},{9,8},{10,11... | collective-permute-start | bytes 12582920 | tf_op jit(solution)/shard_map/ppermute | solution.py:75
  814.2 24.7 %collective-permute-start.25 = (bf16[2,2,2,2,128,1024]{5,4,1,2,0,3:T(8,128)(2,1)}, bf16[2,2,2,2,128,1024]{5,4,1,2,0,3:T(8,128)(2,1)S(1)}, u32[]{:S(2)}, u32[]{:S(2)}) collective-permute-start(bf16[2,2,2,2,128,1024]{5,4,1,2,0,3:T(8,128)(2,1)} %bitcast.232), channel_id=1, source_target_pairs={{0,1},{1,0},{2,3},{3,2},{4,5},{5,4},{6,7},{7,6},{8,9},{9,8},{10,11... | collective-permute-start | bytes 12582920 | tf_op jit(solution)/shard_map/ppermute | solution.py:75
  943.2 25.8 %collective-permute-start.48 = (bf16[1024,512]{1,0:T(8,128)(2,1)}, bf16[1024,512]{1,0:T(8,128)(2,1)}, u32[]{:S(2)}, u32[]{:S(2)}) collective-permute-start(bf16[1024,512]{1,0:T(8,128)(2,1)} %dynamic-slice_convert_fusion.1), channel_id=1, source_target_pairs={{0,16},{16,0},{1,17},{17,1},{2,18},{18,2},{3,19},{19,3},{4,20},{20... | collective-permute-start | bytes 3145736 | tf_op jit(solution)/shard_map/ppermute | solution.py:75
  948.6 15.7 %collective-permute-start.38 = (bf16[2,2,128,576]{2,3,0,1:T(8,128)(2,1)}, bf16[2,2,128,576]{2,3,0,1:T(8,128)(2,1)}, u32[]{:S(2)}, u32[]{:S(2)}) collective-permute-start(bf16[2,2,128,576]{2,3,0,1:T(8,128)(2,1)} %fusion.80), channel_id=1, source_target_pairs={{0,2},{1,3},{2,0},{3,1},{4,6},{5,7},{6,4},{7,5},{8,10},{9,11},{10,... | collective-permute-start | bytes 1769480 | tf_op jit(solution)/shard_map/ppermute | solution.py:75
  972.2 179.9 %reduce-scatter.9.cloned.1.call-start = ((), (), s32[]{:S(2)}) async-start(), calls=%async_computation.8 | async-start | bytes 2703360 | tf_op jit(solution)/shard_map/reduce_scatter | solution.py:608
  978.9 18.8 %collective-permute-start.40 = (bf16[128,576]{0,1:T(8,128)(2,1)}, bf16[128,576]{0,1:T(8,128)(2,1)}, u32[]{:S(2)}, u32[]{:S(2)}) collective-permute-start(bf16[128,576]{0,1:T(8,128)(2,1)} %fusion.96), channel_id=1, source_target_pairs={{0,8},{4,12},{8,0},{12,4},{1,9},{5,13},{9,1},{13,5},{2,10},{6,14},... | collective-permute-start | bytes 442376 | tf_op jit(solution)/shard_map/ppermute | solution.py:75
  1006.6 234.1 %reduce-scatter.7.cloned.1.call-start = ((), (), s32[]{:S(2)}) async-start(), calls=%async_computation.6 | async-start | bytes 2621440 | tf_op jit(solution)/shard_map/reduce_scatter | solution.py:739
  1009.4 46.3 %collective-permute-start.47 = (bf16[1024,1024]{0,1:T(8,128)(2,1)S(1)}, bf16[1024,1024]{0,1:T(8,128)(2,1)S(1)}, u32[]{:S(2)}, u32[]{:S(2)}) collective-permute-start(bf16[1024,1024]{0,1:T(8,128)(2,1)S(1)} %dynamic-slice_convert_fusion), channel_id=1, source_target_pairs={{0,16},{16,0},{1,17},{17,1},{2,18},{18,2},{3,19},{19,3},{4,20},{20... | collective-permute-start | bytes 6291464 | tf_op jit(solution)/shard_map/ppermute | solution.py:75
  1060.2 224.2 %all-gather.13.cloned.1.call-start = ((), (), s32[]{:S(2)}) async-start(), calls=%async_computation.11 | async-start | bytes 1310720 | tf_op jit(solution)/shard_map/all_gather | solution.py:742
  1066.0 18.5 %collective-permute-start.49 = (f32[34816]{0:T(1024)}, f32[34816]{0:T(1024)}, u32[]{:S(2)}, u32[]{:S(2)}) collective-permute-start(f32[34816]{0:T(1024)} %pad_maximum_fusion.22), channel_id=1, source_target_pairs={{0,1},{1,0},{2,3},{3,2},{4,5},{5,4},{6,7},{7,6},{8,9},{9,8},{10,11... | collective-permute-start | bytes 417800 | tf_op jit(solution)/shard_map/ppermute | solution.py:75
  1069.1 83.4 %collective-permute-start.31 = (bf16[2,2,2,128,1024]{4,3,2,0,1:T(8,128)(2,1)}, bf16[2,2,2,128,1024]{4,3,2,0,1:T(8,128)(2,1)}, u32[]{:S(2)}, u32[]{:S(2)}) collective-permute-start(bf16[2,2,2,128,1024]{4,3,2,0,1:T(8,128)(2,1)} %dynamic-slice_bitcast_fusion), channel_id=1, source_target_pairs={{0,4},{4,0},{8,12},{12,8},{1,5},{5,1},{9,13},{13,9},{2,6},{6,2},{1... | collective-permute-start | bytes 6291464 | tf_op jit(solution)/shard_map/ppermute | solution.py:75
  1070.6 89.7 %collective-permute-start.27 = (bf16[2,2,2,128,1024]{4,3,1,2,0:T(8,128)(2,1)}, bf16[2,2,2,128,1024]{4,3,1,2,0:T(8,128)(2,1)}, u32[]{:S(2)}, u32[]{:S(2)}) collective-permute-start(bf16[2,2,2,128,1024]{4,3,1,2,0:T(8,128)(2,1)} %dynamic-slice_bitcast_fusion.1), channel_id=1, source_target_pairs={{0,2},{1,3},{2,0},{3,1},{4,6},{5,7},{6,4},{7,5},{8,10},{9,11},{10,... | collective-permute-start | bytes 6291464 | tf_op jit(solution)/shard_map/ppermute | solution.py:75
  1084.2 61.2 %collective-permute-start.35 = (bf16[256,2048]{1,0:T(8,128)(2,1)}, bf16[256,2048]{1,0:T(8,128)(2,1)}, u32[]{:S(2)}, u32[]{:S(2)}) collective-permute-start(bf16[256,2048]{1,0:T(8,128)(2,1)} %pad_maximum_fusion.12), channel_id=1, source_target_pairs={{0,1},{1,0},{2,3},{3,2},{4,5},{5,4},{6,7},{7,6},{8,9},{9,8},{10,11... | collective-permute-start | bytes 3145736 | tf_op jit(solution)/shard_map/ppermute | solution.py:75
  1084.5 225.3 %all-gather.11.cloned.1.call-start = ((), (), s32[]{:S(2)}) async-start(), calls=%async_computation.9 | async-start | bytes 1392640 | tf_op jit(solution)/shard_map/all_gather | solution.py:781
  1085.4 52.6 %collective-permute-start.50 = (f32[34816]{0:T(1024)S(1)}, f32[34816]{0:T(1024)S(1)}, u32[]{:S(2)}, u32[]{:S(2)}) collective-permute-start(f32[34816]{0:T(1024)S(1)} %fusion.132), channel_id=1, source_target_pairs={{0,2},{1,3},{2,0},{3,1},{4,6},{5,7},{6,4},{7,5},{8,10},{9,11},{10,... | collective-permute-start | bytes 417800 | tf_op jit(solution)/shard_map/ppermute | solution.py:75
  1138.9 29.2 %collective-permute-start.41 = (bf16[576,1024]{1,0:T(8,128)(2,1)}, bf16[576,1024]{1,0:T(8,128)(2,1)}, u32[]{:S(2)}, u32[]{:S(2)}) collective-permute-start(bf16[576,1024]{1,0:T(8,128)(2,1)} %bitcast.251), channel_id=1, source_target_pairs={{0,16},{16,0},{1,17},{17,1},{2,18},{18,2},{3,19},{19,3},{4,20},{20... | collective-permute-start | bytes 3538952 | tf_op jit(solution)/shard_map/ppermute | solution.py:75
  1144.7 28.4 %collective-permute-start.52 = (f32[34816]{0:T(1024)S(1)}, f32[34816]{0:T(1024)}, u32[]{:S(2)}, u32[]{:S(2)}) collective-permute-start(f32[34816]{0:T(1024)S(1)} %add.594), channel_id=1, source_target_pairs={{0,8},{4,12},{8,0},{12,4},{1,9},{5,13},{9,1},{13,5},{2,10},{6,14},... | collective-permute-start | bytes 417800 | tf_op jit(solution)/shard_map/ppermute | solution.py:75
  1150.3 17.8 %collective-permute-start.36 = (bf16[128,2048]{1,0:T(8,128)(2,1)}, bf16[128,2048]{1,0:T(8,128)(2,1)}, u32[]{:S(2)}, u32[]{:S(2)}) collective-permute-start(bf16[128,2048]{1,0:T(8,128)(2,1)} %fusion.55), channel_id=1, source_target_pairs={{0,2},{1,3},{2,0},{3,1},{4,6},{5,7},{6,4},{7,5},{8,10},{9,11},{10,... | collective-permute-start | bytes 1572872 | tf_op jit(solution)/shard_map/ppermute | solution.py:75
  1152.1 204.2 %all-gather.9.cloned.1.call-start = ((), (), s32[]{:S(2)}) async-start(), calls=%async_computation.7 | async-start | bytes 2621440 | tf_op jit(solution)/shard_map/all_gather | solution.py:742
  1157.4 78.1 %collective-permute-start.32 = (bf16[2,2,128,1024]{3,2,1,0:T(8,128)(2,1)}, bf16[2,2,128,1024]{3,2,1,0:T(8,128)(2,1)}, u32[]{:S(2)}, u32[]{:S(2)}) collective-permute-start(bf16[2,2,128,1024]{3,2,1,0:T(8,128)(2,1)} %dynamic-slice_bitcast_fusion.2), channel_id=1, source_target_pairs={{0,8},{4,12},{8,0},{12,4},{1,9},{5,13},{9,1},{13,5},{2,10},{6,14},... | collective-permute-start | bytes 3145736 | tf_op jit(solution)/shard_map/ppermute | solution.py:75
  1164.1 76.7 %collective-permute-start.28 = (bf16[2,2,128,1024]{3,2,0,1:T(8,128)(2,1)}, bf16[2,2,128,1024]{3,2,0,1:T(8,128)(2,1)}, u32[]{:S(2)}, u32[]{:S(2)}) collective-permute-start(bf16[2,2,128,1024]{3,2,0,1:T(8,128)(2,1)} %dynamic-slice_bitcast_fusion.3), channel_id=1, source_target_pairs={{0,16},{16,0},{1,17},{17,1},{2,18},{18,2},{3,19},{19,3},{4,20},{20... | collective-permute-start | bytes 3145736 | tf_op jit(solution)/shard_map/ppermute | solution.py:75
  1174.7 17.1 %collective-permute-start.53 = (f32[34816]{0:T(1024)}, f32[34816]{0:T(1024)S(1)}, u32[]{:S(2)}, u32[]{:S(2)}) collective-permute-start(f32[34816]{0:T(1024)} %add.595), channel_id=1, source_target_pairs={{0,16},{16,0},{1,17},{17,1},{2,18},{18,2},{3,19},{19,3},{4,20},{20... | collective-permute-start | bytes 417800 | tf_op jit(solution)/shard_map/ppermute | solution.py:75
  1179.9 26.3 %collective-permute-start.44 = (f32[2560]{0:T(1024)}, f32[2560]{0:T(1024)}, u32[]{:S(2)}, u32[]{:S(2)}) collective-permute-start(f32[2560]{0:T(1024)} %add.583), channel_id=1, source_target_pairs={{0,4},{4,0},{8,12},{12,8},{1,5},{5,1},{9,13},{13,9},{2,6},{6,2},{1... | collective-permute-start | bytes 30728 | tf_op jit(solution)/shard_map/ppermute | solution.py:75
  1206.9 36.1 %collective-permute-start.45 = (f32[2560]{0:T(1024)S(1)}, f32[2560]{0:T(1024)S(1)}, u32[]{:S(2)}, u32[]{:S(2)}) collective-permute-start(f32[2560]{0:T(1024)S(1)} %add.584), channel_id=1, source_target_pairs={{0,8},{4,12},{8,0},{12,4},{1,9},{5,13},{9,1},{13,5},{2,10},{6,14},... | collective-permute-start | bytes 30728 | tf_op jit(solution)/shard_map/ppermute | solution.py:75
  1239.3 14.0 %collective-permute-start.33 = (bf16[2,128,1024]{2,1,0:T(8,128)(2,1)}, bf16[2,128,1024]{2,1,0:T(8,128)(2,1)}, u32[]{:S(2)}, u32[]{:S(2)}) collective-permute-start(bf16[2,128,1024]{2,1,0:T(8,128)(2,1)} %dynamic-slice_bitcast_fusion.4), channel_id=1, source_target_pairs={{0,16},{16,0},{1,17},{17,1},{2,18},{18,2},{3,19},{19,3},{4,20},{20... | collective-permute-start | bytes 1572872 | tf_op jit(solution)/shard_map/ppermute | solution.py:75
  1242.9 24.8 %collective-permute-start.29 = (bf16[2,128,1024]{2,1,0:T(8,128)(2,1)S(1)}, bf16[2,128,1024]{2,1,0:T(8,128)(2,1)S(1)}, u32[]{:S(2)}, u32[]{:S(2)}) collective-permute-start(bf16[2,128,1024]{2,1,0:T(8,128)(2,1)S(1)} %dynamic-slice_bitcast_fusion.5), channel_id=1, source_target_pairs={{0,4},{4,0},{8,12},{12,8},{1,5},{5,1},{9,13},{13,9},{2,6},{6,2},{1... | collective-permute-start | bytes 1572872 | tf_op jit(solution)/shard_map/ppermute | solution.py:75
  1243.0 27.3 %collective-permute-start.46 = (f32[2560]{0:T(1024)S(1)}, f32[2560]{0:T(1024)S(1)}, u32[]{:S(2)}, u32[]{:S(2)}) collective-permute-start(f32[2560]{0:T(1024)S(1)} %add.585), channel_id=1, source_target_pairs={{0,16},{16,0},{1,17},{17,1},{2,18},{18,2},{3,19},{19,3},{4,20},{20... | collective-permute-start | bytes 30728 | tf_op jit(solution)/shard_map/ppermute | solution.py:75
  1254.6 17.0 %collective-permute-start.34 = (bf16[128,1024]{1,0:T(8,128)(2,1)S(1)}, bf16[128,1024]{1,0:T(8,128)(2,1)S(1)}, u32[]{:S(2)}, u32[]{:S(2)}) collective-permute-start(bf16[128,1024]{1,0:T(8,128)(2,1)S(1)} %dynamic-slice_bitcast_fusion.6), channel_id=1, source_target_pairs={{0,2},{1,3},{2,0},{3,1},{4,6},{5,7},{6,4},{7,5},{8,10},{9,11},{10,... | collective-permute-start | bytes 786440 | tf_op jit(solution)/shard_map/ppermute | solution.py:75
  1268.0 15.1 %collective-permute-start.30 = (bf16[128,1024]{1,0:T(8,128)(2,1)S(1)}, bf16[128,1024]{1,0:T(8,128)(2,1)S(1)}, u32[]{:S(2)}, u32[]{:S(2)}) collective-permute-start(bf16[128,1024]{1,0:T(8,128)(2,1)S(1)} %dynamic-slice_bitcast_fusion.7), channel_id=1, source_target_pairs={{0,8},{4,12},{8,0},{12,4},{1,9},{5,13},{9,1},{13,5},{2,10},{6,14},... | collective-permute-start | bytes 786440 | tf_op jit(solution)/shard_map/ppermute | solution.py:75
  (123 other events, 1963.2 us)
Sparse Core Ops, SparseCore 0:
  10.9 158.5 all-gather.14
  249.0 121.4 all-gather.6
  445.4 192.4 reduce-scatter.4
  972.3 31.4 reduce-scatter.10
  1006.7 142.1 reduce-scatter.8
  1151.0 70.7 reduce-scatter.6
  1223.4 42.0 all-gather.12
  1267.7 41.9 all-gather.10
  1311.3 45.0 all-gather.8

commit v4 on v3

--- a/solution.py
+++ b/solution.py
@@ -777,10 +777,11 @@
     compressed_grad = jnp.concatenate(
         [latent_grad, rotate_back(latent_part[:, RANK:], own_cosine, own_sine)], axis=1
     ).astype(jnp.bfloat16)
-    latent_proj_grad = mm(own_normed, compressed_grad, TN).astype(jnp.bfloat16)
-    latent_proj_grad = lax.all_gather(
-        scatter_every(latent_proj_grad), INNER, axis=0, tiled=True
-    ).astype(jnp.float32)
+    latent_proj_grad = mm(own_normed, compressed_grad, TN)
+    latent_proj_grad = ordered_scatter(latent_proj_grad, EVERY, inner + along + across)
+    latent_proj_grad = ordered_gather(latent_proj_grad.astype(jnp.bfloat16), INNER).astype(
+        jnp.float32
+    )
     head_grads, output_proj_grad = full_heads(head_grads), full_heads(output_part).T
     query_wide = heads * (NOPE + ROPE)
     query_proj_grad = head_grads[:, :query_wide]

time: 1390 us -> 1280 us (0.921)
  waiting for transfers between devices: 567 us -> 446 us
    ppermute x54 -> x63, waiting for transfers between devices: 435 us -> 379 us  [swap(): return lax.ppermute(values, axis, [(i, i ^ mask) for i in range(count)])]
    all_gather x2, waiting for transfers between devices: 43.9 us -> 0.01 us  [full_heads(): lax.all_gather(values, 'context', axis=0, tiled=True).astype(jnp.float32)]
    all_gather x1 -> x0, waiting for transfers between devices: 19.6 us -> none  [layer(): lax.all_gather(scatter_every(latent_proj_grad), INNER, axis=0, tiled=True)]
    ppermute x54 -> x63, starting transfers between devices: 128 us -> 133 us  [swap(): return lax.ppermute(values, axis, [(i, i ^ mask) for i in range(count)])]
    unnamed x230 -> x244, local copies, waits for them, and re-layouts: 48.5 us -> 48.4 us
  transfers between devices with their start and end apart: 63 -> 70, of which waited for: 34 -> 32; matrix products, arithmetic and copies ran while one was open for 27% -> 36% of each run, Pallas kernels for 3% -> 5%
where the time goes in v4:
time: 1280 us; the launch traced here: 1270 us
  waiting for transfers between devices  446 us (35%)
  matrix products  242 us (19%)
  local copies, waits for them, and re-layouts  183 us (14%)
  other arithmetic  151 us (12%)
  starting transfers between devices  134 us (10%)
  Pallas kernels  94.8 us (7%)
  between operations  16.3 us (1%)
    ppermute x63, waiting for transfers between devices, swap(): return lax.ppermute(values, axis, [(i, i ^ mask) for i in range(count)])  379 us
    dot_general x17, matrix products, mm(): lax.dot_general(left, right, dims, preferred_element_type=jnp.float32)  182 us
    ppermute x63, starting transfers between devices, swap(): return lax.ppermute(values, axis, [(i, i ^ mask) for i in range(count)])  133 us
    all_gather x1, waiting for transfers between devices, layer(): lax.all_gather(jnp.concatenate([hidden_normed, weights_high, weights_low,...  66.1 us
    dot_general x10, matrix products, mm(): return jnp.dot(left, right, preferred_element_type=jnp.float32)  54.7 us
    unnamed x244, local copies, waits for them, and re-layouts  48.4 us
    pallas_call x1, Pallas kernels, attend_bwd(): pl.pallas_call(lambda *refs: attend_bwd_body(scale, *refs), grid=(chunks,...  28 us
    pallas_call x1, Pallas kernels, attend_fwd(): pl.pallas_call(lambda *refs: attend_fwd_body(scale, *refs), grid=(heads,...  27.4 us
  transfers between devices with their start and end apart: 70, of which 32 were waited for; matrix products, arithmetic and copies ran while one was open for 36% of the time, Pallas kernels for 5%

profile of v4, /device:TPU:0, one launch (start us, length us, event | category | flops | bytes accessed | tf_op | source)
XLA Modules:
  0.0 1267.5 jit_solution(17228732549781288142)
XLA Ops:
  49.4 12.6 collective-permute-done.5
  66.7 12.5 collective-permute-done.6
  97.1 21.6 %collective-permute-done.8 = bf16[2,2,128,576]{2,3,0,1:T(8,128)(2,1)S(1)} collective-permute-done((bf16[2,2,128,576]{2,3,0,1:T(8,128)(2,1)S(1)}, bf16[2,2,128,576]{2,3,0,1:T(8,128)(2,1)S(1)}, u32[]{:S(2)}, u32[]{:S(2)}) %collective-permute-start.8) | collective-permute-done | bytes 589856 | tf_op jit(solution)/shard_map/ppermute | solution.py:75
  121.1 29.7 %collective-permute-done.4 = bf16[1024,768]{1,0:T(8,128)(2,1)S(1)} collective-permute-done((bf16[1024,768]{1,0:T(8,128)(2,1)}, bf16[1024,768]{1,0:T(8,128)(2,1)S(1)}, u32[]{:S(2)}, u32[]{:S(2)}) %collective-permute-start.4) | collective-permute-done | bytes 1572896 | tf_op jit(solution)/shard_map/ppermute | solution.py:75
  187.0 6.5 convolution_convert_fusion.2.refs_2_
  193.5 27.4 %af.1 = (bf16[512,512]{1,0:T(8,128)(2,1)}, f32[4,512,1]{2,1,0:T(8,128)}) custom-call(bf16[512,512]{1,0:T(8,128)(2,1)} %copy.200.refs_0_, bf16[4,512,64]{2,1,0:T(8,128)(2,1)} %fusion.85.refs_1_, bf16[2048,1024]{1,0:T(8,128)(2,1)} %convolution_convert_fusion.2.refs_2_, bf16[2048,64]{1,0:T(8,128)(2,1)} %slice.262.refs_3_, s32[512,1]{1,0:T(8,128)} %fusion.97.refs_4_, ...), custom_call_target="tpu_custom_call" | custom-call | flops 2684354560 | bytes 8388608 | tf_op jit(solution)/shard_map/af/pallas_call | solution.py:268
  231.3 12.9 %collective-permute-done.13 = bf16[128,2048]{1,0:T(8,128)(2,1)} collective-permute-done((bf16[128,2048]{1,0:T(8,128)(2,1)}, bf16[128,2048]{1,0:T(8,128)(2,1)}, u32[]{:S(2)}, u32[]{:S(2)}) %collective-permute-start.13) | collective-permute-done | bytes 524320 | tf_op jit(solution)/shard_map/ppermute | solution.py:75
  261.8 9.4 collective-permute-done.16
  271.4 6.3 collective-permute-done.17
  283.9 9.3 pick.2
  296.5 7.9 fusion.14
  304.4 66.1 %all-gather.6.cloned.1.call-done.refs_0_ = bf16[4096,2176]{1,0:T(8,128)(2,1)} async-done(((bf16[128,2176]{1,0:T(8,128)(2,1)}), bf16[4096,2176]{1,0:T(8,128)(2,1)}) %all-gather.6.cloned.1.call-update) | async-done | bytes 17825808 | tf_op jit(solution)/shard_map/all_gather | solution.py:553
  370.5 9.4 pick.3
  385.4 16.6 %fusion.157 = f32[2048,1408]{0,1:T(8,128)S(1)} fusion(bf16[2048,2048]{1,0:T(8,128)(2,1)} %copy-done.2, bf16[1408,2048]{1,0:T(8,128)(2,1)} %bitcast.361), kind=kOutput, calls=%fused_computation.396 | convolution fusion | flops 11811160064 | bytes 25690112 | tf_op jit(solution)/shard_map/dot_general | solution.py:66
  402.0 8.6 fusion.7
  410.6 6.3 pad_maximum_fusion.3
  416.9 17.2 %convolution_convert_fusion.1.refs_0_ = bf16[2048,2048]{1,0:T(8,128)(2,1)S(1)} fusion(bf16[1408,2048]{1,0:T(8,128)(2,1)} %bitcast.362, bf16[2048,704]{0,1:T(8,128)(2,1)} %get-tuple-element.181, bf16[2048,704]{0,1:T(8,128)(2,1)} %get-tuple-element.182), kind=kOutput, calls=%fused_computation.23 | convolution fusion | flops 11826888704 | bytes 19922944 | tf_op jit(solution)/shard_map/dot_general | solution.py:65
  435.9 9.4 place.2
  447.4 63.6 %collective-permute-done.19 = bf16[1408,1024]{1,0:T(8,128)(2,1)} collective-permute-done((bf16[1408,1024]{1,0:T(8,128)(2,1)}, bf16[1408,1024]{1,0:T(8,128)(2,1)}, u32[]{:S(2)}, u32[]{:S(2)}) %collective-permute-start.19) | collective-permute-done | bytes 2883616 | tf_op jit(solution)/shard_map/ppermute | solution.py:75
  511.1 34.3 %fusion.70 = f32[4096,1408]{0,1:T(8,128)} fusion(bf16[1408,1024]{1,0:T(8,128)(2,1)} %collective-permute-done.19, bf16[1408,1024]{1,0:T(8,128)(2,1)} %bitcast.364, pred[]{:T(512)S(6)} %eq.141, bf16[4096,2176]{1,0:T(8,128)(2,1)} %all-gather.6.cloned.1.call-done.refs_0_), kind=kOutput, calls=%fused_computation.189 | convolution fusion | flops 23648272384 | bytes 45613056 | tf_op jit(solution)/shard_map/dot_general | solution.py:66
  545.4 14.2 %slice.216 = bf16[4096,2048]{1,0:T(8,128)(2,1)} slice(bf16[4096,2176]{1,0:T(8,128)(2,1)} %all-gather.6.cloned.1.call-done.refs_0_), slice={[0:4096], [0:2048]} | slice | bytes 33554432 | tf_op jit(solution)/shard_map/slice | solution.py:652
  559.6 29.9 %multiply_convert_fusion = (bf16[4096,704]{0,1:T(8,128)(2,1)}, bf16[4096,704]{0,1:T(8,128)(2,1)}, bf16[4096,704]{0,1:T(8,128)(2,1)}) fusion(f32[4096,1408]{0,1:T(8,128)} %fusion.70, bf16[4096,2048]{1,0:T(8,128)(2,1)} %bitcast.294, bf16[704,1024]{1,0:T(8,128)(2,1)} %collective-permute-done.20, bf16[704,1024]{1,0:T(8,128)(2,1)} %param.29, pred[]{:T(512)S(6)} %eq.141), kind=kOutput, calls=%fused_computation.10 | convolution fusion | flops 11870273536 | bytes 60030976 | tf_op jit(solution)/shard_map/dot_general | solution.py:66
  596.6 7.3 convolution_convert_fusion.5
  606.8 19.1 %fusion = f32[1408,1024]{1,0:T(8,128)} fusion(bf16[4096,704]{0,1:T(8,128)(2,1)} %get-tuple-element.176, bf16[4096,704]{0,1:T(8,128)(2,1)} %get-tuple-element.177, bf16[4096,2048]{1,0:T(8,128)(2,1)} %slice.216, s32[]{:T(128)S(6)} %select_n.649), kind=kOutput, calls=%fused_computation.9 | convolution fusion | flops 11834228736 | bytes 25690116 | tf_op jit(solution)/shard_map/dot_general | solution.py:66
  625.9 19.2 %fusion.158 = f32[1408,2048]{1,0:T(8,128)} fusion(bf16[2048,1408]{0,1:T(8,128)(2,1)} %pad_maximum_fusion.3, bf16[2048,2048]{1,0:T(8,128)(2,1)} %copy-done.2), kind=kOutput, calls=%fused_computation.397 | convolution fusion | flops 11811160064 | bytes 25690112 | tf_op jit(solution)/shard_map/dot_general | solution.py:66
  645.1 10.3 fusion.159
  658.4 72.3 %collective-permute-start.22 = (bf16[128,4096]{1,0:T(8,128)(2,1)S(1)}, bf16[128,4096]{1,0:T(8,128)(2,1)S(1)}, u32[]{:S(2)}, u32[]{:S(2)}) collective-permute-start(bf16[128,4096]{1,0:T(8,128)(2,1)S(1)} %fusion.23), channel_id=1, source_target_pairs={{0,2},{1,3},{2,0},{3,1},{4,6},{5,7},{6,4},{7,5},{8,10},{9,11},{10,... | collective-permute-start | bytes 3145736 | tf_op jit(solution)/shard_map/ppermute | solution.py:75
  730.7 9.4 fusion.3
  740.1 14.4 %collective-permute-done.22 = bf16[128,4096]{1,0:T(8,128)(2,1)S(1)} collective-permute-done((bf16[128,4096]{1,0:T(8,128)(2,1)S(1)}, bf16[128,4096]{1,0:T(8,128)(2,1)S(1)}, u32[]{:S(2)}, u32[]{:S(2)}) %collective-permute-start.22) | collective-permute-done | bytes 1048608 | tf_op jit(solution)/shard_map/ppermute | solution.py:75
  771.0 9.0 convolution_convert_fusion.refs_0_
  780.0 11.3 place.3
  791.3 8.4 constant_dynamic-slice_fusion.3
  820.5 11.3 collective-permute-done.23
  859.2 6.4 fusion.1
  865.7 6.4 fusion.2
  879.1 28.0 %ab.1 = (f32[1,512,512]{2,1,0:T(8,128)}, f32[1,4,512,64]{3,2,1,0:T(8,128)}, bf16[2048,1024]{1,0:T(8,128)(2,1)}, bf16[2048,64]{1,0:T(8,128)(2,1)}) custom-call(bf16[512,512]{1,0:T(8,128)(2,1)} %copy.200.refs_0_, bf16[4,512,64]{2,1,0:T(8,128)(2,1)} %fusion.85.refs_1_, bf16[2048,1024]{1,0:T(8,128)(2,1)} %convolution_convert_fusion.2.refs_2_, ...), custom_call_target="tpu_custom_call" | custom-call | flops 6979321856 | bytes 16777216 | tf_op jit(solution)/shard_map/ab/pallas_call | solution.py:368
  907.1 6.5 fusion.28
  941.8 7.3 pad_maximum_fusion.2
  956.0 6.8 reshape.1380
  1038.8 25.5 %collective-permute-done.36 = bf16[128,2048]{1,0:T(8,128)(2,1)} collective-permute-done((bf16[128,2048]{1,0:T(8,128)(2,1)}, bf16[128,2048]{1,0:T(8,128)(2,1)}, u32[]{:S(2)}, u32[]{:S(2)}) %collective-permute-start.36) | collective-permute-done | bytes 524320 | tf_op jit(solution)/shard_map/ppermute | solution.py:75
  1077.3 16.5 %collective-permute-done.44 = f32[2560]{0:T(1024)S(1)} collective-permute-done((f32[2560]{0:T(1024)S(1)}, f32[2560]{0:T(1024)S(1)}, u32[]{:S(2)}, u32[]{:S(2)}) %collective-permute-start.44) | collective-permute-done | bytes 10272 | tf_op jit(solution)/shard_map/ppermute | solution.py:75
  1096.9 20.7 %collective-permute-done.45 = f32[2560]{0:T(1024)S(1)} collective-permute-done((f32[2560]{0:T(1024)S(1)}, f32[2560]{0:T(1024)S(1)}, u32[]{:S(2)}, u32[]{:S(2)}) %collective-permute-start.45) | collective-permute-done | bytes 10272 | tf_op jit(solution)/shard_map/ppermute | solution.py:75
  1126.9 10.2 collective-permute-done.49
  1144.3 15.2 %collective-permute-done.50 = bf16[2,2,64,576]{3,2,1,0:T(8,128)(2,1)S(1)} collective-permute-done((bf16[2,2,64,576]{3,2,1,0:T(8,128)(2,1)S(1)}, bf16[2,2,64,576]{3,2,1,0:T(8,128)(2,1)S(1)}, u32[]{:S(2)}, u32[]{:S(2)}) %collective-permute-start.50) | collective-permute-done | bytes 294944 | tf_op jit(solution)/shard_map/ppermute | solution.py:75
  1163.6 8.7 collective-permute-done.51
  1183.1 16.5 %collective-permute-done.53 = bf16[64,576]{1,0:T(8,128)(2,1)S(1)} collective-permute-done((bf16[64,576]{1,0:T(8,128)(2,1)S(1)}, bf16[64,576]{1,0:T(8,128)(2,1)S(1)}, u32[]{:S(2)}, u32[]{:S(2)}) %collective-permute-start.53) | collective-permute-done | bytes 73760 | tf_op jit(solution)/shard_map/ppermute | solution.py:75
  1200.8 21.3 %collective-permute-done.54 = bf16[2,64,576]{2,1,0:T(8,128)(2,1)S(1)} collective-permute-done((bf16[2,64,576]{2,1,0:T(8,128)(2,1)S(1)}, bf16[2,64,576]{2,1,0:T(8,128)(2,1)S(1)}, u32[]{:S(2)}, u32[]{:S(2)}) %collective-permute-start.54) | collective-permute-done | bytes 147488 | tf_op jit(solution)/shard_map/ppermute | solution.py:75
  1224.2 7.4 collective-permute-done.55
  (605 shorter events, 424.2 us)
Async XLA Ops:
  7.2 276.7 %all-gather.12.cloned.1.call-start = ((), (), s32[]{:S(2)}) async-start(), calls=%async_computation.9 | async-start | bytes 17301504 | tf_op jit(solution)/shard_map/all_gather | solution.py:457
  7.9 362.6 %all-gather.6.cloned.1.call-start = ((), (), s32[]{:S(2)}) async-start(), calls=%async_computation.3 | async-start | bytes 18382848 | tf_op jit(solution)/shard_map/all_gather | solution.py:553
  16.5 16.0 %collective-permute-start.2 = (bf16[18688]{0:T(1024)(128)(2,1)}, bf16[18688]{0:T(1024)(128)(2,1)}, u32[]{:S(2)}, u32[]{:S(2)}) collective-permute-start(bf16[18688]{0:T(1024)(128)(2,1)} %dynamic-update-slice.3), channel_id=1, source_target_pairs={{0,16},{16,0},{1,17},{17,1},{2,18},{18,2},{3,19},{19,3},{4,20},{20... | collective-permute-start | bytes 112136 | tf_op jit(solution)/shard_map/ppermute | solution.py:75
  19.5 27.8 %collective-permute-start = (bf16[128,2048]{1,0:T(8,128)(2,1)}, bf16[128,2048]{1,0:T(8,128)(2,1)}, u32[]{:S(2)}, u32[]{:S(2)}) collective-permute-start(bf16[128,2048]{1,0:T(8,128)(2,1)} %bitcast.286), channel_id=1, source_target_pairs={{0,2},{1,3},{2,0},{3,1},{4,6},{5,7},{6,4},{7,5},{8,10},{9,11},{10,... | collective-permute-start | bytes 1572872 | tf_op jit(solution)/shard_map/ppermute | solution.py:75
  46.7 15.2 %collective-permute-start.5 = (f32[128,576]{0,1:T(8,128)S(1)}, f32[128,576]{0,1:T(8,128)S(1)}, u32[]{:S(2)}, u32[]{:S(2)}) collective-permute-start(f32[128,576]{0,1:T(8,128)S(1)} %fusion.156), channel_id=1, source_target_pairs={{0,16},{16,0},{1,17},{17,1},{2,18},{18,2},{3,19},{19,3},{4,20},{20... | collective-permute-start | bytes 884744 | tf_op jit(solution)/shard_map/ppermute | solution.py:75
  49.4 44.5 %collective-permute-start.1 = (bf16[256,2048]{1,0:T(8,128)(2,1)}, bf16[256,2048]{1,0:T(8,128)(2,1)}, u32[]{:S(2)}, u32[]{:S(2)}) collective-permute-start(bf16[256,2048]{1,0:T(8,128)(2,1)} %pad_maximum_fusion.9), channel_id=1, source_target_pairs={{0,1},{1,0},{2,3},{3,2},{4,5},{5,4},{6,7},{7,6},{8,9},{9,8},{10,11... | collective-permute-start | bytes 3145736 | tf_op jit(solution)/shard_map/ppermute | solution.py:75
  63.4 15.8 %collective-permute-start.6 = (bf16[128,576]{0,1:T(8,128)(2,1)S(1)}, bf16[128,576]{0,1:T(8,128)(2,1)S(1)}, u32[]{:S(2)}, u32[]{:S(2)}) collective-permute-start(bf16[128,576]{0,1:T(8,128)(2,1)S(1)} %get-tuple-element.219), channel_id=1, source_target_pairs={{0,8},{4,12},{8,0},{12,4},{1,9},{5,13},{9,1},{13,5},{2,10},{6,14},... | collective-permute-start | bytes 442376 | tf_op jit(solution)/shard_map/ppermute | solution.py:75
  87.5 63.3 %collective-permute-start.4 = (bf16[1024,768]{1,0:T(8,128)(2,1)}, bf16[1024,768]{1,0:T(8,128)(2,1)S(1)}, u32[]{:S(2)}, u32[]{:S(2)}) collective-permute-start(bf16[1024,768]{1,0:T(8,128)(2,1)} %param.21), channel_id=1, source_target_pairs={{0,16},{16,0},{1,17},{17,1},{2,18},{18,2},{3,19},{19,3},{4,20},{20... | collective-permute-start | bytes 4718600 | tf_op jit(solution)/shard_map/ppermute | solution.py:75
  91.5 27.3 %collective-permute-start.8 = (bf16[2,2,128,576]{2,3,0,1:T(8,128)(2,1)S(1)}, bf16[2,2,128,576]{2,3,0,1:T(8,128)(2,1)S(1)}, u32[]{:S(2)}, u32[]{:S(2)}) collective-permute-start(bf16[2,2,128,576]{2,3,0,1:T(8,128)(2,1)S(1)} %maximum_select_fusion.17), channel_id=1, source_target_pairs={{0,2},{1,3},{2,0},{3,1},{4,6},{5,7},{6,4},{7,5},{8,10},{9,11},{10,... | collective-permute-start | bytes 1769480 | tf_op jit(solution)/shard_map/ppermute | solution.py:75
  119.9 56.3 %collective-permute-start.9 = (bf16[2,2,2,128,576]{3,4,0,1,2:T(8,128)(2,1)}, bf16[2,2,2,128,576]{3,4,0,1,2:T(8,128)(2,1)}, u32[]{:S(2)}, u32[]{:S(2)}) collective-permute-start(bf16[2,2,2,128,576]{3,4,0,1,2:T(8,128)(2,1)} %maximum_select_fusion.9), channel_id=1, source_target_pairs={{0,1},{1,0},{2,3},{3,2},{4,5},{5,4},{6,7},{7,6},{8,9},{9,8},{10,11... | collective-permute-start | bytes 3538952 | tf_op jit(solution)/shard_map/ppermute | solution.py:75
  150.8 17.1 %collective-permute-start.10 = (bf16[256,1024]{1,0:T(8,128)(2,1)}, bf16[256,1024]{1,0:T(8,128)(2,1)}, u32[]{:S(2)}, u32[]{:S(2)}) collective-permute-start(bf16[256,1024]{1,0:T(8,128)(2,1)} %param.24), channel_id=1, source_target_pairs={{0,16},{16,0},{1,17},{17,1},{2,18},{18,2},{3,19},{19,3},{4,20},{20... | collective-permute-start | bytes 1572872 | tf_op jit(solution)/shard_map/ppermute | solution.py:75
  167.9 53.0 %collective-permute-start.11 = (bf16[512,1024]{1,0:T(8,128)(2,1)}, bf16[512,1024]{1,0:T(8,128)(2,1)}, u32[]{:S(2)}, u32[]{:S(2)}) collective-permute-start(bf16[512,1024]{1,0:T(8,128)(2,1)} %param.25), channel_id=1, source_target_pairs={{0,16},{16,0},{1,17},{17,1},{2,18},{18,2},{3,19},{19,3},{4,20},{20... | collective-permute-start | bytes 3145736 | tf_op jit(solution)/shard_map/ppermute | solution.py:75
  229.9 14.3 %collective-permute-start.13 = (bf16[128,2048]{1,0:T(8,128)(2,1)}, bf16[128,2048]{1,0:T(8,128)(2,1)}, u32[]{:S(2)}, u32[]{:S(2)}) collective-permute-start(bf16[128,2048]{1,0:T(8,128)(2,1)} %fusion.60), channel_id=1, source_target_pairs={{0,2},{1,3},{2,0},{3,1},{4,6},{5,7},{6,4},{7,5},{8,10},{9,11},{10,... | collective-permute-start | bytes 1572872 | tf_op jit(solution)/shard_map/ppermute | solution.py:75
  249.6 506.6 %reduce-scatter.4.cloned.1.call-start = ((), (), s32[]{:S(2)}) async-start(), calls=%async_computation.4 | async-start | bytes 18382848 | tf_op jit(solution)/shard_map/reduce_scatter | solution.py:608
  445.3 681.3 %reduce-scatter.8.cloned.1.call-start = ((), (), s32[]{:S(2)}) async-start(), calls=%async_computation.7 | async-start | bytes 1310720 | tf_op jit(solution)/shard_map/reduce_scatter | solution.py:739
  445.3 65.7 %collective-permute-start.19 = (bf16[1408,1024]{1,0:T(8,128)(2,1)}, bf16[1408,1024]{1,0:T(8,128)(2,1)}, u32[]{:S(2)}, u32[]{:S(2)}) collective-permute-start(bf16[1408,1024]{1,0:T(8,128)(2,1)} %bitcast.363), channel_id=1, source_target_pairs={{0,16},{16,0},{1,17},{17,1},{2,18},{18,2},{3,19},{19,3},{4,20},{20... | collective-permute-start | bytes 8650760 | tf_op jit(solution)/shard_map/ppermute | solution.py:75
  446.8 112.8 %collective-permute-start.20 = (bf16[704,1024]{1,0:T(8,128)(2,1)}, bf16[704,1024]{1,0:T(8,128)(2,1)}, u32[]{:S(2)}, u32[]{:S(2)}) collective-permute-start(bf16[704,1024]{1,0:T(8,128)(2,1)} %param.29), channel_id=1, source_target_pairs={{0,16},{16,0},{1,17},{17,1},{2,18},{18,2},{3,19},{19,3},{4,20},{20... | collective-permute-start | bytes 4325384 | tf_op jit(solution)/shard_map/ppermute | solution.py:75
  606.8 48.6 %collective-permute-start.21 = (bf16[256,4096]{1,0:T(8,128)(2,1)}, bf16[256,4096]{1,0:T(8,128)(2,1)}, u32[]{:S(2)}, u32[]{:S(2)}) collective-permute-start(bf16[256,4096]{1,0:T(8,128)(2,1)} %pad_maximum_fusion.6), channel_id=1, source_target_pairs={{0,1},{1,0},{2,3},{3,2},{4,5},{5,4},{6,7},{7,6},{8,9},{9,8},{10,11... | collective-permute-start | bytes 6291464 | tf_op jit(solution)/shard_map/ppermute | solution.py:75
  658.4 96.1 %collective-permute-start.22 = (bf16[128,4096]{1,0:T(8,128)(2,1)S(1)}, bf16[128,4096]{1,0:T(8,128)(2,1)S(1)}, u32[]{:S(2)}, u32[]{:S(2)}) collective-permute-start(bf16[128,4096]{1,0:T(8,128)(2,1)S(1)} %fusion.23), channel_id=1, source_target_pairs={{0,2},{1,3},{2,0},{3,1},{4,6},{5,7},{6,4},{7,5},{8,10},{9,11},{10,... | collective-permute-start | bytes 3145736 | tf_op jit(solution)/shard_map/ppermute | solution.py:75
  804.6 54.7 %collective-permute-start.26 = (bf16[2,2,2,2,128,1024]{5,4,3,0,1,2:T(8,128)(2,1)}, bf16[2,2,2,2,128,1024]{5,4,3,0,1,2:T(8,128)(2,1)}, u32[]{:S(2)}, u32[]{:S(2)}) collective-permute-start(bf16[2,2,2,2,128,1024]{5,4,3,0,1,2:T(8,128)(2,1)} %bitcast.277), channel_id=1, source_target_pairs={{0,1},{1,0},{2,3},{3,2},{4,5},{5,4},{6,7},{7,6},{8,9},{9,8},{10,11... | collective-permute-start | bytes 12582920 | tf_op jit(solution)/shard_map/ppermute | solution.py:75
  814.2 51.5 %collective-permute-start.25 = (bf16[2,2,2,2,128,1024]{5,4,1,2,0,3:T(8,128)(2,1)}, bf16[2,2,2,2,128,1024]{5,4,1,2,0,3:T(8,128)(2,1)}, u32[]{:S(2)}, u32[]{:S(2)}) collective-permute-start(bf16[2,2,2,2,128,1024]{5,4,1,2,0,3:T(8,128)(2,1)} %bitcast.278), channel_id=1, source_target_pairs={{0,1},{1,0},{2,3},{3,2},{4,5},{5,4},{6,7},{7,6},{8,9},{9,8},{10,11... | collective-permute-start | bytes 12582920 | tf_op jit(solution)/shard_map/ppermute | solution.py:75
  817.9 13.9 %collective-permute-start.23 = (bf16[128,2048]{1,0:T(8,128)(2,1)S(1)}, bf16[128,2048]{1,0:T(8,128)(2,1)S(1)}, u32[]{:S(2)}, u32[]{:S(2)}) collective-permute-start(bf16[128,2048]{1,0:T(8,128)(2,1)S(1)} %copy-done.33), channel_id=1, source_target_pairs={{0,2},{1,3},{2,0},{3,1},{4,6},{5,7},{6,4},{7,5},{8,10},{9,11},{10,... | collective-permute-start | bytes 1572872 | tf_op jit(solution)/shard_map/ppermute | solution.py:75
  833.6 23.1 %collective-permute-start.24 = (bf16[256,2048]{1,0:T(8,128)(2,1)}, bf16[256,2048]{1,0:T(8,128)(2,1)}, u32[]{:S(2)}, u32[]{:S(2)}) collective-permute-start(bf16[256,2048]{1,0:T(8,128)(2,1)} %pad_maximum_fusion.11), channel_id=1, source_target_pairs={{0,1},{1,0},{2,3},{3,2},{4,5},{5,4},{6,7},{7,6},{8,9},{9,8},{10,11... | collective-permute-start | bytes 3145736 | tf_op jit(solution)/shard_map/ppermute | solution.py:75
  855.3 141.9 %collective-permute-start.62 = (f32[34816]{0:T(1024)S(1)}, f32[34816]{0:T(1024)}, u32[]{:S(2)}, u32[]{:S(2)}) collective-permute-start(f32[34816]{0:T(1024)S(1)} %add.637), channel_id=1, source_target_pairs={{0,16},{16,0},{1,17},{17,1},{2,18},{18,2},{3,19},{19,3},{4,20},{20... | collective-permute-start | bytes 417800 | tf_op jit(solution)/shard_map/ppermute | solution.py:75
  931.8 95.5 %collective-permute-start.31 = (bf16[2,2,2,128,1024]{4,3,2,0,1:T(8,128)(2,1)}, bf16[2,2,2,128,1024]{4,3,2,0,1:T(8,128)(2,1)}, u32[]{:S(2)}, u32[]{:S(2)}) collective-permute-start(bf16[2,2,2,128,1024]{4,3,2,0,1:T(8,128)(2,1)} %dynamic-slice_bitcast_fusion), channel_id=1, source_target_pairs={{0,4},{4,0},{8,12},{12,8},{1,5},{5,1},{9,13},{13,9},{2,6},{6,2},{1... | collective-permute-start | bytes 6291464 | tf_op jit(solution)/shard_map/ppermute | solution.py:75
  934.6 48.4 %collective-permute-start.57 = (bf16[1024,512]{1,0:T(8,128)(2,1)}, bf16[1024,512]{1,0:T(8,128)(2,1)}, u32[]{:S(2)}, u32[]{:S(2)}) collective-permute-start(bf16[1024,512]{1,0:T(8,128)(2,1)} %dynamic-slice_convert_fusion.2), channel_id=1, source_target_pairs={{0,16},{16,0},{1,17},{17,1},{2,18},{18,2},{3,19},{19,3},{4,20},{20... | collective-permute-start | bytes 3145736 | tf_op jit(solution)/shard_map/ppermute | solution.py:75
  966.8 55.2 %collective-permute-start.47 = (bf16[1024,1024]{0,1:T(8,128)(2,1)}, bf16[1024,1024]{0,1:T(8,128)(2,1)}, u32[]{:S(2)}, u32[]{:S(2)}) collective-permute-start(bf16[1024,1024]{0,1:T(8,128)(2,1)} %dynamic-slice_convert_fusion), channel_id=1, source_target_pairs={{0,16},{16,0},{1,17},{17,1},{2,18},{18,2},{3,19},{19,3},{4,20},{20... | collective-permute-start | bytes 6291464 | tf_op jit(solution)/shard_map/ppermute | solution.py:75
  983.1 22.8 %collective-permute-start.35 = (bf16[256,2048]{1,0:T(8,128)(2,1)}, bf16[256,2048]{1,0:T(8,128)(2,1)}, u32[]{:S(2)}, u32[]{:S(2)}) collective-permute-start(bf16[256,2048]{1,0:T(8,128)(2,1)} %pad_maximum_fusion.12), channel_id=1, source_target_pairs={{0,1},{1,0},{2,3},{3,2},{4,5},{5,4},{6,7},{7,6},{8,9},{9,8},{10,11... | collective-permute-start | bytes 3145736 | tf_op jit(solution)/shard_map/ppermute | solution.py:75
  987.1 186.0 %reduce-scatter.6.cloned.1.call-start = ((), (), s32[]{:S(2)}) async-start(), calls=%async_computation.5 | async-start | bytes 2621440 | tf_op jit(solution)/shard_map/reduce_scatter | solution.py:739
  992.4 15.8 %collective-permute-start.38 = (bf16[2,2,128,576]{2,3,0,1:T(8,128)(2,1)}, bf16[2,2,128,576]{2,3,0,1:T(8,128)(2,1)}, u32[]{:S(2)}, u32[]{:S(2)}) collective-permute-start(bf16[2,2,128,576]{2,3,0,1:T(8,128)(2,1)} %fusion.83), channel_id=1, source_target_pairs={{0,2},{1,3},{2,0},{3,1},{4,6},{5,7},{6,4},{7,5},{8,10},{9,11},{10,... | collective-permute-start | bytes 1769480 | tf_op jit(solution)/shard_map/ppermute | solution.py:75
  997.2 41.6 %collective-permute-start.41 = (bf16[576,1024]{1,0:T(8,128)(2,1)}, bf16[576,1024]{1,0:T(8,128)(2,1)}, u32[]{:S(2)}, u32[]{:S(2)}) collective-permute-start(bf16[576,1024]{1,0:T(8,128)(2,1)} %bitcast.301), channel_id=1, source_target_pairs={{0,16},{16,0},{1,17},{17,1},{2,18},{18,2},{3,19},{19,3},{4,20},{20... | collective-permute-start | bytes 3538952 | tf_op jit(solution)/shard_map/ppermute | solution.py:75
  1005.8 66.0 %collective-permute-start.27 = (bf16[2,2,2,128,1024]{4,3,1,2,0:T(8,128)(2,1)}, bf16[2,2,2,128,1024]{4,3,1,2,0:T(8,128)(2,1)}, u32[]{:S(2)}, u32[]{:S(2)}) collective-permute-start(bf16[2,2,2,128,1024]{4,3,1,2,0:T(8,128)(2,1)} %dynamic-slice_bitcast_fusion.1), channel_id=1, source_target_pairs={{0,2},{1,3},{2,0},{3,1},{4,6},{5,7},{6,4},{7,5},{8,10},{9,11},{10,... | collective-permute-start | bytes 6291464 | tf_op jit(solution)/shard_map/ppermute | solution.py:75
  1018.8 45.5 %collective-permute-start.36 = (bf16[128,2048]{1,0:T(8,128)(2,1)}, bf16[128,2048]{1,0:T(8,128)(2,1)}, u32[]{:S(2)}, u32[]{:S(2)}) collective-permute-start(bf16[128,2048]{1,0:T(8,128)(2,1)} %fusion.57), channel_id=1, source_target_pairs={{0,2},{1,3},{2,0},{3,1},{4,6},{5,7},{6,4},{7,5},{8,10},{9,11},{10,... | collective-permute-start | bytes 1572872 | tf_op jit(solution)/shard_map/ppermute | solution.py:75
  1027.2 206.6 %all-gather.10.cloned.1.call-start = ((), (), s32[]{:S(2)}) async-start(), calls=%async_computation.8 | async-start | bytes 1310720 | tf_op jit(solution)/shard_map/all_gather | solution.py:742
  1033.2 86.0 %collective-permute-start.48 = (bf16[2,2,2,2,64,576]{5,4,3,2,1,0:T(8,128)(2,1)S(1)}, bf16[2,2,2,2,64,576]{5,4,3,2,1,0:T(8,128)(2,1)S(1)}, u32[]{:S(2)}, u32[]{:S(2)}) collective-permute-start(bf16[2,2,2,2,64,576]{5,4,3,2,1,0:T(8,128)(2,1)S(1)} %fusion.38), channel_id=1, source_target_pairs={{0,1},{1,0},{2,3},{3,2},{4,5},{5,4},{6,7},{7,6},{8,9},{9,8},{10,11... | collective-permute-start | bytes 3538952 | tf_op jit(solution)/shard_map/ppermute | solution.py:75
  1068.1 56.2 %collective-permute-start.32 = (bf16[2,2,128,1024]{3,2,1,0:T(8,128)(2,1)S(1)}, bf16[2,2,128,1024]{3,2,1,0:T(8,128)(2,1)S(1)}, u32[]{:S(2)}, u32[]{:S(2)}) collective-permute-start(bf16[2,2,128,1024]{3,2,1,0:T(8,128)(2,1)S(1)} %dynamic-slice_bitcast_fusion.2), channel_id=1, source_target_pairs={{0,8},{4,12},{8,0},{12,4},{1,9},{5,13},{9,1},{13,5},{2,10},{6,14},... | collective-permute-start | bytes 3145736 | tf_op jit(solution)/shard_map/ppermute | solution.py:75
  1074.5 19.4 %collective-permute-start.44 = (f32[2560]{0:T(1024)S(1)}, f32[2560]{0:T(1024)S(1)}, u32[]{:S(2)}, u32[]{:S(2)}) collective-permute-start(f32[2560]{0:T(1024)S(1)} %add.620), channel_id=1, source_target_pairs={{0,4},{4,0},{8,12},{12,8},{1,5},{5,1},{9,13},{13,9},{2,6},{6,2},{1... | collective-permute-start | bytes 30728 | tf_op jit(solution)/shard_map/ppermute | solution.py:75
  1076.3 62.6 %collective-permute-start.28 = (bf16[2,2,128,1024]{3,2,0,1:T(8,128)(2,1)}, bf16[2,2,128,1024]{3,2,0,1:T(8,128)(2,1)}, u32[]{:S(2)}, u32[]{:S(2)}) collective-permute-start(bf16[2,2,128,1024]{3,2,0,1:T(8,128)(2,1)} %dynamic-slice_bitcast_fusion.3), channel_id=1, source_target_pairs={{0,16},{16,0},{1,17},{17,1},{2,18},{18,2},{3,19},{19,3},{4,20},{20... | collective-permute-start | bytes 3145736 | tf_op jit(solution)/shard_map/ppermute | solution.py:75
  1093.9 23.7 %collective-permute-start.45 = (f32[2560]{0:T(1024)S(1)}, f32[2560]{0:T(1024)S(1)}, u32[]{:S(2)}, u32[]{:S(2)}) collective-permute-start(f32[2560]{0:T(1024)S(1)} %add.621), channel_id=1, source_target_pairs={{0,8},{4,12},{8,0},{12,4},{1,9},{5,13},{9,1},{13,5},{2,10},{6,14},... | collective-permute-start | bytes 30728 | tf_op jit(solution)/shard_map/ppermute | solution.py:75
  1120.5 16.6 %collective-permute-start.49 = (bf16[2,2,2,64,576]{4,3,2,1,0:T(8,128)(2,1)}, bf16[2,2,2,64,576]{4,3,2,1,0:T(8,128)(2,1)}, u32[]{:S(2)}, u32[]{:S(2)}) collective-permute-start(bf16[2,2,2,64,576]{4,3,2,1,0:T(8,128)(2,1)} %fusion.78), channel_id=1, source_target_pairs={{0,2},{1,3},{2,0},{3,1},{4,6},{5,7},{6,4},{7,5},{8,10},{9,11},{10,... | collective-permute-start | bytes 1769480 | tf_op jit(solution)/shard_map/ppermute | solution.py:75
  1125.6 35.0 %collective-permute-start.33 = (bf16[2,128,1024]{2,1,0:T(8,128)(2,1)S(1)}, bf16[2,128,1024]{2,1,0:T(8,128)(2,1)}, u32[]{:S(2)}, u32[]{:S(2)}) collective-permute-start(bf16[2,128,1024]{2,1,0:T(8,128)(2,1)S(1)} %dynamic-slice_bitcast_fusion.4), channel_id=1, source_target_pairs={{0,16},{16,0},{1,17},{17,1},{2,18},{18,2},{3,19},{19,3},{4,20},{20... | collective-permute-start | bytes 1572872 | tf_op jit(solution)/shard_map/ppermute | solution.py:75
  1126.6 119.6 %all-gather.8.cloned.1.call-start = ((), (), s32[]{:S(2)}) async-start(), calls=%async_computation.6 | async-start | bytes 2621440 | tf_op jit(solution)/shard_map/all_gather | solution.py:742
  1138.8 20.7 %collective-permute-start.50 = (bf16[2,2,64,576]{3,2,1,0:T(8,128)(2,1)S(1)}, bf16[2,2,64,576]{3,2,1,0:T(8,128)(2,1)S(1)}, u32[]{:S(2)}, u32[]{:S(2)}) collective-permute-start(bf16[2,2,64,576]{3,2,1,0:T(8,128)(2,1)S(1)} %fusion.94), channel_id=1, source_target_pairs={{0,4},{4,0},{8,12},{12,8},{1,5},{5,1},{9,13},{13,9},{2,6},{6,2},{1... | collective-permute-start | bytes 884744 | tf_op jit(solution)/shard_map/ppermute | solution.py:75
  1142.4 33.4 %collective-permute-start.29 = (bf16[2,128,1024]{2,1,0:T(8,128)(2,1)}, bf16[2,128,1024]{2,1,0:T(8,128)(2,1)}, u32[]{:S(2)}, u32[]{:S(2)}) collective-permute-start(bf16[2,128,1024]{2,1,0:T(8,128)(2,1)} %dynamic-slice_bitcast_fusion.5), channel_id=1, source_target_pairs={{0,4},{4,0},{8,12},{12,8},{1,5},{5,1},{9,13},{13,9},{2,6},{6,2},{1... | collective-permute-start | bytes 1572872 | tf_op jit(solution)/shard_map/ppermute | solution.py:75
  1162.6 37.1 %collective-permute-start.34 = (bf16[128,1024]{1,0:T(8,128)(2,1)}, bf16[128,1024]{1,0:T(8,128)(2,1)}, u32[]{:S(2)}, u32[]{:S(2)}) collective-permute-start(bf16[128,1024]{1,0:T(8,128)(2,1)} %dynamic-slice_bitcast_fusion.6), channel_id=1, source_target_pairs={{0,2},{1,3},{2,0},{3,1},{4,6},{5,7},{6,4},{7,5},{8,10},{9,11},{10,... | collective-permute-start | bytes 786440 | tf_op jit(solution)/shard_map/ppermute | solution.py:75
  1179.5 20.1 %collective-permute-start.53 = (bf16[64,576]{1,0:T(8,128)(2,1)S(1)}, bf16[64,576]{1,0:T(8,128)(2,1)S(1)}, u32[]{:S(2)}, u32[]{:S(2)}) collective-permute-start(bf16[64,576]{1,0:T(8,128)(2,1)S(1)} %fusion.101), channel_id=1, source_target_pairs={{0,8},{4,12},{8,0},{12,4},{1,9},{5,13},{9,1},{13,5},{2,10},{6,14},... | collective-permute-start | bytes 221192 | tf_op jit(solution)/shard_map/ppermute | solution.py:75
  1183.0 40.9 %collective-permute-start.30 = (bf16[128,1024]{1,0:T(8,128)(2,1)S(1)}, bf16[128,1024]{1,0:T(8,128)(2,1)S(1)}, u32[]{:S(2)}, u32[]{:S(2)}) collective-permute-start(bf16[128,1024]{1,0:T(8,128)(2,1)S(1)} %dynamic-slice_bitcast_fusion.7), channel_id=1, source_target_pairs={{0,8},{4,12},{8,0},{12,4},{1,9},{5,13},{9,1},{13,5},{2,10},{6,14},... | collective-permute-start | bytes 786440 | tf_op jit(solution)/shard_map/ppermute | solution.py:75
  1199.7 22.4 %collective-permute-start.54 = (bf16[2,64,576]{2,1,0:T(8,128)(2,1)S(1)}, bf16[2,64,576]{2,1,0:T(8,128)(2,1)S(1)}, u32[]{:S(2)}, u32[]{:S(2)}) collective-permute-start(bf16[2,64,576]{2,1,0:T(8,128)(2,1)S(1)} %maximum_select_fusion.33), channel_id=1, source_target_pairs={{0,4},{4,0},{8,12},{12,8},{1,5},{5,1},{9,13},{13,9},{2,6},{6,2},{1... | collective-permute-start | bytes 442376 | tf_op jit(solution)/shard_map/ppermute | solution.py:75
  (137 other events, 2081.9 us)
Sparse Core Ops, SparseCore 0:
  10.9 158.4 all-gather.11
  249.7 120.7 all-gather.5
  445.4 192.6 reduce-scatter.3
  987.2 26.8 reduce-scatter.7
  1027.3 42.1 reduce-scatter.5
  1126.8 35.8 all-gather.9
  1173.2 62.7 all-gather.7
